TPU v7x, 128 devices: a whole 4x4x4 slice. The times are simulated.
128 devices in a mesh: tm: 8 (over z, core), row: 16 (over y, x).
Axes of the slice: x: 4, y: 4, z: 4, core: 2. Of those that a mesh axis runs over, the one named last changes fastest.
Arguments:
- visible: bfloat16 [8, 16, 16, 4, 1024], P('tm', 'row'), may hold values from -6 to 6
- slot_pos: int32 [8, 16, 16, 4], P('tm', 'row'), may hold values from -1 to 255, as said below
- window_shift: int32 [2, 2], replicated, may hold values from 0 to 3, as said below
- mask_token: bfloat16 [1024], replicated, may hold values from -6 to 6
- w_qkv: bfloat16 [1024, 3072], replicated, may hold values from -6.25 to 6.25
- w_out: bfloat16 [1024, 1024], replicated, may hold values from -0.1875 to 0.1875
- w_head: bfloat16 [1024, 1536], replicated, may hold values from -0.1875 to 0.1875
- pixels: bfloat16 [32, 64, 16, 1536], P('tm', 'row'), may hold values from 0 to 1
Outputs:
- d_visible: bfloat16 [8, 16, 16, 4, 1024], P('tm', 'row')
- d_mask_token: float32 [1024], replicated
Inputs may be any that keep to these rules, and one draw needn't show every extreme that they name: Each live entry slot_pos[i, s, d, c] is a token index of decoder shard (i, d) in frame, row, column order; the live entries aimed at one shard (i, d) are distinct; every slot slot_pos[i, s, s, c] is live, so each shard receives all 4 slots from the packed shard of its own band; other slots are live or -1 at rates that differ from packed shard to packed shard. window_shift[0, g] lies in 0 to 1 and window_shift[1, g] in 0 to 3; some block of columns has row offset 4 - 1 and some block has frame offset 0.
All inputs are finite; a program needn't handle non-finite values.
Results may differ from a plain program's by a relative error of at most 0.014.
Values may be sent and summed in bfloat16 or wider, within the bound.
No kernel may reach another device: no remote copies, remote signals or barrier semaphores. Data moves between devices by JAX's collectives and lax.ppermute only.
A program may use at most 128 MiB of HBM per device.

v0:
```python
import math

import jax
import jax.numpy as jnp
from jax import lax
from jax.sharding import Mesh
from jax.sharding import PartitionSpec as P

HEADS = 16
WT = 2
WH = 4
WW = 8
TM = ("tm_0", "tm_1")
ROW = ("row_0", "row_1")
TM_ROW = ("tm_0", "tm_1", "row_0", "row_1")


def from_behind(value, axis, steps):
    count = lax.axis_size(axis)
    pairs = [(source, (source + steps) % count) for source in range(count)]
    return lax.ppermute(value, axis, pairs)


def as_sent(shard):
    return jax.tree.map(lambda a: a.astype(jnp.bfloat16) if a.dtype == jnp.float32 else a, shard)


def one_axis_at_a_time(shard, axes):
    for axis in axes:
        shard = lax.psum(shard, axis)
    return shard


def layer_norm(values):
    center = values - jnp.mean(values, axis=-1, keepdims=True)
    return center * lax.rsqrt(jnp.mean(center * center, axis=-1, keepdims=True) + 1e-05)


def sinusoid(coordinate, channel_count):
    half_count = channel_count // 2
    frequency = jnp.exp(-math.log(10000.0) * jnp.arange(half_count, dtype=jnp.float32) / half_count)
    angles = coordinate.astype(jnp.float32)[..., None] * frequency
    return jnp.concatenate([jnp.sin(angles), jnp.cos(angles)], axis=-1)


def position_table(frame_pos, row_pos, column_pos, model_width):
    quarter = model_width // 4
    remainder = (model_width - quarter) // 2
    return jnp.concatenate(
        [
            sinusoid(frame_pos, quarter),
            sinusoid(row_pos, remainder),
            sinusoid(column_pos, model_width - quarter - remainder),
        ],
        axis=-1,
    )


def window_core(grid_block, w_qkv, w_out):
    frame_count, row_count, column_count, model_width = grid_block.shape
    head_dim = model_width // HEADS
    normed = layer_norm(grid_block).astype(jnp.bfloat16)
    packed = jnp.dot(
        normed.reshape(-1, model_width), w_qkv, preferred_element_type=jnp.float32
    ).astype(jnp.bfloat16)
    packed = packed.reshape(
        frame_count // WT, WT, row_count // WH, WH, column_count // WW, WW, 3, HEADS, head_dim
    )
    packed = packed.transpose(6, 0, 2, 4, 7, 1, 3, 5, 8).reshape(
        3, -1, HEADS, WT * WH * WW, head_dim
    )
    scores = jnp.einsum(
        "nhqe,nhke->nhqk", packed[0], packed[1], preferred_element_type=jnp.float32
    ) * head_dim ** (-0.5)
    weights = jax.nn.softmax(scores, axis=-1).astype(jnp.bfloat16)
    mixed_heads = jnp.einsum(
        "nhqk,nhke->nhqe", weights, packed[2], preferred_element_type=jnp.float32
    ).astype(jnp.bfloat16)
    mixed_heads = mixed_heads.reshape(
        frame_count // WT, row_count // WH, column_count // WW, HEADS, WT, WH, WW, head_dim
    )
    mixed_heads = mixed_heads.transpose(0, 4, 1, 5, 2, 6, 3, 7).reshape(-1, model_width)
    result_rows = jnp.dot(mixed_heads, w_out, preferred_element_type=jnp.float32)
    return result_rows.reshape(frame_count, row_count, column_count, model_width)


def pixel_gradient(stream_rows, pixel_rows, masked, w_head):
    row_total, pixel_count = pixel_rows.shape
    group_size = pixel_count // 3
    raw_pixels = pixel_rows.astype(jnp.float32).reshape(row_total, 3, group_size)
    center = raw_pixels - jnp.mean(raw_pixels, axis=-1, keepdims=True)
    spread = jnp.sqrt(jnp.sum(center * center, axis=-1, keepdims=True) / (group_size - 1))
    target = (center / (spread + 1e-06)).reshape(row_total, pixel_count)

    def pixel_loss(values):
        normed = layer_norm(values).astype(jnp.bfloat16)
        predicted = jnp.dot(normed, w_head, preferred_element_type=jnp.float32)
        errors = predicted - target
        return 0.5 * jnp.sum(masked[:, None] * errors * errors)

    return jax.grad(pixel_loss)(stream_rows)


def regroup(joined, offsets, base, length, axis, sign):
    pieces = []
    for group in range(offsets.shape[0]):
        piece = joined[:, :, group * WW : (group + 1) * WW]
        pieces.append(lax.dynamic_slice_in_dim(piece, base + sign * offsets[group], length, axis))
    return jnp.concatenate(pieces, axis=2)


def align_block(grid_block, time_offsets, row_offsets):
    rim_time = WT - 1
    rim_row = WH - 1
    frame_count = grid_block.shape[0]
    row_count = grid_block.shape[1]
    lower_frames = from_behind(grid_block[frame_count - rim_time :], TM, 1)
    joined = jnp.concatenate([lower_frames, grid_block], axis=0)
    grid_block = regroup(joined, time_offsets, rim_time, frame_count, 0, -1)
    lower_rows = from_behind(grid_block[:, row_count - rim_row :], ROW, 1)
    joined = jnp.concatenate([lower_rows, grid_block], axis=1)
    return regroup(joined, row_offsets, rim_row, row_count, 1, -1)


def return_values(aligned, time_offsets, row_offsets):
    rim_time = WT - 1
    rim_row = WH - 1
    frame_count = aligned.shape[0]
    row_count = aligned.shape[1]
    upper_rows = from_behind(aligned[:, :rim_row], ROW, -1)
    joined = jnp.concatenate([aligned, upper_rows], axis=1)
    aligned = regroup(joined, row_offsets, 0, row_count, 1, 1)
    upper_frames = from_behind(aligned[:rim_time], TM, -1)
    joined = jnp.concatenate([aligned, upper_frames], axis=0)
    return regroup(joined, time_offsets, 0, frame_count, 0, 1)


def return_grads(aligned, time_offsets, row_offsets):
    rim_time = WT - 1
    rim_row = WH - 1
    frame_count = aligned.shape[0]
    row_count = aligned.shape[1]
    upper_rows = from_behind(aligned[:, :rim_row].astype(jnp.bfloat16), ROW, -1).astype(jnp.float32)
    joined = jnp.concatenate([aligned, upper_rows], axis=1)
    aligned = regroup(joined, row_offsets, 0, row_count, 1, 1)
    upper_frames = from_behind(as_sent(aligned[:rim_time]), TM, -1)
    joined = jnp.concatenate([aligned, upper_frames], axis=0)
    return regroup(joined, time_offsets, 0, frame_count, 0, 1)


def per_device(visible, slot_pos, window_shift, mask_token, w_qkv, w_out, w_head, pixels):
    frame_count, row_count, column_count, pixel_count = pixels.shape
    model_width = mask_token.shape[0]
    tokens = frame_count * row_count * column_count
    peer_count = slot_pos.shape[2]
    slot_count = slot_pos.shape[3]
    sent_rows = visible.reshape(peer_count, slot_count, model_width)
    sent_index = slot_pos.reshape(peer_count, slot_count)
    got_rows, got_index = (
        lax.all_to_all(sent_rows, ROW, split_axis=0, concat_axis=0, tiled=True),
        lax.all_to_all(sent_index, ROW, split_axis=0, concat_axis=0, tiled=True),
    )
    flat_index = got_index.reshape(-1)
    is_live = flat_index >= 0
    target_index = jnp.where(is_live, flat_index, tokens).astype(jnp.int32)
    visible_grid = (
        jnp.zeros((tokens, model_width), jnp.float32)
        .at[target_index]
        .set(got_rows.reshape(-1, model_width).astype(jnp.float32), mode="drop")
    )
    seen_flags = jnp.zeros((tokens,), jnp.float32).at[target_index].set(1.0, mode="drop")
    local_index = jnp.arange(tokens, dtype=jnp.int32)
    frame_global = lax.axis_index(TM) * frame_count + local_index // (row_count * column_count)
    row_global = lax.axis_index(ROW) * row_count + local_index // column_count % row_count
    position_rows = position_table(
        frame_global, row_global, local_index % column_count, model_width
    )
    start_rows = jnp.where(
        seen_flags[:, None] > 0, visible_grid, mask_token.astype(jnp.float32)[None, :]
    )
    embedded = (
        (start_rows + position_rows)
        .astype(jnp.bfloat16)
        .reshape(frame_count, row_count, column_count, model_width)
    )
    stream = embedded.astype(jnp.float32)
    time_offsets = window_shift[0]
    row_offsets = window_shift[1]

    def core_only(grid_block):
        return window_core(grid_block, w_qkv, w_out)

    aligned = align_block(embedded, time_offsets, row_offsets)
    attn_aligned, pull_back = jax.vjp(core_only, aligned.astype(jnp.float32))
    attn_value = return_values(attn_aligned.astype(jnp.bfloat16), time_offsets, row_offsets)
    residual = stream + attn_value.astype(jnp.float32)
    masked = 1.0 - seen_flags
    grad_stream = pixel_gradient(
        residual.reshape(tokens, model_width), pixels.reshape(tokens, pixel_count), masked, w_head
    )
    grad_attn = lax.optimization_barrier(grad_stream.astype(jnp.bfloat16)).reshape(
        frame_count, row_count, column_count, model_width
    )
    grad_in = align_block(grad_attn, time_offsets, row_offsets).astype(jnp.float32)
    grad_aligned = pull_back(grad_in)[0]
    grad_core = return_grads(grad_aligned, time_offsets, row_offsets)
    grad_embedded = grad_stream + grad_core.reshape(tokens, model_width)
    picked = grad_embedded[jnp.minimum(target_index, tokens - 1)] * is_live[:, None].astype(
        jnp.float32
    )
    picked = picked.astype(jnp.bfloat16).reshape(peer_count, slot_count, model_width)
    returned = lax.all_to_all(picked, ROW, split_axis=0, concat_axis=0, tiled=True)
    d_visible = returned.reshape(visible.shape)
    local_total = jnp.sum(masked[:, None] * grad_embedded, axis=0)
    mask_total = one_axis_at_a_time(local_total, TM_ROW)
    grad_scale = (tokens * lax.axis_size(TM) * lax.axis_size(ROW)) ** (-0.5)
    return (d_visible, mask_total * grad_scale)


def solution(mesh):
    torus = Mesh(mesh.devices.reshape(4, 2, 4, 4), ("tm_0", "tm_1", "row_0", "row_1"))
    return jax.shard_map(
        per_device,
        mesh=torus,
        in_specs=(
            P(TM, ROW, None, None, None),
            P(TM, ROW, None, None),
            P(),
            P(),
            P(),
            P(),
            P(),
            P(TM, ROW, None, None),
        ),
        out_specs=(P(TM, ROW, None, None, None), P()),
        check_vma=False,
    )
```

profile of v0, /device:TPU:0, one launch (start us, length us, event | category | flops | bytes accessed | tf_op | source)
XLA Modules:
  0.0 237.5 jit_solution(4123407618860540178)
XLA Ops:
  2.1 7.1 %all-to-all-start = ((s32[16,1,4]{2,1,0:T(1,128)}), s32[16,1,4]{2,1,0:T(1,128)S(1)}, u32[]{:S(2)}, u32[]{:S(2)}) async-start(s32[16,1,4]{2,1,0:T(1,128)} %copy.47), calls=%async_computation | async-start | bytes 16384 | tf_op jit(solution)/shard_map/all_to_all | solution.py:161
  11.2 3.8 %reshape.338 = f32[256,3,512]{2,1,0:T(4,128)} reshape(bf16[4,4,16,1536]{3,2,1,0:T(8,128)(2,1)} %param.15) | data formatting | bytes 2359296 | tf_op jit(solution)/shard_map/convert_element_type | solution.py:90
  18.2 3.6 %multiply_cosine_fusion = (f32[256,192]{1,0:T(8,128)S(1)}, f32[256,192]{1,0:T(8,128)}, f32[256,192]{1,0:T(8,128)}, f32[256,192]{1,0:T(8,128)}) fusion(f32[256]{0:T(256)S(1)} %get-tuple-element.43, f32[192]{0:T(256)} %multiply_exponential_fusion, f32[256]{0:T(256)} %get-tuple-element.44), kind=kLoop, calls=%fused_computation.97 | loop fusion | flops 98304 | bytes 789248 | tf_op jit(solution)/shard_map/cos | solution.py:43
  21.8 2.2 concatenate.51
  24.0 7.2 %all-to-all-start.1 = ((bf16[16,4,1024]{2,1,0:T(4,128)(2,1)}), bf16[16,4,1024]{2,1,0:T(4,128)(2,1)S(1)}, u32[]{:S(2)}, u32[]{:S(2)}) async-start(bf16[16,4,1024]{2,1,0:T(4,128)(2,1)} %bitcast.121), calls=%async_computation.1 | async-start | bytes 262144 | tf_op jit(solution)/shard_map/all_to_all | solution.py:160
  33.9 5.3 %all-to-all-done.1 = bf16[16,4,1024]{2,1,0:T(4,128)(2,1)S(1)} async-done(((bf16[16,4,1024]{2,1,0:T(4,128)(2,1)}), bf16[16,4,1024]{2,1,0:T(4,128)(2,1)S(1)}, u32[]{:S(2)}, u32[]{:S(2)}) %all-to-all-start.1) | async-done | bytes 131104 | tf_op jit(solution)/shard_map/all_to_all | solution.py:160
  39.9 2.2 scatter_custom_fusion.1
  57.1 3.1 %copy.56 = f32[256,1536]{1,0:T(8,128)} copy(f32[256,1536]{0,1:T(8,128)} %bitcast.104) | data formatting | bytes 3145728 | tf_op jit(solution)/shard_map/div | solution.py:93
  61.4 3.1 %copy.54 = f32[256,1536]{1,0:T(8,128)} copy(f32[256,1536]{0,1:T(8,128)} %bitcast.105) | data formatting | bytes 3145728 | tf_op jit(solution)/shard_map/sub | solution.py:91
  64.6 3.6 %collective-permute-done.1 = bf16[4,3,16,1024]{3,2,1,0:T(8,128)(2,1)} collective-permute-done((bf16[4,3,16,1024]{3,2,1,0:T(8,128)(2,1)}, bf16[4,3,16,1024]{3,2,1,0:T(8,128)(2,1)}, u32[]{:S(2)}, u32[]{:S(2)}) %collective-permute-start.1) | collective-permute-done | bytes 393248 | tf_op jit(solution)/shard_map/ppermute | solution.py:21
  73.0 5.8 %convolution_convert_fusion = bf16[256,3072]{1,0:T(8,128)(2,1)} fusion(bf16[256,1024]{1,0:T(8,128)(2,1)S(1)} %multiply_convert_fusion.1, bf16[1024,3072]{1,0:T(8,128)(2,1)} %param.12), kind=kOutput, calls=%fused_computation.4 | convolution fusion | flops 1611399168 | bytes 8388608 | tf_op jit(solution)/shard_map/jvp()/dot_general | solution.py:63
  78.7 4.9 %reshape.324 = bf16[2,2,1,4,2,8,3,16,64]{8,7,6,5,4,3,1,0,2:T(8,128)(2,1)} reshape(bf16[256,3072]{1,0:T(8,128)(2,1)} %convolution_convert_fusion) | data formatting | bytes 3145728 | tf_op jit(solution)/shard_map/jvp()/reshape | solution.py:66
  83.6 2.7 %fusion.66 = (bf16[1,2,1,2,16,2,4,8,64]{8,4,0,7,3,6,5,1,2:T(8,128)(2,1)S(1)}, bf16[1,2,1,2,16,2,4,8,64]{8,4,0,7,3,6,5,1,2:T(8,128)(2,1)S(1)}, bf16[1,2,1,2,16,2,4,8,64]{8,4,0,7,3,6,5,1,2:T(8,128)(2,1)S(1)}) fusion(bf16[3,2,1,2,16,2,4,8,64]{8,4,0,7,3,6,5,1,2:T(8,128)(2,1)} %bitcast.100), kind=kLoop, calls=%fused_computation.177 | loop fusion | bytes 3145728 | tf_op jit(solution)/shard_map/jvp()/slice | solution.py:77
  90.1 3.7 %fusion.72 = (f32[4,16,64]{2,1,0:T(8,128)S(1)}, f32[4,16,64,64]{2,3,1,0:T(8,128)}) fusion(bf16[4,16,64,64]{3,2,1,0:T(8,128)(2,1)} %bitcast.116, bf16[4,16,64,64]{3,2,1,0:T(8,128)(2,1)} %bitcast.114), kind=kOutput, calls=%fused_computation.183 | convolution fusion | flops 34340928 | bytes 2113536 | tf_op jit(solution)/shard_map/jvp()/sub | solution.py:75
  93.8 2.4 convolution_convert_fusion.5
  96.1 2.2 copy.52
  98.3 2.6 %dot_general.41 = bf16[4,4,16,1024]{3,2,1,0:T(8,128)(2,1)} reshape(bf16[2,2,1,4,2,8,16,64]{7,6,5,4,3,1,0,2:T(8,128)(2,1)} %copy.52) | data formatting | bytes 1048576 | tf_op jit(solution)/shard_map/jvp()/dot_general | solution.py:83
  100.9 2.6 %fusion.22 = bf16[4,4,16,1024]{3,2,1,0:T(8,128)(2,1)S(1)} fusion(bf16[4,4,16,1024]{3,2,1,0:T(8,128)(2,1)} %dot_general.41, bf16[1024,1024]{1,0:T(8,128)(2,1)} %param.13), kind=kOutput, calls=%fused_computation.48 | convolution fusion | flops 537133056 | bytes 3145728 | tf_op jit(solution)/shard_map/jvp()/dot_general | solution.py:83
  119.5 2.5 %collective-permute-done.3 = bf16[1,4,16,1024]{3,2,1,0:T(8,128)(2,1)S(1)} collective-permute-done((bf16[1,4,16,1024]{3,2,1,0:T(8,128)(2,1)S(1)}, bf16[1,4,16,1024]{3,2,1,0:T(8,128)(2,1)S(1)}, u32[]{:S(2)}, u32[]{:S(2)}) %collective-permute-start.3) | collective-permute-done | bytes 131104 | tf_op jit(solution)/shard_map/ppermute | solution.py:21
  123.1 4.7 %fusion.25 = (f32[256]{0:T(256)S(1)}, bf16[256,1024]{1,0:T(8,128)(2,1)}) fusion(bf16[256,1024]{1,0:T(8,128)(2,1)} %copy-done.2, bf16[4,4,16,1024]{3,2,1,0:T(8,128)(2,1)} %copy-done.10, f32[256]{0:T(256)S(1)} %broadcast_multiply_fusion.4, bf16[1024,1536]{1,0:T(8,128)(2,1)S(1)} %copy-done, f32[256]{0:T(256)S(1)} %get-tuple-element.25, ...), kind=kOutput, calls=%fused_computation.50 | convolution fusion | flops 1616248576 | bytes 6820864 | tf_op jit(solution)/shard_map/transpose(jvp())/dot_general | solution.py:97
  130.8 4.8 %collective-permute-done.4 = bf16[1,4,16,1024]{3,2,1,0:T(8,128)(2,1)S(1)} collective-permute-done((bf16[1,4,16,1024]{3,2,1,0:T(8,128)(2,1)S(1)}, bf16[1,4,16,1024]{3,2,1,0:T(8,128)(2,1)S(1)}, u32[]{:S(2)}, u32[]{:S(2)}) %collective-permute-start.4) | collective-permute-done | bytes 131104 | tf_op jit(solution)/shard_map/ppermute | solution.py:21
  135.8 11.5 %collective-permute-done.5 = bf16[4,3,16,1024]{3,2,1,0:T(8,128)(2,1)S(1)} collective-permute-done((bf16[4,3,16,1024]{3,2,1,0:T(8,128)(2,1)S(1)}, bf16[4,3,16,1024]{3,2,1,0:T(8,128)(2,1)S(1)}, u32[]{:S(2)}, u32[]{:S(2)}) %collective-permute-start.5) | collective-permute-done | bytes 393248 | tf_op jit(solution)/shard_map/ppermute | solution.py:21
  156.4 5.3 %copy.67 = bf16[3,2,1,2,16,2,4,8,64]{8,4,0,7,3,6,5,1,2:T(8,128)(2,1)} copy(bf16[3,2,1,2,16,2,4,8,64]{8,7,6,5,4,3,1,0,2:T(8,128)(2,1)S(1)} %bitcast.101) | data formatting | bytes 3145728 | tf_op jit(solution)/shard_map/transpose(jvp())/reshape | solution.py:69
  161.8 5.0 %reshape.331 = bf16[256,3072]{1,0:T(8,128)(2,1)} reshape(bf16[2,2,1,4,2,8,3,16,64]{8,7,6,5,4,3,1,0,2:T(8,128)(2,1)} %bitcast.102) | data formatting | bytes 3145728 | tf_op jit(solution)/shard_map/transpose(jvp())/reshape | solution.py:66
  166.8 5.2 %multiply_reduce_fusion.3 = (f32[256]{0:T(256)S(1)}, f32[256,1024]{1,0:T(8,128)S(1)}) fusion(f32[256]{0:T(256)S(1)} %div.129, bf16[4,4,8,1024]{3,2,1,0:T(8,128)(2,1)S(1)} %copy-done.9, bf16[4,4,8,1024]{3,2,1,0:T(8,128)(2,1)S(1)} %constant_dynamic-slice_fusion.7, bf16[256,3072]{1,0:T(8,128)(2,1)} %reshape.331, bf16[1024,3072]{1,0:T(8,128)(2,1)} %param.12), kind=kOutput, calls=%fused_computation.58 | convolution fusion | flops 1612971776 | bytes 9439232 | tf_op jit(solution)/shard_map/transpose(jvp())/dot_general | solution.py:63
  174.8 6.3 %collective-permute-done.6 = bf16[4,3,16,1024]{3,2,1,0:T(8,128)(2,1)S(1)} collective-permute-done((bf16[4,3,16,1024]{3,2,1,0:T(8,128)(2,1)S(1)}, bf16[4,3,16,1024]{3,2,1,0:T(8,128)(2,1)S(1)}, u32[]{:S(2)}, u32[]{:S(2)}) %collective-permute-start.6) | collective-permute-done | bytes 393248 | tf_op jit(solution)/shard_map/ppermute | solution.py:21
  186.7 11.7 %psum.28 = f32[1024]{0:T(1024)S(1)} all-reduce(f32[1024]{0:T(1024)S(1)} %get-tuple-element.2), channel_id=1, replica_groups=mesh['tm_0'=4,'tm_1'=2,'row_0'=4,'row_1'=4] {'tm_0'}, use_global_device_ids=true, to_apply=%region_16.17 | all-reduce | flops 1024 | bytes 8192 | tf_op jit(solution)/shard_map/psum | solution.py:30
  198.4 2.5 %psum.29 = f32[1024]{0:T(1024)S(1)} all-reduce(f32[1024]{0:T(1024)S(1)} %psum.28), channel_id=1, replica_groups=mesh['tm_0'=4,'tm_1'=2,'row_0'=4,'row_1'=4] {'tm_1'}, use_global_device_ids=true, to_apply=%region_17.18 | all-reduce | flops 1024 | bytes 8192 | tf_op jit(solution)/shard_map/psum | solution.py:30
  200.9 7.7 %psum.30 = f32[1024]{0:T(1024)S(1)} all-reduce(f32[1024]{0:T(1024)S(1)} %psum.29), channel_id=1, replica_groups=mesh['tm_0'=4,'tm_1'=2,'row_0'=4,'row_1'=4] {'row_0'}, use_global_device_ids=true, to_apply=%region_18.19 | all-reduce | flops 1024 | bytes 8192 | tf_op jit(solution)/shard_map/psum | solution.py:30
  208.6 12.3 %psum.31 = f32[1024]{0:T(1024)S(1)} all-reduce(f32[1024]{0:T(1024)S(1)} %psum.30), channel_id=1, replica_groups=mesh['tm_0'=4,'tm_1'=2,'row_0'=4,'row_1'=4] {'row_1'}, use_global_device_ids=true, to_apply=%region_19.20 | all-reduce | flops 1024 | bytes 8192 | tf_op jit(solution)/shard_map/psum | solution.py:30
  225.4 3.5 %all-to-all-start.2 = ((bf16[16,4,1024]{2,1,0:T(4,128)(2,1)}), bf16[16,4,1024]{2,1,0:T(4,128)(2,1)S(1)}, u32[]{:S(2)}, u32[]{:S(2)}) async-start(bf16[16,4,1024]{2,1,0:T(4,128)(2,1)} %multiply_convert_fusion.4), calls=%async_computation.2 | async-start | bytes 262144 | tf_op jit(solution)/shard_map/all_to_all | solution.py:212
  229.5 7.4 %all-to-all-done.2 = bf16[16,4,1024]{2,1,0:T(4,128)(2,1)S(1)} async-done(((bf16[16,4,1024]{2,1,0:T(4,128)(2,1)}), bf16[16,4,1024]{2,1,0:T(4,128)(2,1)S(1)}, u32[]{:S(2)}, u32[]{:S(2)}) %all-to-all-start.2) | async-done | bytes 131104 | tf_op jit(solution)/shard_map/all_to_all | solution.py:212
  (184 shorter events, 67.9 us)
Async XLA Ops:
  0.6 122.4 %copy-start = (bf16[1024,1536]{1,0:T(8,128)(2,1)S(1)}, bf16[1024,1536]{1,0:T(8,128)(2,1)}, u32[]{:S(2)}) copy-start(bf16[1024,1536]{1,0:T(8,128)(2,1)} %param.14) | copy-start | bytes 9437188
  2.1 21.8 %all-to-all-start = ((s32[16,1,4]{2,1,0:T(1,128)}), s32[16,1,4]{2,1,0:T(1,128)S(1)}, u32[]{:S(2)}, u32[]{:S(2)}) async-start(s32[16,1,4]{2,1,0:T(1,128)} %copy.47), calls=%async_computation | async-start | bytes 16384 | tf_op jit(solution)/shard_map/all_to_all | solution.py:161
  24.0 15.2 %all-to-all-start.1 = ((bf16[16,4,1024]{2,1,0:T(4,128)(2,1)}), bf16[16,4,1024]{2,1,0:T(4,128)(2,1)S(1)}, u32[]{:S(2)}, u32[]{:S(2)}) async-start(bf16[16,4,1024]{2,1,0:T(4,128)(2,1)} %bitcast.121), calls=%async_computation.1 | async-start | bytes 262144 | tf_op jit(solution)/shard_map/all_to_all | solution.py:160
  33.9 8.3 %copy-start.23 = (f32[256]{0:T(256)}, f32[256]{0:T(256)S(1)}, u32[]{:S(2)}) copy-start(f32[256]{0:T(256)S(1)} %scatter_custom_fusion) | copy-start | bytes 3076
  33.9 10.8 %copy-start.22 = (s32[2,2]{1,0:T(2,128)S(1)}, s32[2,2]{1,0:T(2,128)}, u32[]{:S(2)}) copy-start(s32[2,2]{1,0:T(2,128)} %param.10) | copy-start | bytes 52
  44.6 5.6 %collective-permute-start = (bf16[1,4,16,1024]{3,2,1,0:T(8,128)(2,1)S(1)}, bf16[1,4,16,1024]{3,2,1,0:T(8,128)(2,1)S(1)}, u32[]{:S(2)}, u32[]{:S(2)}) collective-permute-start(bf16[1,4,16,1024]{3,2,1,0:T(8,128)(2,1)S(1)} %bitcast.122), channel_id=1, source_target_pairs={{0,16},{16,32},{32,48},{48,64},{64,80},{80,96},{96,112},{112,0},{1... | collective-permute-start | bytes 393224 | tf_op jit(solution)/shard_map/ppermute | solution.py:21
  47.9 3.1 %copy-start.3 = (bf16[256,1024]{1,0:T(8,128)(2,1)S(1)}, bf16[256,1024]{1,0:T(8,128)(2,1)}, u32[]{:S(2)}) copy-start(bf16[256,1024]{1,0:T(8,128)(2,1)} %copy-done.2) | copy-start | bytes 1572868
  47.9 5.4 %copy-start.5 = (f32[256,3,512]{2,1,0:T(4,128)S(1)}, f32[256,3,512]{2,1,0:T(4,128)}, u32[]{:S(2)}) copy-start(f32[256,3,512]{2,1,0:T(4,128)} %reshape.338) | copy-start | bytes 4718596
  51.0 1.0 copy-start.17
  52.7 15.4 %collective-permute-start.1 = (bf16[4,3,16,1024]{3,2,1,0:T(8,128)(2,1)}, bf16[4,3,16,1024]{3,2,1,0:T(8,128)(2,1)}, u32[]{:S(2)}, u32[]{:S(2)}) collective-permute-start(bf16[4,3,16,1024]{3,2,1,0:T(8,128)(2,1)} %pad_maximum_fusion.7), channel_id=1, source_target_pairs={{0,1},{1,2},{2,3},{3,4},{4,5},{5,6},{6,7},{7,8},{8,9},{9,10},{10,1... | collective-permute-start | bytes 1179656 | tf_op jit(solution)/shard_map/ppermute | solution.py:21
  100.9 5.4 %copy-start.11 = (f32[256,1536]{1,0:T(8,128)S(1)}, f32[256,1536]{1,0:T(8,128)}, u32[]{:S(2)}) copy-start(f32[256,1536]{1,0:T(8,128)} %copy.56) | copy-start | bytes 4718596
  100.9 5.4 %copy-start.12 = (f32[256,1536]{1,0:T(8,128)S(1)}, f32[256,1536]{1,0:T(8,128)}, u32[]{:S(2)}) copy-start(f32[256,1536]{1,0:T(8,128)} %copy.54) | copy-start | bytes 4718596
  100.9 5.4 %copy-start.16 = (bf16[4,4,16,1536]{3,2,1,0:T(8,128)(2,1)S(1)}, bf16[4,4,16,1536]{3,2,1,0:T(8,128)(2,1)}, u32[]{:S(2)}) copy-start(bf16[4,4,16,1536]{3,2,1,0:T(8,128)(2,1)} %param.15) | copy-start | bytes 2359300
  105.1 11.3 %collective-permute-start.2 = (bf16[4,3,16,1024]{3,2,1,0:T(8,128)(2,1)}, bf16[4,3,16,1024]{3,2,1,0:T(8,128)(2,1)}, u32[]{:S(2)}, u32[]{:S(2)}) collective-permute-start(bf16[4,3,16,1024]{3,2,1,0:T(8,128)(2,1)} %slice.169), channel_id=1, source_target_pairs={{0,15},{1,0},{2,1},{3,2},{4,3},{5,4},{6,5},{7,6},{8,7},{9,8},{10,9... | collective-permute-start | bytes 1179656 | tf_op jit(solution)/shard_map/ppermute | solution.py:21
  115.2 2.3 copy-start.15
  115.2 4.3 %copy-start.24 = (f32[256]{0:T(256)S(1)}, f32[256]{0:T(256)}, u32[]{:S(2)}) copy-start(f32[256]{0:T(256)} %copy-done.23) | copy-start | bytes 3076
  118.5 3.5 %collective-permute-start.3 = (bf16[1,4,16,1024]{3,2,1,0:T(8,128)(2,1)S(1)}, bf16[1,4,16,1024]{3,2,1,0:T(8,128)(2,1)S(1)}, u32[]{:S(2)}, u32[]{:S(2)}) collective-permute-start(bf16[1,4,16,1024]{3,2,1,0:T(8,128)(2,1)S(1)} %pad_maximum_fusion.9), channel_id=1, source_target_pairs={{0,112},{16,0},{32,16},{48,32},{64,48},{80,64},{96,80},{112,96},{1... | collective-permute-start | bytes 393224 | tf_op jit(solution)/shard_map/ppermute | solution.py:21
  119.5 2.7 %copy-start.4 = (bf16[256,1024]{1,0:T(8,128)(2,1)S(1)}, bf16[256,1024]{1,0:T(8,128)(2,1)}, u32[]{:S(2)}) copy-start(bf16[256,1024]{1,0:T(8,128)(2,1)} %copy-done.2) | copy-start | bytes 1572868
  129.6 6.1 %copy-start.6 = (f32[256,1024]{1,0:T(8,128)}, f32[256,1024]{1,0:T(8,128)S(1)}, u32[]{:S(2)}) copy-start(f32[256,1024]{1,0:T(8,128)S(1)} %get-tuple-element.5) | copy-start | bytes 3145732
  129.8 5.8 %collective-permute-start.4 = (bf16[1,4,16,1024]{3,2,1,0:T(8,128)(2,1)S(1)}, bf16[1,4,16,1024]{3,2,1,0:T(8,128)(2,1)S(1)}, u32[]{:S(2)}, u32[]{:S(2)}) collective-permute-start(bf16[1,4,16,1024]{3,2,1,0:T(8,128)(2,1)S(1)} %bitcast.123), channel_id=1, source_target_pairs={{0,16},{16,32},{32,48},{48,64},{64,80},{80,96},{96,112},{112,0},{1... | collective-permute-start | bytes 393224 | tf_op jit(solution)/shard_map/ppermute | solution.py:21
  135.7 11.6 %collective-permute-start.5 = (bf16[4,3,16,1024]{3,2,1,0:T(8,128)(2,1)S(1)}, bf16[4,3,16,1024]{3,2,1,0:T(8,128)(2,1)S(1)}, u32[]{:S(2)}, u32[]{:S(2)}) collective-permute-start(bf16[4,3,16,1024]{3,2,1,0:T(8,128)(2,1)S(1)} %pad_maximum_fusion.6), channel_id=1, source_target_pairs={{0,1},{1,2},{2,3},{3,4},{4,5},{5,6},{6,7},{7,8},{8,9},{9,10},{10,1... | collective-permute-start | bytes 1179656 | tf_op jit(solution)/shard_map/ppermute | solution.py:21
  147.4 1.6 copy-start.26
  149.8 1.2 copy-start.13
  150.4 1.7 copy-start.18
  152.1 1.2 copy-start.19
  153.3 1.2 copy-start.20
  161.8 5.0 %copy-start.9 = (bf16[4,4,8,1024]{3,2,1,0:T(8,128)(2,1)S(1)}, bf16[4,4,8,1024]{3,2,1,0:T(8,128)(2,1)}, u32[]{:S(2)}) copy-start(bf16[4,4,8,1024]{3,2,1,0:T(8,128)(2,1)} %copy-done.8) | copy-start | bytes 786436
  172.9 8.1 %collective-permute-start.6 = (bf16[4,3,16,1024]{3,2,1,0:T(8,128)(2,1)S(1)}, bf16[4,3,16,1024]{3,2,1,0:T(8,128)(2,1)S(1)}, u32[]{:S(2)}, u32[]{:S(2)}) collective-permute-start(bf16[4,3,16,1024]{3,2,1,0:T(8,128)(2,1)S(1)} %slice.193), channel_id=1, source_target_pairs={{0,15},{1,0},{2,1},{3,2},{4,3},{5,4},{6,5},{7,6},{8,7},{9,8},{10,9... | collective-permute-start | bytes 1179656 | tf_op jit(solution)/shard_map/ppermute | solution.py:21
  181.4 2.5 %collective-permute-start.7 = (bf16[1,4,16,1024]{3,2,1,0:T(8,128)(2,1)S(1)}, bf16[1,4,16,1024]{3,2,1,0:T(8,128)(2,1)S(1)}, u32[]{:S(2)}, u32[]{:S(2)}) collective-permute-start(bf16[1,4,16,1024]{3,2,1,0:T(8,128)(2,1)S(1)} %fusion.44), channel_id=1, source_target_pairs={{0,112},{16,0},{32,16},{48,32},{64,48},{80,64},{96,80},{112,96},{1... | collective-permute-start | bytes 393224 | tf_op jit(solution)/shard_map/ppermute | solution.py:21
  184.3 1.2 copy-start.7
  185.5 52.0 %copy-start.1 = (bf16[1024,1536]{1,0:T(8,128)(2,1)S(1)}, bf16[1024,1536]{1,0:T(8,128)(2,1)}, u32[]{:S(2)}) copy-start(bf16[1024,1536]{1,0:T(8,128)(2,1)} %param.14) | copy-start | bytes 9437188
  225.4 11.5 %all-to-all-start.2 = ((bf16[16,4,1024]{2,1,0:T(4,128)(2,1)}), bf16[16,4,1024]{2,1,0:T(4,128)(2,1)S(1)}, u32[]{:S(2)}, u32[]{:S(2)}) async-start(bf16[16,4,1024]{2,1,0:T(4,128)(2,1)} %multiply_convert_fusion.4), calls=%async_computation.2 | async-start | bytes 262144 | tf_op jit(solution)/shard_map/all_to_all | solution.py:212
  (6 other events, 4.4 us)
where the time goes:
time: 239 us; the launch traced here: 238 us
  local copies, waits for them, and re-layouts  66.7 us (28%)
  waiting for transfers between devices  44.8 us (19%)
  blocking collectives  34.2 us (14%)
  other arithmetic  29.7 us (12%)
  matrix products  27.6 us (12%)
  starting transfers between devices  23.3 us (10%)
  between operations  11.2 us (5%)
    psum x4, blocking collectives, one_axis_at_a_time(): shard = lax.psum(shard, axis)  34.2 us
    ppermute x8, waiting for transfers between devices, from_behind(): return lax.ppermute(value, axis, pairs)  32.1 us
    dot_general x2, matrix products, window_core(): jnp.dot(normed.reshape(-1, model_width), w_qkv, preferred_element_type=jn...  10.9 us
    reshape x2, local copies, waits for them, and re-layouts, window_core(): packed.reshape(frame_count // WT, WT, row_count // WH, WH, column_count /...  9.85 us
    unnamed x56, local copies, waits for them, and re-layouts  9.14 us
    all_to_all x1, waiting for transfers between devices, per_device(): lax.all_to_all(picked, ROW, split_axis=0, concat_axis=0, tiled=True)  7.36 us
    all_to_all x1, starting transfers between devices, per_device(): lax.all_to_all(sent_rows, ROW, split_axis=0, concat_axis=0, tiled=True)  7.21 us
    all_to_all x1, starting transfers between devices, per_device(): lax.all_to_all(sent_index, ROW, split_axis=0, concat_axis=0, tiled=True)  7.15 us
  transfers between devices with their start and end apart: 11, of which 10 were waited for; matrix products, arithmetic and copies ran while one was open for 14% of the time, Pallas kernels for 0%

commit v1 on v0

v1 whole, which is shorter than its diff:
```python
import math

import jax
import jax.numpy as jnp
from jax import lax
from jax.experimental import pallas as pl
from jax.experimental.pallas import tpu as pltpu
from jax.sharding import Mesh
from jax.sharding import PartitionSpec as P

WT = 2
WH = 4
WW = 8
D = 1024
PIX = 1536
GROUP = PIX // 3
TOK = 256
WIN = WT * WH * WW
PAIRS = D // 128
SLOTS = 128
TM = ("tm_0", "tm_1")
ROW = ("row_0", "row_1")
ALL = TM + ROW
BF = jnp.bfloat16
F32 = jnp.float32
NT_DIMS = (((1,), (1,)), ((), ()))
TN_DIMS = (((0,), (0,)), ((), ()))
NN_DIMS = (((1,), (0,)), ((), ()))
VMEM = pltpu.MemorySpace.VMEM
SMEM = pltpu.MemorySpace.SMEM


def dot(a, b, dims):
    return lax.dot_general(a, b, dims, preferred_element_type=F32)


def lane_mean(values):
    return jnp.sum(values, axis=-1, keepdims=True) * (1.0 / values.shape[-1])


def normalise(values):
    center = values - lane_mean(values)
    scale = lax.rsqrt(lane_mean(center * center) + 1e-05)
    return center * scale, scale


def normalise_back(cotangent, normed, scale):
    return scale * (cotangent - lane_mean(cotangent) - normed * lane_mean(cotangent * normed))


def two_heads(rows):
    first = lax.broadcasted_iota(jnp.int32, rows.shape, 1) < 64
    zero = jnp.zeros_like(rows)
    return jnp.concatenate([jnp.where(first, rows, zero), jnp.where(first, zero, rows)], axis=0)


def own_head(rows):
    first = lax.broadcasted_iota(jnp.int32, (WIN, 128), 1) < 64
    return jnp.where(first, rows[:WIN], rows[WIN:])


def slot_one_hot(shift_ref, rows_ref, behind):
    place = rows_ref[:, D : D + 128].astype(F32).astype(jnp.int32)
    frame = place >> 6
    row = (place >> 4) & 3
    column = place & 15
    group = column >> 3
    slot = lax.broadcasted_iota(jnp.int32, (SLOTS, 128), 0) & 7
    lane = lax.broadcasted_iota(jnp.int32, (SLOTS, 128), 1)
    time_offset = jnp.where(group == 0, shift_ref[0, 0], shift_ref[0, 1])
    row_offset = jnp.where(group == 0, shift_ref[1, 0], shift_ref[1, 1])
    frame = frame + time_offset - 4 * behind
    row = row + row_offset - jnp.where(slot >= 4, 4, 0)
    inside = (place >= 0) & (frame >= 0) & (frame < 4) & (row >= 0) & (row < 4)
    token = (((frame >> 1) * 2 + group) * 64) + ((frame & 1) * 32) + row * 8 + (column & 7)
    token = jnp.where(inside, token, -1)
    halves = [jnp.where(token == lane + 128 * half, 1.0, 0.0) for half in range(2)]
    return jnp.concatenate(halves, axis=1).astype(BF)


def forward_kernel(
    shift_ref, own_ref, behind_ref, mask_ref, frames_ref, rows_ref, columns_ref, w_qkv_hbm, w_out_hbm,
    embedded_ref, residual_ref, qkv_ref, probs_ref, seen_ref, one_hot_ref,
    w_qkv_ref, w_out_ref, chosen_ref, normed_ref, heads_ref, sems,
):
    copies = [
        pltpu.make_async_copy(
            w_qkv_hbm.at[:, pl.ds(at * D, D)], w_qkv_ref.at[:, pl.ds(at * D, D)], sems.at[at]
        )
        for at in range(3)
    ]
    copies.append(pltpu.make_async_copy(w_out_hbm, w_out_ref, sems.at[3]))
    for copy in copies:
        copy.start()
    one_hot_ref[:SLOTS] = slot_one_hot(shift_ref, own_ref, 0)
    one_hot_ref[SLOTS:] = slot_one_hot(shift_ref, behind_ref, 1)
    own_hot = one_hot_ref[:SLOTS]
    behind_hot = one_hot_ref[SLOTS:]
    chosen_ref[...] = dot(own_hot, own_ref[:, :D], TN_DIMS) + dot(behind_hot, behind_ref[:, :D], TN_DIMS)
    ones = jnp.ones((2 * SLOTS, 128), BF)
    seen_ref[...] = dot(one_hot_ref[...], ones, TN_DIMS)

    for block in range(TOK // 16):
        window, half = divmod(block, 4)
        frame_pair, group = divmod(window, 2)
        at_frame = group * 4 + frame_pair * 2 + half // 2
        rows = pl.ds(block * 16, 16)
        start = jnp.where(
            jnp.concatenate([seen_ref[rows]] * 8, axis=1) > 0,
            chosen_ref[rows],
            mask_ref[...].astype(F32),
        )
        position = []
        for at in range(2):
            at_row = group * 4 + (half % 2) * 2 + at
            position.append(
                jnp.concatenate(
                    [
                        jnp.broadcast_to(frames_ref[at_frame : at_frame + 1], (8, 256)),
                        jnp.broadcast_to(rows_ref[at_row : at_row + 1], (8, 384)),
                        columns_ref[group * 8 : group * 8 + 8],
                    ],
                    axis=1,
                )
            )
        embedded = (start + jnp.concatenate(position, axis=0)).astype(BF)
        embedded_ref[rows] = embedded
        normed_ref[rows] = normalise(embedded.astype(F32))[0].astype(BF)

    for at in range(3):
        copies[at].wait()
        for part in range(2):
            cols = slice(at * D + part * 512, at * D + part * 512 + 512)
            qkv_ref[:, cols] = dot(normed_ref[...], w_qkv_ref[:, cols], NN_DIMS).astype(BF)

    def one_window(window, carry):
        rows = pl.ds(pl.multiple_of(window * WIN, WIN), WIN)
        for pair in range(PAIRS):
            cols = slice(pair * 128, pair * 128 + 128)
            q = qkv_ref[rows, pair * 128 : pair * 128 + 128]
            k = qkv_ref[rows, D + pair * 128 : D + pair * 128 + 128]
            v = qkv_ref[rows, 2 * D + pair * 128 : 2 * D + pair * 128 + 128]
            scores = dot(k, two_heads(q), NT_DIMS) * 0.125
            weights = jnp.exp(scores - jnp.max(scores, axis=0, keepdims=True))
            probs = (weights * (1.0 / jnp.sum(weights, axis=0, keepdims=True))).astype(BF)
            probs_ref[window, pair] = probs
            heads_ref[rows, cols] = own_head(dot(probs, v, TN_DIMS)).astype(BF)
        return carry

    lax.fori_loop(0, TOK // WIN, one_window, 0)
    copies[3].wait()
    for part in range(2):
        cols = slice(part * 512, part * 512 + 512)
        attn = dot(heads_ref[...], w_out_ref[:, cols], NN_DIMS).astype(BF)
        residual_ref[:, cols] = embedded_ref[:, cols].astype(F32) + attn.astype(F32)


def backward_kernel(
    shift_ref, embedded_ref, residual_ref, qkv_ref, probs_ref, seen_ref, one_hot_ref,
    own_px, row_px, time_px, corner_px, w_head_hbm, w_out_hbm, w_qkv_hbm,
    picked_ref, total_ref,
    px_ref, w_head_ref, w_out_ref, w_qkv_ref, normed_ref, scale_ref, predicted_ref, error_ref,
    narrow_ref, wide_ref, stream_ref, dqkv_ref, sems,
):
    pixel_copies = [
        pltpu.make_async_copy(own_px, px_ref.at[pl.ds(1, 4), pl.ds(3, 4)], sems.at[0]),
        pltpu.make_async_copy(row_px, px_ref.at[pl.ds(1, 4), pl.ds(0, 3)], sems.at[1]),
        pltpu.make_async_copy(time_px, px_ref.at[pl.ds(0, 1), pl.ds(3, 4)], sems.at[2]),
        pltpu.make_async_copy(corner_px, px_ref.at[pl.ds(0, 1), pl.ds(0, 3)], sems.at[3]),
    ]
    head_copy = pltpu.make_async_copy(w_head_hbm, w_head_ref, sems.at[4])
    out_copy = pltpu.make_async_copy(w_out_hbm, w_out_ref, sems.at[5])
    qkv_copy = pltpu.make_async_copy(w_qkv_hbm, w_qkv_ref, sems.at[6])
    head_copy.start()
    for copy in pixel_copies:
        copy.start()
    out_copy.start()
    qkv_copy.start()

    def tokens_of(block):
        return pl.ds(pl.multiple_of(block * 16, 16), 16)

    def head_norm(block, carry):
        rows = tokens_of(block)
        normed, scale = normalise(residual_ref[rows])
        normed_ref[rows] = normed
        scale_ref[rows] = jnp.broadcast_to(scale, (16, 128))
        narrow_ref[rows] = normed.astype(BF)
        return carry

    lax.fori_loop(0, TOK // 16, head_norm, 0, unroll=2)
    head_copy.wait()
    for copy in pixel_copies:
        copy.wait()
    for part in range(3):
        cols = slice(part * GROUP, part * GROUP + GROUP)
        predicted_ref[...] = dot(narrow_ref[...], w_head_ref[:, cols], NN_DIMS)

        def pixel_block(block, carry, cols=cols):
            at_frame = block // 2
            half = block % 2
            for group in range(2):
                rows = tokens_of(((at_frame // 2) * 2 + group) * 4 + (at_frame % 2) * 2 + half)
                targets = []
                for at in range(2):
                    raw = px_ref[
                        at_frame - shift_ref[0, group] + 1,
                        half * 2 + at - shift_ref[1, group] + 3,
                        group * 8 : group * 8 + 8,
                        cols,
                    ].astype(F32)
                    center = raw - lane_mean(raw)
                    spread = jnp.sqrt(jnp.sum(center * center, axis=-1, keepdims=True) * (1.0 / (GROUP - 1)))
                    targets.append(center * (1.0 / (spread + 1e-06)))
                masked = 1.0 - jnp.concatenate([seen_ref[rows]] * 4, axis=1)
                gap = predicted_ref[rows] - jnp.concatenate(targets, axis=0)
                error_ref[rows, cols] = (masked * gap).astype(BF)
            return carry

        lax.fori_loop(0, 8, pixel_block, 0)

    for part in range(2):
        cols = slice(part * 512, part * 512 + 512)
        wide_ref[:, cols] = dot(error_ref[...], w_head_ref[cols, :], NT_DIMS)

    def head_norm_back(block, carry):
        rows = tokens_of(block)
        scale = jnp.concatenate([scale_ref[rows]] * 8, axis=1)
        cotangent = wide_ref[rows].astype(BF).astype(F32)
        grad = normalise_back(cotangent, normed_ref[rows], scale)
        stream_ref[rows] = grad
        narrow_ref[rows] = grad.astype(BF)
        return carry

    lax.fori_loop(0, TOK // 16, head_norm_back, 0, unroll=2)
    out_copy.wait()
    d_heads = dot(narrow_ref[...], w_out_ref[...], NT_DIMS).astype(BF)
    narrow_ref[...] = d_heads

    def one_window(window, carry):
        rows = pl.ds(pl.multiple_of(window * WIN, WIN), WIN)
        for pair in range(PAIRS):
            cols = [slice(at * D + pair * 128, at * D + pair * 128 + 128) for at in range(3)]
            q_heads = two_heads(qkv_ref[rows, cols[0]])
            k = qkv_ref[rows, cols[1]]
            v = qkv_ref[rows, cols[2]]
            out_heads = two_heads(narrow_ref[rows, cols[0]])
            narrow_probs = probs_ref[window, pair]
            probs = narrow_probs.astype(F32)
            d_probs = dot(v, out_heads, NT_DIMS).astype(BF).astype(F32)
            mean = jnp.sum(d_probs * probs, axis=0, keepdims=True)
            d_scores = (probs * (d_probs - mean) * 0.125).astype(BF)
            dqkv_ref[rows, cols[2]] = dot(narrow_probs, out_heads, NN_DIMS).astype(BF)
            dqkv_ref[rows, cols[1]] = dot(d_scores, q_heads, NN_DIMS).astype(BF)
            dqkv_ref[rows, cols[0]] = own_head(dot(d_scores, k, TN_DIMS)).astype(BF)
        return carry

    lax.fori_loop(0, TOK // WIN, one_window, 0)
    qkv_copy.wait()
    for part in range(2):
        cols = slice(part * 512, part * 512 + 512)
        wide_ref[:, cols] = dot(dqkv_ref[...], w_qkv_ref[cols, :], NT_DIMS)

    def first_norm_back(block, carry):
        rows = tokens_of(block)
        normed, scale = normalise(embedded_ref[rows].astype(F32))
        cotangent = wide_ref[rows].astype(BF).astype(F32)
        grad = stream_ref[rows] + normalise_back(cotangent, normed, scale)
        narrow_ref[rows] = grad.astype(BF)
        masked = 1.0 - jnp.concatenate([seen_ref[rows]] * 8, axis=1)
        part = masked * grad
        return carry + part[:8] + part[8:]

    total_ref[...] = lax.fori_loop(0, TOK // 16, first_norm_back, jnp.zeros((8, D), F32), unroll=2)
    picked_ref[...] = dot(one_hot_ref[...], narrow_ref[...], NN_DIMS).astype(BF)


def sinusoid(coordinate, channel_count):
    half_count = channel_count // 2
    frequency = jnp.exp(-math.log(10000.0) * jnp.arange(half_count, dtype=F32) / half_count)
    angles = coordinate.astype(F32)[..., None] * frequency
    return jnp.concatenate([jnp.sin(angles), jnp.cos(angles)], axis=-1)


def move(value, axis, steps):
    count = lax.axis_size(axis)
    return lax.ppermute(value, axis, [(at, (at + steps) % count) for at in range(count)])


def move_corner(value):
    count_tm = lax.axis_size(TM)
    count_row = lax.axis_size(ROW)
    pairs = [
        (i * count_row + d, (i + 1) % count_tm * count_row + (d + 1) % count_row)
        for i in range(count_tm)
        for d in range(count_row)
    ]
    return lax.ppermute(value, ALL, pairs)


def per_device(visible, slot_pos, window_shift, mask_token, w_qkv, w_out, w_head, pixels):
    frame_count, row_count = pixels.shape[:2]
    peers, slots = slot_pos.shape[2:]
    rows = visible.reshape(peers, slots, D)
    places = slot_pos.reshape(peers, slots).astype(BF)
    packed = jnp.concatenate([rows, jnp.broadcast_to(places[..., None], (peers, slots, 128))], axis=-1)
    packed = jnp.concatenate([packed, jnp.roll(packed, 1, axis=0)], axis=1)
    own = lax.all_to_all(packed, ROW, split_axis=0, concat_axis=0, tiled=True).reshape(SLOTS, D + 128)
    behind = move(own, TM, 1)

    row_px = move(pixels[:, 1:], ROW, 1)
    time_px = move(pixels[3:], TM, 1)
    corner_px = move_corner(pixels[3:, 1:])

    local = jnp.arange(4, dtype=jnp.int32)
    frame_total = frame_count * lax.axis_size(TM)
    row_total = row_count * lax.axis_size(ROW)
    frames = (lax.axis_index(TM) * frame_count + local[None] - window_shift[0][:, None]) % frame_total
    band = (lax.axis_index(ROW) * row_count + local[None] - window_shift[1][:, None]) % row_total
    frame_table = sinusoid(frames.reshape(-1), 256)
    row_table = sinusoid(band.reshape(-1), 384)
    column_table = sinusoid(jnp.arange(16, dtype=jnp.int32), 384)

    vmem = pl.BlockSpec(memory_space=VMEM)
    smem = pl.BlockSpec(memory_space=SMEM)
    hbm = pl.BlockSpec(memory_space=pl.ANY)
    embedded, residual, qkv, probs, seen, one_hot = pl.pallas_call(
        forward_kernel,
        name="forward_part",
        in_specs=[smem] + [vmem] * 6 + [hbm] * 2,
        out_specs=[vmem] * 6,
        out_shape=[
            jax.ShapeDtypeStruct((TOK, D), BF),
            jax.ShapeDtypeStruct((TOK, D), F32),
            jax.ShapeDtypeStruct((TOK, 3 * D), BF),
            jax.ShapeDtypeStruct((TOK // WIN, PAIRS, WIN, 128), BF),
            jax.ShapeDtypeStruct((TOK, 128), F32),
            jax.ShapeDtypeStruct((2 * SLOTS, TOK), BF),
        ],
        scratch_shapes=[
            pltpu.VMEM((D, 3 * D), BF),
            pltpu.VMEM((D, D), BF),
            pltpu.VMEM((TOK, D), F32),
            pltpu.VMEM((TOK, D), BF),
            pltpu.VMEM((TOK, D), BF),
            pltpu.SemaphoreType.DMA((4,)),
        ],
        compiler_params=pltpu.CompilerParams(vmem_limit_bytes=28 << 20),
    )(
        window_shift, own, behind, mask_token.reshape(1, D), frame_table, row_table, column_table,
        w_qkv, w_out,
    )
    picked, total = pl.pallas_call(
        backward_kernel,
        name="backward_part",
        in_specs=[smem] + [vmem] * 6 + [hbm] * 7,
        out_specs=[vmem] * 2,
        out_shape=[
            jax.ShapeDtypeStruct((2 * SLOTS, D), BF),
            jax.ShapeDtypeStruct((8, D), F32),
        ],
        scratch_shapes=[
            pltpu.VMEM((5, 7, 16, PIX), BF),
            pltpu.VMEM((D, PIX), BF),
            pltpu.VMEM((D, D), BF),
            pltpu.VMEM((D, 3 * D), BF),
            pltpu.VMEM((TOK, D), F32),
            pltpu.VMEM((TOK, 128), F32),
            pltpu.VMEM((TOK, GROUP), F32),
            pltpu.VMEM((TOK, PIX), BF),
            pltpu.VMEM((TOK, D), BF),
            pltpu.VMEM((TOK, D), F32),
            pltpu.VMEM((TOK, D), F32),
            pltpu.VMEM((TOK, 3 * D), BF),
            pltpu.SemaphoreType.DMA((7,)),
        ],
        compiler_params=pltpu.CompilerParams(vmem_limit_bytes=36 << 20),
    )(
        window_shift, embedded, residual, qkv, probs, seen, one_hot,
        pixels, row_px, time_px, corner_px, w_head, w_out, w_qkv,
    )
    mine = picked[:SLOTS] + move(picked[SLOTS:], TM, -1)
    local_total = jnp.sum(total, axis=0).reshape(8, 128)
    local_total = local_total + move(local_total, "tm_1", 1)
    turned = [move(local_total, "tm_0", step) for step in (1, 2, 3)]
    local_total = (local_total + turned[1]) + (turned[0] + turned[2])
    high = local_total.astype(BF)
    low = (local_total - high.astype(F32)).astype(BF)
    sums = jnp.broadcast_to(jnp.concatenate([high, low], axis=1)[None], (peers, 8, 256))
    sent = jnp.concatenate([mine.reshape(peers, 2 * slots, D), sums], axis=-1)
    back = lax.all_to_all(sent, ROW, split_axis=0, concat_axis=0, tiled=True)
    d_visible = back[:, :slots, :D] + jnp.roll(back[:, slots:, :D], -1, axis=0)
    halves = jnp.sum(back[:, :, D:].astype(F32), axis=0)
    grad_scale = (frame_total * row_total * pixels.shape[2]) ** (-0.5)
    d_mask = (halves[:, :128] + halves[:, 128:]).reshape(D) * grad_scale
    return (d_visible.reshape(visible.shape), d_mask)


def solution(mesh):
    torus = Mesh(mesh.devices.reshape(4, 2, 4, 4), ALL)
    return jax.shard_map(
        per_device,
        mesh=torus,
        in_specs=(
            P(TM, ROW, None, None, None),
            P(TM, ROW, None, None),
            P(),
            P(),
            P(),
            P(),
            P(),
            P(TM, ROW, None, None),
        ),
        out_specs=(P(TM, ROW, None, None, None), P()),
        check_vma=False,
    )
```

time: 239 us -> 106 us (0.44)
  local copies, waits for them, and re-layouts: 66.7 us -> 14.2 us
  Pallas kernels: 0 us -> 37 us
  waiting for transfers between devices: 44.8 us -> 11.5 us
  matrix products: 27.6 us -> 0 us
  other arithmetic: 29.7 us -> 4.8 us
  blocking collectives: 34.2 us -> 18.1 us
  between operations: 11.2 us -> 0.86 us
  starting transfers between devices: 23.3 us -> 18 us
    pallas_call x0 -> x2, Pallas kernels: none -> 37 us  [the longest x1 23 us: per_device(): pl.pallas_call(backward_kernel, name='backward_part', in_specs=[smem] + [...]
    psum x4 -> x0, blocking collectives: 34.2 us -> none  [one_axis_at_a_time(): shard = lax.psum(shard, axis)]
    dot_general x10 -> x0, matrix products: 23.9 us -> none  [the longest x2 10.9 us: window_core(): jnp.dot(normed.reshape(-1, model_width), w_qkv, preferred_element_type=jn...]
    ppermute x8 -> x9, waiting for transfers between devices: 32.1 us -> 11.5 us  [the longest x8 11.5 us: move(): lax.ppermute(value, axis, [(at, (at + steps) % count) for at in range(cou...]
    all_to_all x0 -> x1, blocking collectives: none -> 18.1 us  [per_device(): back = lax.all_to_all(sent, ROW, split_axis=0, concat_axis=0, tiled=True)]
    reshape x5 -> x1, local copies, waits for them, and re-layouts: 15.9 us -> 0.69 us  [per_device(): mask_token.reshape(1, D)]
    all_to_all x3 -> x1, waiting for transfers between devices: 12.7 us -> 0.01 us  [per_device(): lax.all_to_all(packed, ROW, split_axis=0, concat_axis=0, tiled=True)]
    all_to_all x3 -> x1, starting transfers between devices: 17.9 us -> 7.15 us  [per_device(): lax.all_to_all(packed, ROW, split_axis=0, concat_axis=0, tiled=True)]
  transfers between devices with their start and end apart: 11 -> 10, of which waited for: 10 -> 4; matrix products, arithmetic and copies ran while one was open for 14% -> 6% of each run, Pallas kernels for 0% -> 13%
where the time goes in v1:
time: 106 us; the launch traced here: 104 us
  Pallas kernels  37 us (35%)
  blocking collectives  18.1 us (17%)
  starting transfers between devices  18 us (17%)
  local copies, waits for them, and re-layouts  14.2 us (13%)
  waiting for transfers between devices  11.5 us (11%)
  other arithmetic  4.8 us (5%)
    pallas_call x1, Pallas kernels, per_device(): pl.pallas_call(backward_kernel, name='backward_part', in_specs=[smem] + [...  23 us
    all_to_all x1, blocking collectives, per_device(): back = lax.all_to_all(sent, ROW, split_axis=0, concat_axis=0, tiled=True)  18.1 us
    pallas_call x1, Pallas kernels, per_device(): pl.pallas_call(forward_kernel, name='forward_part', in_specs=[smem] + [vm...  14 us
    ppermute x8, waiting for transfers between devices, move(): lax.ppermute(value, axis, [(at, (at + steps) % count) for at in range(cou...  11.5 us
    unnamed x20, local copies, waits for them, and re-layouts  7.86 us
    ppermute x8, starting transfers between devices, move(): lax.ppermute(value, axis, [(at, (at + steps) % count) for at in range(cou...  7.65 us
    all_to_all x1, starting transfers between devices, per_device(): lax.all_to_all(packed, ROW, split_axis=0, concat_axis=0, tiled=True)  7.15 us
    ppermute x1, starting transfers between devices, move_corner(): return lax.ppermute(value, ALL, pairs)  3.17 us
  transfers between devices with their start and end apart: 10, of which 4 were waited for; matrix products, arithmetic and copies ran while one was open for 6% of the time, Pallas kernels for 13%

profile of v1, /device:TPU:0, one launch (start us, length us, event | category | flops | bytes accessed | tf_op | source)
XLA Modules:
  0.0 104.4 jit_solution(7857650589707218626)
XLA Ops:
  0.7 0.8 convert_bitcast_fusion
  1.5 0.1 copy.10
  1.7 1.8 %fusion.1 = bf16[16,8,1152]{2,1,0:T(8,128)(2,1)} fusion(bf16[16,4,128]{2,1,0:T(4,128)(2,1)S(1)} %broadcast_in_dim.4, bf16[16,4,1024]{2,1,0:T(4,128)(2,1)} %bitcast.20), kind=kLoop, calls=%fused_computation.3 | loop fusion | flops 1769472 | bytes 442368 | tf_op jit(solution)/shard_map/concatenate | solution.py:307
  3.5 7.1 %all-to-all-start = ((bf16[16,8,1152]{2,1,0:T(8,128)(2,1)}), bf16[16,8,1152]{2,1,0:T(8,128)(2,1)S(1)}, u32[]{:S(2)}, u32[]{:S(2)}) async-start(bf16[16,8,1152]{2,1,0:T(8,128)(2,1)} %fusion.1), calls=%async_computation | async-start | bytes 589824 | tf_op jit(solution)/shard_map/all_to_all | solution.py:308
  10.7 1.9 %slice.56 = bf16[4,3,16,1536]{3,2,1,0:T(8,128)(2,1)} slice(bf16[4,4,16,1536]{3,2,1,0:T(8,128)(2,1)} %own_px.1), slice={[0:4], [1:4], [0:16], [0:1536]} | slice | bytes 1179648 | tf_op jit(solution)/shard_map/slice | solution.py:311
  12.6 1.9 %collective-permute-start.1 = (bf16[4,3,16,1536]{3,2,1,0:T(8,128)(2,1)}, bf16[4,3,16,1536]{3,2,1,0:T(8,128)(2,1)S(1)}, u32[]{:S(2)}, u32[]{:S(2)}) collective-permute-start(bf16[4,3,16,1536]{3,2,1,0:T(8,128)(2,1)} %slice.56), channel_id=1, source_target_pairs={{0,1},{1,2},{2,3},{3,4},{4,5},{5,6},{6,7},{7,8},{8,9},{9,10},{10,1... | collective-permute-start | bytes 1769480 | tf_op jit(solution)/shard_map/ppermute | solution.py:287
  14.5 1.6 %slice.57 = bf16[1,4,16,1536]{3,2,1,0:T(8,128)(2,1)} slice(bf16[4,4,16,1536]{3,2,1,0:T(8,128)(2,1)} %own_px.1), slice={[3:4], [0:4], [0:16], [0:1536]} | slice | bytes 393216 | tf_op jit(solution)/shard_map/slice | solution.py:312
  16.2 0.9 slice.58
  17.1 3.2 %collective-permute-start.3 = (bf16[1,3,16,1536]{3,2,1,0:T(8,128)(2,1)S(1)}, bf16[1,3,16,1536]{3,2,1,0:T(8,128)(2,1)S(1)}, u32[]{:S(2)}, u32[]{:S(2)}) collective-permute-start(bf16[1,3,16,1536]{3,2,1,0:T(8,128)(2,1)S(1)} %slice.58), channel_id=1, source_target_pairs={{0,17},{1,18},{2,19},{3,20},{4,21},{5,22},{6,23},{7,24},{8,25},{9,... | collective-permute-start | bytes 442376 | tf_op jit(solution)/shard_map/ppermute | solution.py:298
  20.3 0.8 slice_bitcast_fusion
  21.3 0.1 multiply_sine_fusion.1
  21.5 0.1 multiply_sine_fusion.2
  21.6 0.1 multiply_sine_fusion
  21.8 0.7 reshape.111.mask_ref
  22.6 6.5 %collective-permute-done.behind_ref = bf16[128,1152]{1,0:T(8,128)(2,1)S(1)} collective-permute-done((bf16[128,1152]{1,0:T(8,128)(2,1)S(1)}, bf16[128,1152]{1,0:T(8,128)(2,1)S(1)}, u32[]{:S(2)}, u32[]{:S(2)}) %collective-permute-start) | collective-permute-done | bytes 294944 | tf_op jit(solution)/shard_map/ppermute | solution.py:287
  29.1 2.8 %copy-done = bf16[1024,3072]{1,0:T(8,128)(2,1)S(1)} copy-done((bf16[1024,3072]{1,0:T(8,128)(2,1)S(1)}, bf16[1024,3072]{1,0:T(8,128)(2,1)}, u32[]{:S(2)}) %copy-start) | copy-done | bytes 6291480
  31.9 14.0 %forward_part.1 = (bf16[256,1024]{1,0:T(8,128)(2,1)S(1)}, f32[256,1024]{1,0:T(8,128)S(1)}, bf16[256,3072]{1,0:T(8,128)(2,1)S(1)}, bf16[4,8,64,128]{3,2,1,0:T(8,1...) custom-call(s32[2,2]{1,0:T(2,128)S(1)} %copy-done.9, bf16[128,1152]{1,0:T(8,128)(2,1)S(1)} %bitcast.19, ...), custom_call_target="tpu_custom_call" | custom-call | tf_op jit(solution)/shard_map/forward_part/pallas_call | solution.py:327
  45.9 0.7 copy-done.7
  46.6 0.7 copy-done.5
  47.3 1.9 %copy-done.4 = bf16[1024,1536]{1,0:T(8,128)(2,1)S(1)} copy-done((bf16[1024,1536]{1,0:T(8,128)(2,1)S(1)}, bf16[1024,1536]{1,0:T(8,128)(2,1)}, u32[]{:S(2)}) %copy-start.4) | copy-done | bytes 3145752
  49.2 0.9 copy-done.6
  50.1 0.9 copy-done.8
  51.0 23.0 %backward_part.1 = (bf16[256,1024]{1,0:T(8,128)(2,1)S(1)}, f32[8,1024]{1,0:T(8,128)S(1)}) custom-call(s32[2,2]{1,0:T(2,128)S(1)} %copy-done.9, bf16[256,1024]{1,0:T(8,128)(2,1)S(1)} %get-tuple-element.10.embedded_ref, f32[256,1024]{1,0:T(8,128)S(1)} %get-tuple-element.11.residual_ref, bf16[256,3072]{1,0:T(8,128)(2,1)S(1)} %get-tuple-element.12.qkv_ref, ...), custom_call_target="tpu_custom_call" | custom-call | tf_op jit(solution)/shard_map/backward_part/pallas_call | solution.py:353
  74.0 0.1 collective-permute-start.5
  74.1 1.2 %collective-permute-done.5 = f32[8,128]{1,0:T(8,128)S(1)} collective-permute-done((f32[8,128]{1,0:T(8,128)S(1)}, f32[8,128]{1,0:T(8,128)S(1)}, u32[]{:S(2)}, u32[]{:S(2)}) %collective-permute-start.5) | collective-permute-done | bytes 4128 | tf_op jit(solution)/shard_map/ppermute | solution.py:287
  75.3 2.4 %collective-permute-start.6 = (f32[8,128]{1,0:T(8,128)S(1)}, f32[8,128]{1,0:T(8,128)S(1)}, u32[]{:S(2)}, u32[]{:S(2)}) collective-permute-start(f32[8,128]{1,0:T(8,128)S(1)} %bitcast_add_fusion), channel_id=1, source_target_pairs={{0,64},{32,96},{64,0},{96,32},{1,65},{33,97},{65,1},{97,33},{2,66}... | collective-permute-start | bytes 12296 | tf_op jit(solution)/shard_map/ppermute | solution.py:287
  77.6 3.2 %collective-permute-start.8 = (f32[8,128]{1,0:T(8,128)S(1)}, f32[8,128]{1,0:T(8,128)S(1)}, u32[]{:S(2)}, u32[]{:S(2)}) collective-permute-start(f32[8,128]{1,0:T(8,128)S(1)} %bitcast_add_fusion), channel_id=1, source_target_pairs={{0,96},{32,0},{64,32},{96,64},{1,97},{33,1},{65,33},{97,65},{2,98}... | collective-permute-start | bytes 12296 | tf_op jit(solution)/shard_map/ppermute | solution.py:287
  80.9 1.5 %collective-permute-done.7 = f32[8,128]{1,0:T(8,128)S(1)} collective-permute-done((f32[8,128]{1,0:T(8,128)S(1)}, f32[8,128]{1,0:T(8,128)S(1)}, u32[]{:S(2)}, u32[]{:S(2)}) %collective-permute-start.7) | collective-permute-done | bytes 4128 | tf_op jit(solution)/shard_map/ppermute | solution.py:287
  82.5 2.3 %collective-permute-done.4 = bf16[128,1024]{1,0:T(8,128)(2,1)S(1)} collective-permute-done((bf16[128,1024]{1,0:T(8,128)(2,1)S(1)}, bf16[128,1024]{1,0:T(8,128)(2,1)S(1)}, u32[]{:S(2)}, u32[]{:S(2)}) %collective-permute-start.4) | collective-permute-done | bytes 262176 | tf_op jit(solution)/shard_map/ppermute | solution.py:287
  84.9 18.1 %all_to_all.10 = bf16[16,8,1280]{2,1,0:T(8,128)(2,1)S(1)} all-to-all(bf16[16,8,1280]{2,1,0:T(8,128)(2,1)S(1)} %pad_maximum_fusion), channel_id=1, replica_groups=mesh['tm_0'=4,'tm_1'=2,'row_0'=4,'row_1'=4] {'row_0','row_1'}, dimensions={0} | all-to-all | bytes 655360 | tf_op jit(solution)/shard_map/all_to_all | solution.py:391
  103.0 0.6 fusion.4
  103.7 0.8 fusion.2
  (49 shorter events, 0.8 us)
Async XLA Ops:
  0.6 28.5 %copy-start.9 = (s32[2,2]{1,0:T(2,128)S(1)}, s32[2,2]{1,0:T(2,128)}, u32[]{:S(2)}) copy-start(s32[2,2]{1,0:T(2,128)} %shift_ref.3) | copy-start | bytes 52
  0.6 28.5 %copy-start.2 = (bf16[1024,1024]{1,0:T(8,128)(2,1)S(1)}, bf16[1024,1024]{1,0:T(8,128)(2,1)}, u32[]{:S(2)}) copy-start(bf16[1024,1024]{1,0:T(8,128)(2,1)} %w_out_hbm.3) | copy-start | bytes 6291460
  3.5 18.2 %all-to-all-start = ((bf16[16,8,1152]{2,1,0:T(8,128)(2,1)}), bf16[16,8,1152]{2,1,0:T(8,128)(2,1)S(1)}, u32[]{:S(2)}, u32[]{:S(2)}) async-start(bf16[16,8,1152]{2,1,0:T(8,128)(2,1)} %fusion.1), calls=%async_computation | async-start | bytes 589824 | tf_op jit(solution)/shard_map/all_to_all | solution.py:308
  12.6 34.6 %collective-permute-start.1 = (bf16[4,3,16,1536]{3,2,1,0:T(8,128)(2,1)}, bf16[4,3,16,1536]{3,2,1,0:T(8,128)(2,1)S(1)}, u32[]{:S(2)}, u32[]{:S(2)}) collective-permute-start(bf16[4,3,16,1536]{3,2,1,0:T(8,128)(2,1)} %slice.56), channel_id=1, source_target_pairs={{0,1},{1,2},{2,3},{3,4},{4,5},{5,6},{6,7},{7,8},{8,9},{9,10},{10,1... | collective-permute-start | bytes 1769480 | tf_op jit(solution)/shard_map/ppermute | solution.py:287
  16.2 30.4 %collective-permute-start.2 = (bf16[1,4,16,1536]{3,2,1,0:T(8,128)(2,1)}, bf16[1,4,16,1536]{3,2,1,0:T(8,128)(2,1)S(1)}, u32[]{:S(2)}, u32[]{:S(2)}) collective-permute-start(bf16[1,4,16,1536]{3,2,1,0:T(8,128)(2,1)} %slice.57), channel_id=1, source_target_pairs={{0,16},{16,32},{32,48},{48,64},{64,80},{80,96},{96,112},{112,0},{1... | collective-permute-start | bytes 589832 | tf_op jit(solution)/shard_map/ppermute | solution.py:287
  17.1 28.8 %collective-permute-start.3 = (bf16[1,3,16,1536]{3,2,1,0:T(8,128)(2,1)S(1)}, bf16[1,3,16,1536]{3,2,1,0:T(8,128)(2,1)S(1)}, u32[]{:S(2)}, u32[]{:S(2)}) collective-permute-start(bf16[1,3,16,1536]{3,2,1,0:T(8,128)(2,1)S(1)} %slice.58), channel_id=1, source_target_pairs={{0,17},{1,18},{2,19},{3,20},{4,21},{5,22},{6,23},{7,24},{8,25},{9,... | collective-permute-start | bytes 442376 | tf_op jit(solution)/shard_map/ppermute | solution.py:298
  21.7 7.4 %collective-permute-start = (bf16[128,1152]{1,0:T(8,128)(2,1)S(1)}, bf16[128,1152]{1,0:T(8,128)(2,1)S(1)}, u32[]{:S(2)}, u32[]{:S(2)}) collective-permute-start(bf16[128,1152]{1,0:T(8,128)(2,1)S(1)} %bitcast.18), channel_id=1, source_target_pairs={{0,16},{16,32},{32,48},{48,64},{64,80},{80,96},{96,112},{112,0},{1... | collective-permute-start | bytes 884744 | tf_op jit(solution)/shard_map/ppermute | solution.py:287
  29.1 2.8 %copy-start = (bf16[1024,3072]{1,0:T(8,128)(2,1)S(1)}, bf16[1024,3072]{1,0:T(8,128)(2,1)}, u32[]{:S(2)}) copy-start(bf16[1024,3072]{1,0:T(8,128)(2,1)} %w_qkv_hbm.3) | copy-start | bytes 18874372
  31.9 15.4 %copy-start.1 = (bf16[1024,3072]{1,0:T(8,128)(2,1)S(1)}, bf16[1024,3072]{1,0:T(8,128)(2,1)}, u32[]{:S(2)}) copy-start(bf16[1024,3072]{1,0:T(8,128)(2,1)} %w_qkv_hbm.3) | copy-start | bytes 18874372
  31.9 15.4 %copy-start.3 = (bf16[4,4,16,1536]{3,2,1,0:T(8,128)(2,1)S(1)}, bf16[4,4,16,1536]{3,2,1,0:T(8,128)(2,1)}, u32[]{:S(2)}) copy-start(bf16[4,4,16,1536]{3,2,1,0:T(8,128)(2,1)} %own_px.1) | copy-start | bytes 2359300
  45.9 0.7 copy-start.7
  46.6 0.7 copy-start.5
  47.3 1.9 %copy-start.4 = (bf16[1024,1536]{1,0:T(8,128)(2,1)S(1)}, bf16[1024,1536]{1,0:T(8,128)(2,1)}, u32[]{:S(2)}) copy-start(bf16[1024,1536]{1,0:T(8,128)(2,1)} %w_head_hbm.1) | copy-start | bytes 9437188
  49.1 0.9 copy-start.6
  50.1 0.9 copy-start.8
  74.0 1.2 %collective-permute-start.5 = (f32[8,128]{1,0:T(8,128)S(1)}, f32[8,128]{1,0:T(8,128)S(1)}, u32[]{:S(2)}, u32[]{:S(2)}) collective-permute-start(f32[8,128]{1,0:T(8,128)S(1)} %bitcast.21), channel_id=1, source_target_pairs={{0,16},{16,0},{1,17},{17,1},{2,18},{18,2},{3,19},{19,3},{4,20},{20... | collective-permute-start | bytes 12296 | tf_op jit(solution)/shard_map/ppermute | solution.py:287
  75.3 5.7 %collective-permute-start.6 = (f32[8,128]{1,0:T(8,128)S(1)}, f32[8,128]{1,0:T(8,128)S(1)}, u32[]{:S(2)}, u32[]{:S(2)}) collective-permute-start(f32[8,128]{1,0:T(8,128)S(1)} %bitcast_add_fusion), channel_id=1, source_target_pairs={{0,64},{32,96},{64,0},{96,32},{1,65},{33,97},{65,1},{97,33},{2,66}... | collective-permute-start | bytes 12296 | tf_op jit(solution)/shard_map/ppermute | solution.py:287
  77.6 4.8 %collective-permute-start.7 = (f32[8,128]{1,0:T(8,128)S(1)}, f32[8,128]{1,0:T(8,128)S(1)}, u32[]{:S(2)}, u32[]{:S(2)}) collective-permute-start(f32[8,128]{1,0:T(8,128)S(1)} %bitcast_add_fusion), channel_id=1, source_target_pairs={{0,32},{32,64},{64,96},{96,0},{1,33},{33,65},{65,97},{97,1},{2,34}... | collective-permute-start | bytes 12296 | tf_op jit(solution)/shard_map/ppermute | solution.py:287
  77.6 4.8 %collective-permute-start.8 = (f32[8,128]{1,0:T(8,128)S(1)}, f32[8,128]{1,0:T(8,128)S(1)}, u32[]{:S(2)}, u32[]{:S(2)}) collective-permute-start(f32[8,128]{1,0:T(8,128)S(1)} %bitcast_add_fusion), channel_id=1, source_target_pairs={{0,96},{32,0},{64,32},{96,64},{1,97},{33,1},{65,33},{97,65},{2,98}... | collective-permute-start | bytes 12296 | tf_op jit(solution)/shard_map/ppermute | solution.py:287
  80.9 3.9 %collective-permute-start.4 = (bf16[128,1024]{1,0:T(8,128)(2,1)S(1)}, bf16[128,1024]{1,0:T(8,128)(2,1)S(1)}, u32[]{:S(2)}, u32[]{:S(2)}) collective-permute-start(bf16[128,1024]{1,0:T(8,128)(2,1)S(1)} %slice.60), channel_id=1, source_target_pairs={{0,112},{16,0},{32,16},{48,32},{64,48},{80,64},{96,80},{112,96},{1... | collective-permute-start | bytes 786440 | tf_op jit(solution)/shard_map/ppermute | solution.py:287

commit v2 on v1

--- a/solution.py
+++ b/solution.py
@@ -133,21 +133,24 @@
             cols = slice(at * D + part * 512, at * D + part * 512 + 512)
             qkv_ref[:, cols] = dot(normed_ref[...], w_qkv_ref[:, cols], NN_DIMS).astype(BF)
 
-    def one_window(window, carry):
-        rows = pl.ds(pl.multiple_of(window * WIN, WIN), WIN)
-        for pair in range(PAIRS):
-            cols = slice(pair * 128, pair * 128 + 128)
+    def one_window(window):
+        rows = slice(window * WIN, window * WIN + WIN)
+        scores = []
+        for pair in range(PAIRS):
             q = qkv_ref[rows, pair * 128 : pair * 128 + 128]
             k = qkv_ref[rows, D + pair * 128 : D + pair * 128 + 128]
+            scores.append(dot(k, two_heads(q), NT_DIMS) * 0.125)
+        probs = []
+        for pair in range(PAIRS):
+            weights = jnp.exp(scores[pair] - jnp.max(scores[pair], axis=0, keepdims=True))
+            probs.append((weights * (1.0 / jnp.sum(weights, axis=0, keepdims=True))).astype(BF))
+            probs_ref[window, pair] = probs[pair]
+        for pair in range(PAIRS):
             v = qkv_ref[rows, 2 * D + pair * 128 : 2 * D + pair * 128 + 128]
-            scores = dot(k, two_heads(q), NT_DIMS) * 0.125
-            weights = jnp.exp(scores - jnp.max(scores, axis=0, keepdims=True))
-            probs = (weights * (1.0 / jnp.sum(weights, axis=0, keepdims=True))).astype(BF)
-            probs_ref[window, pair] = probs
-            heads_ref[rows, cols] = own_head(dot(probs, v, TN_DIMS)).astype(BF)
-        return carry
-
-    lax.fori_loop(0, TOK // WIN, one_window, 0)
+            heads_ref[rows, pair * 128 : pair * 128 + 128] = own_head(dot(probs[pair], v, TN_DIMS)).astype(BF)
+
+    for window in range(TOK // WIN):
+        one_window(window)
     copies[3].wait()
     for part in range(2):
         cols = slice(part * 512, part * 512 + 512)
@@ -162,20 +165,17 @@
     px_ref, w_head_ref, w_out_ref, w_qkv_ref, normed_ref, scale_ref, predicted_ref, error_ref,
     narrow_ref, wide_ref, stream_ref, dqkv_ref, sems,
 ):
-    pixel_copies = [
-        pltpu.make_async_copy(own_px, px_ref.at[pl.ds(1, 4), pl.ds(3, 4)], sems.at[0]),
-        pltpu.make_async_copy(row_px, px_ref.at[pl.ds(1, 4), pl.ds(0, 3)], sems.at[1]),
-        pltpu.make_async_copy(time_px, px_ref.at[pl.ds(0, 1), pl.ds(3, 4)], sems.at[2]),
-        pltpu.make_async_copy(corner_px, px_ref.at[pl.ds(0, 1), pl.ds(0, 3)], sems.at[3]),
-    ]
-    head_copy = pltpu.make_async_copy(w_head_hbm, w_head_ref, sems.at[4])
-    out_copy = pltpu.make_async_copy(w_out_hbm, w_out_ref, sems.at[5])
-    qkv_copy = pltpu.make_async_copy(w_qkv_hbm, w_qkv_ref, sems.at[6])
+    pixel_copy = pltpu.make_async_copy(own_px, px_ref.at[pl.ds(1, 4), pl.ds(3, 4)], sems.at[0])
+    head_copy = pltpu.make_async_copy(w_head_hbm, w_head_ref, sems.at[1])
+    out_copy = pltpu.make_async_copy(w_out_hbm, w_out_ref, sems.at[2])
+    qkv_copy = pltpu.make_async_copy(w_qkv_hbm, w_qkv_ref, sems.at[3])
     head_copy.start()
-    for copy in pixel_copies:
-        copy.start()
+    pixel_copy.start()
     out_copy.start()
     qkv_copy.start()
+    px_ref[1:, :3] = row_px[...]
+    px_ref[:1, 3:] = time_px[...]
+    px_ref[:1, :3] = corner_px[...]
 
     def tokens_of(block):
         return pl.ds(pl.multiple_of(block * 16, 16), 16)
@@ -188,19 +188,21 @@
         narrow_ref[rows] = normed.astype(BF)
         return carry
 
-    lax.fori_loop(0, TOK // 16, head_norm, 0, unroll=2)
+    lax.fori_loop(0, TOK // 16, head_norm, 0, unroll=16)
     head_copy.wait()
-    for copy in pixel_copies:
-        copy.wait()
+    pixel_copy.wait()
     for part in range(3):
         cols = slice(part * GROUP, part * GROUP + GROUP)
-        predicted_ref[...] = dot(narrow_ref[...], w_head_ref[:, cols], NN_DIMS)
-
-        def pixel_block(block, carry, cols=cols):
-            at_frame = block // 2
-            half = block % 2
-            for group in range(2):
-                rows = tokens_of(((at_frame // 2) * 2 + group) * 4 + (at_frame % 2) * 2 + half)
+        predicted_ref[:, cols] = dot(narrow_ref[...], w_head_ref[:, cols], NN_DIMS)
+
+    def pixel_block(block, carry):
+        at_frame = block // 2
+        half = block % 2
+        for group in range(2):
+            rows = tokens_of(((at_frame // 2) * 2 + group) * 4 + (at_frame % 2) * 2 + half)
+            masked = 1.0 - jnp.concatenate([seen_ref[rows]] * 4, axis=1)
+            for part in range(3):
+                cols = slice(part * GROUP, part * GROUP + GROUP)
                 targets = []
                 for at in range(2):
                     raw = px_ref[
@@ -212,12 +214,11 @@
                     center = raw - lane_mean(raw)
                     spread = jnp.sqrt(jnp.sum(center * center, axis=-1, keepdims=True) * (1.0 / (GROUP - 1)))
                     targets.append(center * (1.0 / (spread + 1e-06)))
-                masked = 1.0 - jnp.concatenate([seen_ref[rows]] * 4, axis=1)
-                gap = predicted_ref[rows] - jnp.concatenate(targets, axis=0)
+                gap = predicted_ref[rows, cols] - jnp.concatenate(targets, axis=0)
                 error_ref[rows, cols] = (masked * gap).astype(BF)
-            return carry
-
-        lax.fori_loop(0, 8, pixel_block, 0)
+        return carry
+
+    lax.fori_loop(0, 8, pixel_block, 0, unroll=8)
 
     for part in range(2):
         cols = slice(part * 512, part * 512 + 512)
@@ -232,30 +233,36 @@
         narrow_ref[rows] = grad.astype(BF)
         return carry
 
-    lax.fori_loop(0, TOK // 16, head_norm_back, 0, unroll=2)
+    lax.fori_loop(0, TOK // 16, head_norm_back, 0, unroll=16)
     out_copy.wait()
     d_heads = dot(narrow_ref[...], w_out_ref[...], NT_DIMS).astype(BF)
     narrow_ref[...] = d_heads
 
-    def one_window(window, carry):
-        rows = pl.ds(pl.multiple_of(window * WIN, WIN), WIN)
-        for pair in range(PAIRS):
-            cols = [slice(at * D + pair * 128, at * D + pair * 128 + 128) for at in range(3)]
-            q_heads = two_heads(qkv_ref[rows, cols[0]])
-            k = qkv_ref[rows, cols[1]]
-            v = qkv_ref[rows, cols[2]]
-            out_heads = two_heads(narrow_ref[rows, cols[0]])
-            narrow_probs = probs_ref[window, pair]
-            probs = narrow_probs.astype(F32)
-            d_probs = dot(v, out_heads, NT_DIMS).astype(BF).astype(F32)
-            mean = jnp.sum(d_probs * probs, axis=0, keepdims=True)
-            d_scores = (probs * (d_probs - mean) * 0.125).astype(BF)
-            dqkv_ref[rows, cols[2]] = dot(narrow_probs, out_heads, NN_DIMS).astype(BF)
-            dqkv_ref[rows, cols[1]] = dot(d_scores, q_heads, NN_DIMS).astype(BF)
-            dqkv_ref[rows, cols[0]] = own_head(dot(d_scores, k, TN_DIMS)).astype(BF)
-        return carry
-
-    lax.fori_loop(0, TOK // WIN, one_window, 0)
+    def one_window(window):
+        rows = slice(window * WIN, window * WIN + WIN)
+        cols = [[slice(at * D + pair * 128, at * D + pair * 128 + 128) for at in range(3)] for pair in range(PAIRS)]
+        d_probs = []
+        out_heads = []
+        for pair in range(PAIRS):
+            out_heads.append(two_heads(narrow_ref[rows, cols[pair][0]]))
+            d_probs.append(dot(qkv_ref[rows, cols[pair][2]], out_heads[pair], NT_DIMS))
+        for pair in range(PAIRS):
+            dqkv_ref[rows, cols[pair][2]] = dot(probs_ref[window, pair], out_heads[pair], NN_DIMS).astype(BF)
+        d_scores = []
+        for pair in range(PAIRS):
+            probs = probs_ref[window, pair].astype(F32)
+            cotangent = d_probs[pair].astype(BF).astype(F32)
+            mean = jnp.sum(cotangent * probs, axis=0, keepdims=True)
+            d_scores.append((probs * (cotangent - mean) * 0.125).astype(BF))
+        for pair in range(PAIRS):
+            q_heads = two_heads(qkv_ref[rows, cols[pair][0]])
+            dqkv_ref[rows, cols[pair][1]] = dot(d_scores[pair], q_heads, NN_DIMS).astype(BF)
+        for pair in range(PAIRS):
+            d_q = own_head(dot(d_scores[pair], qkv_ref[rows, cols[pair][1]], TN_DIMS))
+            dqkv_ref[rows, cols[pair][0]] = d_q.astype(BF)
+
+    for window in range(TOK // WIN):
+        one_window(window)
     qkv_copy.wait()
     for part in range(2):
         cols = slice(part * 512, part * 512 + 512)
@@ -271,60 +278,15 @@
         part = masked * grad
         return carry + part[:8] + part[8:]
 
-    total_ref[...] = lax.fori_loop(0, TOK // 16, first_norm_back, jnp.zeros((8, D), F32), unroll=2)
+    total_ref[...] = lax.fori_loop(0, TOK // 16, first_norm_back, jnp.zeros((8, D), F32), unroll=16)
     picked_ref[...] = dot(one_hot_ref[...], narrow_ref[...], NN_DIMS).astype(BF)
 
 
-def sinusoid(coordinate, channel_count):
-    half_count = channel_count // 2
-    frequency = jnp.exp(-math.log(10000.0) * jnp.arange(half_count, dtype=F32) / half_count)
-    angles = coordinate.astype(F32)[..., None] * frequency
-    return jnp.concatenate([jnp.sin(angles), jnp.cos(angles)], axis=-1)
-
-
-def move(value, axis, steps):
-    count = lax.axis_size(axis)
-    return lax.ppermute(value, axis, [(at, (at + steps) % count) for at in range(count)])
-
-
-def move_corner(value):
-    count_tm = lax.axis_size(TM)
-    count_row = lax.axis_size(ROW)
-    pairs = [
-        (i * count_row + d, (i + 1) % count_tm * count_row + (d + 1) % count_row)
-        for i in range(count_tm)
-        for d in range(count_row)
-    ]
-    return lax.ppermute(value, ALL, pairs)
-
-
-def per_device(visible, slot_pos, window_shift, mask_token, w_qkv, w_out, w_head, pixels):
-    frame_count, row_count = pixels.shape[:2]
-    peers, slots = slot_pos.shape[2:]
-    rows = visible.reshape(peers, slots, D)
-    places = slot_pos.reshape(peers, slots).astype(BF)
-    packed = jnp.concatenate([rows, jnp.broadcast_to(places[..., None], (peers, slots, 128))], axis=-1)
-    packed = jnp.concatenate([packed, jnp.roll(packed, 1, axis=0)], axis=1)
-    own = lax.all_to_all(packed, ROW, split_axis=0, concat_axis=0, tiled=True).reshape(SLOTS, D + 128)
-    behind = move(own, TM, 1)
-
-    row_px = move(pixels[:, 1:], ROW, 1)
-    time_px = move(pixels[3:], TM, 1)
-    corner_px = move_corner(pixels[3:, 1:])
-
-    local = jnp.arange(4, dtype=jnp.int32)
-    frame_total = frame_count * lax.axis_size(TM)
-    row_total = row_count * lax.axis_size(ROW)
-    frames = (lax.axis_index(TM) * frame_count + local[None] - window_shift[0][:, None]) % frame_total
-    band = (lax.axis_index(ROW) * row_count + local[None] - window_shift[1][:, None]) % row_total
-    frame_table = sinusoid(frames.reshape(-1), 256)
-    row_table = sinusoid(band.reshape(-1), 384)
-    column_table = sinusoid(jnp.arange(16, dtype=jnp.int32), 384)
-
+def forward_part(*operands):
     vmem = pl.BlockSpec(memory_space=VMEM)
     smem = pl.BlockSpec(memory_space=SMEM)
-    hbm = pl.BlockSpec(memory_space=pl.ANY)
-    embedded, residual, qkv, probs, seen, one_hot = pl.pallas_call(
+    hbm = pl.BlockSpec(memory_space=pltpu.MemorySpace.HBM)
+    return pl.pallas_call(
         forward_kernel,
         name="forward_part",
         in_specs=[smem] + [vmem] * 6 + [hbm] * 2,
@@ -346,14 +308,17 @@
             pltpu.SemaphoreType.DMA((4,)),
         ],
         compiler_params=pltpu.CompilerParams(vmem_limit_bytes=28 << 20),
-    )(
-        window_shift, own, behind, mask_token.reshape(1, D), frame_table, row_table, column_table,
-        w_qkv, w_out,
-    )
-    picked, total = pl.pallas_call(
+    )(*operands)
+
+
+def backward_part(*operands):
+    vmem = pl.BlockSpec(memory_space=VMEM)
+    smem = pl.BlockSpec(memory_space=SMEM)
+    hbm = pl.BlockSpec(memory_space=pltpu.MemorySpace.HBM)
+    return pl.pallas_call(
         backward_kernel,
         name="backward_part",
-        in_specs=[smem] + [vmem] * 6 + [hbm] * 7,
+        in_specs=[smem] + [vmem] * 6 + [hbm] + [vmem] * 3 + [hbm] * 3,
         out_specs=[vmem] * 2,
         out_shape=[
             jax.ShapeDtypeStruct((2 * SLOTS, D), BF),
@@ -366,22 +331,80 @@
             pltpu.VMEM((D, 3 * D), BF),
             pltpu.VMEM((TOK, D), F32),
             pltpu.VMEM((TOK, 128), F32),
-            pltpu.VMEM((TOK, GROUP), F32),
+            pltpu.VMEM((TOK, PIX), F32),
             pltpu.VMEM((TOK, PIX), BF),
             pltpu.VMEM((TOK, D), BF),
             pltpu.VMEM((TOK, D), F32),
             pltpu.VMEM((TOK, D), F32),
             pltpu.VMEM((TOK, 3 * D), BF),
-            pltpu.SemaphoreType.DMA((7,)),
+            pltpu.SemaphoreType.DMA((4,)),
         ],
         compiler_params=pltpu.CompilerParams(vmem_limit_bytes=36 << 20),
-    )(
-        window_shift, embedded, residual, qkv, probs, seen, one_hot,
-        pixels, row_px, time_px, corner_px, w_head, w_out, w_qkv,
+    )(*operands)
+
+
+def sinusoid(coordinate, channel_count):
+    half_count = channel_count // 2
+    frequency = jnp.exp(-math.log(10000.0) * jnp.arange(half_count, dtype=F32) / half_count)
+    angles = coordinate.astype(F32)[..., None] * frequency
+    return jnp.concatenate([jnp.sin(angles), jnp.cos(angles)], axis=-1)
+
+
+def move(value, axis, steps):
+    count = lax.axis_size(axis)
+    return lax.ppermute(value, axis, [(at, (at + steps) % count) for at in range(count)])
+
+
+def move_corner(value):
+    count_tm = lax.axis_size(TM)
+    count_row = lax.axis_size(ROW)
+    pairs = [
+        (i * count_row + d, (i + 1) % count_tm * count_row + (d + 1) % count_row)
+        for i in range(count_tm)
+        for d in range(count_row)
+    ]
+    return lax.ppermute(value, ALL, pairs)
+
+
+def per_device(visible, slot_pos, window_shift, mask_token, w_qkv, w_out, w_head, pixels):
+    frame_count, row_count = pixels.shape[:2]
+    peers, slots = slot_pos.shape[2:]
+    rows = visible.reshape(peers, slots, D)
+    places = slot_pos.reshape(peers, slots).astype(BF)
+    packed = jnp.concatenate([rows, jnp.broadcast_to(places[..., None], (peers, slots, 128))], axis=-1)
+    packed = jnp.concatenate([packed, jnp.roll(packed, 1, axis=0)], axis=1)
+    own = lax.all_to_all(packed, ROW, split_axis=0, concat_axis=0, tiled=True).reshape(SLOTS, D + 128)
+    behind = move(own, TM, 1)
+
+    row_px = move(pixels[:, 1:], ROW, 1)
+    time_px = move(pixels[3:], TM, 1)
+    corner_px = move_corner(pixels[3:, 1:])
+
+    local = jnp.arange(4, dtype=jnp.int32)
+    frame_total = frame_count * lax.axis_size(TM)
+    row_total = row_count * lax.axis_size(ROW)
+    frames = (lax.axis_index(TM) * frame_count + local[None] - window_shift[0][:, None]) % frame_total
+    band = (lax.axis_index(ROW) * row_count + local[None] - window_shift[1][:, None]) % row_total
+    frame_table = sinusoid(frames.reshape(-1), 256)
+    row_table = sinusoid(band.reshape(-1), 384)
+    column_table = sinusoid(jnp.arange(16, dtype=jnp.int32), 384)
+
+    w_qkv, w_out, w_head, own_px = (
+        pltpu.with_memory_space_constraint(value, pltpu.MemorySpace.HBM)
+        for value in (w_qkv, w_out, w_head, pixels)
     )
-    mine = picked[:SLOTS] + move(picked[SLOTS:], TM, -1)
+    kept = forward_part(
+        window_shift, own, behind, mask_token.reshape(1, D), frame_table, row_table, column_table,
+        w_qkv, w_out,
+    )
+    picked, total = backward_part(
+        window_shift, *kept, own_px, row_px, time_px, corner_px, w_head, w_out, w_qkv
+    )
+    from_next = move(picked[SLOTS:], TM, -1)
+    mine = picked[:SLOTS] + from_next
     local_total = jnp.sum(total, axis=0).reshape(8, 128)
-    local_total = local_total + move(local_total, "tm_1", 1)
+    other = move(local_total, "tm_1", 1)
+    local_total = local_total + other
     turned = [move(local_total, "tm_0", step) for step in (1, 2, 3)]
     local_total = (local_total + turned[1]) + (turned[0] + turned[2])
     high = local_total.astype(BF)

time: 106 us -> 75 us (0.71)
  Pallas kernels: 37 us -> 16.9 us
  local copies, waits for them, and re-layouts: 14.2 us -> 4.87 us
  waiting for transfers between devices: 11.5 us -> 14.8 us
  blocking collectives: 18.1 us -> 15.3 us
  starting transfers between devices: 18 us -> 16.3 us
    pallas_call x2, Pallas kernels: 37 us -> 16.9 us  [the longest x1 9.9 us: backward_part(): pl.pallas_call(backward_kernel, name='backward_part', in_specs=[smem] + [...]
    unnamed x20 -> x2, local copies, waits for them, and re-layouts: 7.86 us -> 0.01 us
    all_to_all x1, blocking collectives: 18.1 us -> 15.3 us  [per_device(): back = lax.all_to_all(sent, ROW, split_axis=0, concat_axis=0, tiled=True)]
    ppermute x1, waiting for transfers between devices: 0.01 us -> 2.5 us  [move_corner(): return lax.ppermute(value, ALL, pairs)]
    ppermute x8, starting transfers between devices: 7.65 us -> 6.05 us  [move(): lax.ppermute(value, axis, [(at, (at + steps) % count) for at in range(cou...]
  transfers between devices with their start and end apart: 10 -> 10, of which waited for: 4 -> 7; matrix products, arithmetic and copies ran while one was open for 6% -> 7% of each run, Pallas kernels for 13% -> 9%
where the time goes in v2:
time: 75 us; the launch traced here: 73.6 us
  Pallas kernels  16.9 us (23%)
  starting transfers between devices  16.3 us (22%)
  blocking collectives  15.3 us (20%)
  waiting for transfers between devices  14.8 us (20%)
  local copies, waits for them, and re-layouts  4.87 us (6%)
  other arithmetic  4.64 us (6%)
  between operations  0.81 us (1%)
    all_to_all x1, blocking collectives, per_device(): back = lax.all_to_all(sent, ROW, split_axis=0, concat_axis=0, tiled=True)  15.3 us
    ppermute x8, waiting for transfers between devices, move(): lax.ppermute(value, axis, [(at, (at + steps) % count) for at in range(cou...  11.5 us
    pallas_call x1, Pallas kernels, backward_part(): pl.pallas_call(backward_kernel, name='backward_part', in_specs=[smem] + [...  9.9 us
    all_to_all x1, starting transfers between devices, per_device(): lax.all_to_all(packed, ROW, split_axis=0, concat_axis=0, tiled=True)  7.15 us
    pallas_call x1, Pallas kernels, forward_part(): pl.pallas_call(forward_kernel, name='forward_part', in_specs=[smem] + [vm...  6.99 us
    ppermute x8, starting transfers between devices, move(): lax.ppermute(value, axis, [(at, (at + steps) % count) for at in range(cou...  6.05 us
    ppermute x1, starting transfers between devices, move_corner(): return lax.ppermute(value, ALL, pairs)  3.15 us
    ppermute x1, waiting for transfers between devices, move_corner(): return lax.ppermute(value, ALL, pairs)  2.5 us
  transfers between devices with their start and end apart: 10, of which 7 were waited for; matrix products, arithmetic and copies ran while one was open for 7% of the time, Pallas kernels for 9%

profile of v2, /device:TPU:0, one launch (start us, length us, event | category | flops | bytes accessed | tf_op | source)
XLA Modules:
  0.0 73.6 jit_solution(7994772029618858238)
XLA Ops:
  0.6 0.7 convert_bitcast_fusion
  1.3 0.1 copy.10
  1.4 0.1 broadcast_in_dim.4
  1.5 1.8 %fusion.1 = bf16[16,8,1152]{2,1,0:T(8,128)(2,1)} fusion(bf16[16,4,128]{2,1,0:T(4,128)(2,1)S(1)} %broadcast_in_dim.4, bf16[16,4,1024]{2,1,0:T(4,128)(2,1)} %bitcast.20), kind=kLoop, calls=%fused_computation.3 | loop fusion | flops 1769472 | bytes 442368 | tf_op jit(solution)/shard_map/concatenate | solution.py:375
  3.4 7.1 %all-to-all-start = ((bf16[16,8,1152]{2,1,0:T(8,128)(2,1)}), bf16[16,8,1152]{2,1,0:T(8,128)(2,1)S(1)}, u32[]{:S(2)}, u32[]{:S(2)}) async-start(bf16[16,8,1152]{2,1,0:T(8,128)(2,1)} %fusion.1), calls=%async_computation | async-start | bytes 589824 | tf_op jit(solution)/shard_map/all_to_all | solution.py:376
  10.5 1.1 %slice.56 = bf16[4,3,16,1536]{3,2,1,0:T(8,128)(2,1)S(1)} slice(bf16[4,4,16,1536]{3,2,1,0:T(8,128)(2,1)} %own_px.1), slice={[0:4], [1:4], [0:16], [0:1536]} | slice | bytes 1179648 | tf_op jit(solution)/shard_map/slice | solution.py:379
  11.6 2.0 %collective-permute-start.1 = (bf16[4,3,16,1536]{3,2,1,0:T(8,128)(2,1)S(1)}, bf16[4,3,16,1536]{3,2,1,0:T(8,128)(2,1)S(1)}, u32[]{:S(2)}, u32[]{:S(2)}) collective-permute-start(bf16[4,3,16,1536]{3,2,1,0:T(8,128)(2,1)S(1)} %slice.56), channel_id=1, source_target_pairs={{0,1},{1,2},{2,3},{3,4},{4,5},{5,6},{6,7},{7,8},{8,9},{9,10},{10,1... | collective-permute-start | bytes 1769480 | tf_op jit(solution)/shard_map/ppermute | solution.py:355
  13.6 0.9 %slice.57 = bf16[1,4,16,1536]{3,2,1,0:T(8,128)(2,1)S(1)} slice(bf16[4,4,16,1536]{3,2,1,0:T(8,128)(2,1)} %own_px.1), slice={[3:4], [0:4], [0:16], [0:1536]} | slice | bytes 393216 | tf_op jit(solution)/shard_map/slice | solution.py:380
  14.6 0.9 %slice.58 = bf16[1,3,16,1536]{3,2,1,0:T(8,128)(2,1)S(1)} slice(bf16[4,4,16,1536]{3,2,1,0:T(8,128)(2,1)} %own_px.1), slice={[3:4], [1:4], [0:16], [0:1536]} | slice | bytes 294912 | tf_op jit(solution)/shard_map/slice | solution.py:381
  15.5 3.2 %collective-permute-start.3 = (bf16[1,3,16,1536]{3,2,1,0:T(8,128)(2,1)S(1)}, bf16[1,3,16,1536]{3,2,1,0:T(8,128)(2,1)S(1)}, u32[]{:S(2)}, u32[]{:S(2)}) collective-permute-start(bf16[1,3,16,1536]{3,2,1,0:T(8,128)(2,1)S(1)} %slice.58), channel_id=1, source_target_pairs={{0,17},{1,18},{2,19},{3,20},{4,21},{5,22},{6,23},{7,24},{8,25},{9,... | collective-permute-start | bytes 442376 | tf_op jit(solution)/shard_map/ppermute | solution.py:366
  18.7 0.8 %slice_bitcast_fusion = (s32[2]{0:T(128)S(1)}, s32[2]{0:T(128)S(1)}) fusion(s32[2,2]{1,0:T(2,128)} %shift_ref.3), kind=kLoop, calls=%fused_computation.37 | loop fusion | bytes 32 | tf_op jit(solution)/shard_map/sub | solution.py:387
  19.5 0.1 sub.58
  19.7 0.1 multiply_sine_fusion.1
  19.9 0.1 multiply_sine_fusion.2
  20.0 0.1 multiply_sine_fusion
  20.1 0.7 all-to-all-done
  20.9 0.7 reshape.111.mask_ref
  21.7 6.5 %collective-permute-done.behind_ref = bf16[128,1152]{1,0:T(8,128)(2,1)S(1)} collective-permute-done((bf16[128,1152]{1,0:T(8,128)(2,1)S(1)}, bf16[128,1152]{1,0:T(8,128)(2,1)S(1)}, u32[]{:S(2)}, u32[]{:S(2)}) %collective-permute-start) | collective-permute-done | bytes 294944 | tf_op jit(solution)/shard_map/ppermute | solution.py:355
  28.2 7.0 %forward_part.1 = (bf16[256,1024]{1,0:T(8,128)(2,1)S(1)}, f32[256,1024]{1,0:T(8,128)S(1)}, bf16[256,3072]{1,0:T(8,128)(2,1)S(1)}, bf16[4,8,64,128]{3,2,1,0:T(8,1...) custom-call(s32[2,2]{1,0:T(2,128)S(1)} %copy-done, bf16[128,1152]{1,0:T(8,128)(2,1)S(1)} %bitcast.19, ...), custom_call_target="tpu_custom_call" | custom-call | tf_op jit(solution)/shard_map/forward_part/pallas_call | solution.py:289
  35.2 2.5 %collective-permute-done.3.corner_px = bf16[1,3,16,1536]{3,2,1,0:T(8,128)(2,1)S(1)} collective-permute-done((bf16[1,3,16,1536]{3,2,1,0:T(8,128)(2,1)S(1)}, bf16[1,3,16,1536]{3,2,1,0:T(8,128)(2,1)S(1)}, u32[]{:S(2)}, u32[]{:S(2)}) %collective-permute-start.3) | collective-permute-done | bytes 147488 | tf_op jit(solution)/shard_map/ppermute | solution.py:366
  37.7 9.9 %backward_part.1 = (bf16[256,1024]{1,0:T(8,128)(2,1)S(1)}, f32[8,1024]{1,0:T(8,128)S(1)}) custom-call(s32[2,2]{1,0:T(2,128)S(1)} %copy-done, bf16[256,1024]{1,0:T(8,128)(2,1)S(1)} %get-tuple-element.10.embedded_ref, f32[256,1024]{1,0:T(8,128)S(1)} %get-tuple-element.11.residual_ref, bf16[256,3072]{1,0:T(8,128)(2,1)S(1)} %get-tuple-element.12.qkv_ref, ...), custom_call_target="tpu_custom_call" | custom-call | tf_op jit(solution)/shard_map/backward_part/pallas_call | solution.py:318
  47.6 0.1 collective-permute-start.5
  47.7 1.2 %collective-permute-done.5 = f32[8,128]{1,0:T(8,128)S(1)} collective-permute-done((f32[8,128]{1,0:T(8,128)S(1)}, f32[8,128]{1,0:T(8,128)S(1)}, u32[]{:S(2)}, u32[]{:S(2)}) %collective-permute-start.5) | collective-permute-done | bytes 4128 | tf_op jit(solution)/shard_map/ppermute | solution.py:355
  48.9 0.7 collective-permute-start.6
  49.6 1.0 %collective-permute-start.7 = (f32[8,128]{1,0:T(8,128)S(1)}, f32[8,128]{1,0:T(8,128)S(1)}, u32[]{:S(2)}, u32[]{:S(2)}) collective-permute-start(f32[8,128]{1,0:T(8,128)S(1)} %bitcast_add_fusion), channel_id=1, source_target_pairs={{0,32},{32,64},{64,96},{96,0},{1,33},{33,65},{65,97},{97,1},{2,34}... | collective-permute-start | bytes 12296 | tf_op jit(solution)/shard_map/ppermute | solution.py:355
  50.6 2.2 %collective-permute-start.8 = (f32[8,128]{1,0:T(8,128)S(1)}, f32[8,128]{1,0:T(8,128)S(1)}, u32[]{:S(2)}, u32[]{:S(2)}) collective-permute-start(f32[8,128]{1,0:T(8,128)S(1)} %bitcast_add_fusion), channel_id=1, source_target_pairs={{0,96},{32,0},{64,32},{96,64},{1,97},{33,1},{65,33},{97,65},{2,98}... | collective-permute-start | bytes 12296 | tf_op jit(solution)/shard_map/ppermute | solution.py:355
  52.9 1.1 %collective-permute-done.6 = f32[8,128]{1,0:T(8,128)S(1)} collective-permute-done((f32[8,128]{1,0:T(8,128)S(1)}, f32[8,128]{1,0:T(8,128)S(1)}, u32[]{:S(2)}, u32[]{:S(2)}) %collective-permute-start.6) | collective-permute-done | bytes 4128 | tf_op jit(solution)/shard_map/ppermute | solution.py:355
  54.0 0.4 collective-permute-done.7
  54.4 2.3 %collective-permute-done.4 = bf16[128,1024]{1,0:T(8,128)(2,1)S(1)} collective-permute-done((bf16[128,1024]{1,0:T(8,128)(2,1)S(1)}, bf16[128,1024]{1,0:T(8,128)(2,1)S(1)}, u32[]{:S(2)}, u32[]{:S(2)}) %collective-permute-start.4) | collective-permute-done | bytes 262176 | tf_op jit(solution)/shard_map/ppermute | solution.py:355
  56.8 15.3 %all_to_all.10 = bf16[16,8,1280]{2,1,0:T(8,128)(2,1)S(1)} all-to-all(bf16[16,8,1280]{2,1,0:T(8,128)(2,1)S(1)} %pad_maximum_fusion), channel_id=1, replica_groups=mesh['tm_0'=4,'tm_1'=2,'row_0'=4,'row_1'=4] {'row_0','row_1'}, dimensions={0} | all-to-all | bytes 655360 | tf_op jit(solution)/shard_map/all_to_all | solution.py:414
  72.2 0.6 fusion.4
  72.8 0.8 %fusion.2 = bf16[1,1,16,4,1024]{4,3,2,1,0:T(4,128)(2,1)} fusion(bf16[16,8,1280]{2,1,0:T(8,128)(2,1)S(1)} %all_to_all.10, bf16[1,4,1024]{2,1,0:T(4,128)(2,1)S(1)} %slice.69, bf16[15,4,1024]{2,1,0:T(4,128)(2,1)S(1)} %slice.68), kind=kLoop, calls=%fused_computation.7 | loop fusion | flops 131072 | bytes 393216 | tf_op jit(solution)/shard_map/reshape | solution.py:419
  (31 shorter events, 0.6 us)
Async XLA Ops:
  0.6 27.6 %copy-start = (s32[2,2]{1,0:T(2,128)S(1)}, s32[2,2]{1,0:T(2,128)}, u32[]{:S(2)}) copy-start(s32[2,2]{1,0:T(2,128)} %shift_ref.3) | copy-start | bytes 52
  3.4 17.5 %all-to-all-start = ((bf16[16,8,1152]{2,1,0:T(8,128)(2,1)}), bf16[16,8,1152]{2,1,0:T(8,128)(2,1)S(1)}, u32[]{:S(2)}, u32[]{:S(2)}) async-start(bf16[16,8,1152]{2,1,0:T(8,128)(2,1)} %fusion.1), calls=%async_computation | async-start | bytes 589824 | tf_op jit(solution)/shard_map/all_to_all | solution.py:376
  11.6 26.1 %collective-permute-start.1 = (bf16[4,3,16,1536]{3,2,1,0:T(8,128)(2,1)S(1)}, bf16[4,3,16,1536]{3,2,1,0:T(8,128)(2,1)S(1)}, u32[]{:S(2)}, u32[]{:S(2)}) collective-permute-start(bf16[4,3,16,1536]{3,2,1,0:T(8,128)(2,1)S(1)} %slice.56), channel_id=1, source_target_pairs={{0,1},{1,2},{2,3},{3,4},{4,5},{5,6},{6,7},{7,8},{8,9},{9,10},{10,1... | collective-permute-start | bytes 1769480 | tf_op jit(solution)/shard_map/ppermute | solution.py:355
  14.6 23.2 %collective-permute-start.2 = (bf16[1,4,16,1536]{3,2,1,0:T(8,128)(2,1)S(1)}, bf16[1,4,16,1536]{3,2,1,0:T(8,128)(2,1)S(1)}, u32[]{:S(2)}, u32[]{:S(2)}) collective-permute-start(bf16[1,4,16,1536]{3,2,1,0:T(8,128)(2,1)S(1)} %slice.57), channel_id=1, source_target_pairs={{0,16},{16,32},{32,48},{48,64},{64,80},{80,96},{96,112},{112,0},{1... | collective-permute-start | bytes 589832 | tf_op jit(solution)/shard_map/ppermute | solution.py:355
  15.5 22.2 %collective-permute-start.3 = (bf16[1,3,16,1536]{3,2,1,0:T(8,128)(2,1)S(1)}, bf16[1,3,16,1536]{3,2,1,0:T(8,128)(2,1)S(1)}, u32[]{:S(2)}, u32[]{:S(2)}) collective-permute-start(bf16[1,3,16,1536]{3,2,1,0:T(8,128)(2,1)S(1)} %slice.58), channel_id=1, source_target_pairs={{0,17},{1,18},{2,19},{3,20},{4,21},{5,22},{6,23},{7,24},{8,25},{9,... | collective-permute-start | bytes 442376 | tf_op jit(solution)/shard_map/ppermute | solution.py:366
  20.8 7.4 %collective-permute-start = (bf16[128,1152]{1,0:T(8,128)(2,1)S(1)}, bf16[128,1152]{1,0:T(8,128)(2,1)S(1)}, u32[]{:S(2)}, u32[]{:S(2)}) collective-permute-start(bf16[128,1152]{1,0:T(8,128)(2,1)S(1)} %bitcast.18), channel_id=1, source_target_pairs={{0,16},{16,32},{32,48},{48,64},{64,80},{80,96},{96,112},{112,0},{1... | collective-permute-start | bytes 884744 | tf_op jit(solution)/shard_map/ppermute | solution.py:355
  47.6 1.2 %collective-permute-start.5 = (f32[8,128]{1,0:T(8,128)S(1)}, f32[8,128]{1,0:T(8,128)S(1)}, u32[]{:S(2)}, u32[]{:S(2)}) collective-permute-start(f32[8,128]{1,0:T(8,128)S(1)} %bitcast.21), channel_id=1, source_target_pairs={{0,16},{16,0},{1,17},{17,1},{2,18},{18,2},{3,19},{19,3},{4,20},{20... | collective-permute-start | bytes 12296 | tf_op jit(solution)/shard_map/ppermute | solution.py:355
  48.9 5.1 %collective-permute-start.6 = (f32[8,128]{1,0:T(8,128)S(1)}, f32[8,128]{1,0:T(8,128)S(1)}, u32[]{:S(2)}, u32[]{:S(2)}) collective-permute-start(f32[8,128]{1,0:T(8,128)S(1)} %bitcast_add_fusion), channel_id=1, source_target_pairs={{0,64},{32,96},{64,0},{96,32},{1,65},{33,97},{65,1},{97,33},{2,66}... | collective-permute-start | bytes 12296 | tf_op jit(solution)/shard_map/ppermute | solution.py:355
  49.6 4.8 %collective-permute-start.7 = (f32[8,128]{1,0:T(8,128)S(1)}, f32[8,128]{1,0:T(8,128)S(1)}, u32[]{:S(2)}, u32[]{:S(2)}) collective-permute-start(f32[8,128]{1,0:T(8,128)S(1)} %bitcast_add_fusion), channel_id=1, source_target_pairs={{0,32},{32,64},{64,96},{96,0},{1,33},{33,65},{65,97},{97,1},{2,34}... | collective-permute-start | bytes 12296 | tf_op jit(solution)/shard_map/ppermute | solution.py:355
  50.6 3.8 %collective-permute-start.8 = (f32[8,128]{1,0:T(8,128)S(1)}, f32[8,128]{1,0:T(8,128)S(1)}, u32[]{:S(2)}, u32[]{:S(2)}) collective-permute-start(f32[8,128]{1,0:T(8,128)S(1)} %bitcast_add_fusion), channel_id=1, source_target_pairs={{0,96},{32,0},{64,32},{96,64},{1,97},{33,1},{65,33},{97,65},{2,98}... | collective-permute-start | bytes 12296 | tf_op jit(solution)/shard_map/ppermute | solution.py:355
  52.8 3.9 %collective-permute-start.4 = (bf16[128,1024]{1,0:T(8,128)(2,1)S(1)}, bf16[128,1024]{1,0:T(8,128)(2,1)S(1)}, u32[]{:S(2)}, u32[]{:S(2)}) collective-permute-start(bf16[128,1024]{1,0:T(8,128)(2,1)S(1)} %slice.60), channel_id=1, source_target_pairs={{0,112},{16,0},{32,16},{48,32},{64,48},{80,64},{96,80},{112,96},{1... | collective-permute-start | bytes 786440 | tf_op jit(solution)/shard_map/ppermute | solution.py:355

commit v3 on v2

--- a/solution.py
+++ b/solution.py
@@ -1,3 +1,4 @@
+import functools
 import math
 
 import jax
@@ -160,22 +161,21 @@
 
 def backward_kernel(
     shift_ref, embedded_ref, residual_ref, qkv_ref, probs_ref, seen_ref, one_hot_ref,
-    own_px, row_px, time_px, corner_px, w_head_hbm, w_out_hbm, w_qkv_hbm,
-    picked_ref, total_ref,
-    px_ref, w_head_ref, w_out_ref, w_qkv_ref, normed_ref, scale_ref, predicted_ref, error_ref,
+    own_target, row_target, time_target, corner_target, w_head_hbm, w_out_hbm, w_qkv_hbm,
+    own_picked_ref, behind_picked_ref, total_ref,
+    target_ref, w_head_ref, w_out_ref, w_qkv_ref, normed_ref, scale_ref, predicted_ref, error_ref,
     narrow_ref, wide_ref, stream_ref, dqkv_ref, sems,
 ):
-    pixel_copy = pltpu.make_async_copy(own_px, px_ref.at[pl.ds(1, 4), pl.ds(3, 4)], sems.at[0])
-    head_copy = pltpu.make_async_copy(w_head_hbm, w_head_ref, sems.at[1])
-    out_copy = pltpu.make_async_copy(w_out_hbm, w_out_ref, sems.at[2])
-    qkv_copy = pltpu.make_async_copy(w_qkv_hbm, w_qkv_ref, sems.at[3])
+    head_copy = pltpu.make_async_copy(w_head_hbm, w_head_ref, sems.at[0])
+    out_copy = pltpu.make_async_copy(w_out_hbm, w_out_ref, sems.at[1])
+    qkv_copy = pltpu.make_async_copy(w_qkv_hbm, w_qkv_ref, sems.at[2])
     head_copy.start()
-    pixel_copy.start()
     out_copy.start()
     qkv_copy.start()
-    px_ref[1:, :3] = row_px[...]
-    px_ref[:1, 3:] = time_px[...]
-    px_ref[:1, :3] = corner_px[...]
+    target_ref[1:, 3:] = own_target[...]
+    target_ref[1:, :3] = row_target[...]
+    target_ref[:1, 3:] = time_target[...]
+    target_ref[:1, :3] = corner_target[...]
 
     def tokens_of(block):
         return pl.ds(pl.multiple_of(block * 16, 16), 16)
@@ -190,7 +190,6 @@
 
     lax.fori_loop(0, TOK // 16, head_norm, 0, unroll=16)
     head_copy.wait()
-    pixel_copy.wait()
     for part in range(3):
         cols = slice(part * GROUP, part * GROUP + GROUP)
         predicted_ref[:, cols] = dot(narrow_ref[...], w_head_ref[:, cols], NN_DIMS)
@@ -200,22 +199,19 @@
         half = block % 2
         for group in range(2):
             rows = tokens_of(((at_frame // 2) * 2 + group) * 4 + (at_frame % 2) * 2 + half)
-            masked = 1.0 - jnp.concatenate([seen_ref[rows]] * 4, axis=1)
-            for part in range(3):
-                cols = slice(part * GROUP, part * GROUP + GROUP)
-                targets = []
-                for at in range(2):
-                    raw = px_ref[
+            masked = 1.0 - jnp.concatenate([seen_ref[rows]] * 12, axis=1)
+            target = jnp.concatenate(
+                [
+                    target_ref[
                         at_frame - shift_ref[0, group] + 1,
                         half * 2 + at - shift_ref[1, group] + 3,
                         group * 8 : group * 8 + 8,
-                        cols,
                     ].astype(F32)
-                    center = raw - lane_mean(raw)
-                    spread = jnp.sqrt(jnp.sum(center * center, axis=-1, keepdims=True) * (1.0 / (GROUP - 1)))
-                    targets.append(center * (1.0 / (spread + 1e-06)))
-                gap = predicted_ref[rows, cols] - jnp.concatenate(targets, axis=0)
-                error_ref[rows, cols] = (masked * gap).astype(BF)
+                    for at in range(2)
+                ],
+                axis=0,
+            )
+            error_ref[rows] = (masked * (predicted_ref[rows] - target)).astype(BF)
         return carry
 
     lax.fori_loop(0, 8, pixel_block, 0, unroll=8)
@@ -278,8 +274,52 @@
         part = masked * grad
         return carry + part[:8] + part[8:]
 
-    total_ref[...] = lax.fori_loop(0, TOK // 16, first_norm_back, jnp.zeros((8, D), F32), unroll=16)
-    picked_ref[...] = dot(one_hot_ref[...], narrow_ref[...], NN_DIMS).astype(BF)
+    total = lax.fori_loop(0, TOK // 16, first_norm_back, jnp.zeros((8, D), F32), unroll=16)
+    total = jnp.sum(total, axis=0, keepdims=True)
+    total_ref[...] = jnp.concatenate([total[:, at * 128 : at * 128 + 128] for at in range(8)], axis=0)
+    own_picked_ref[...] = dot(one_hot_ref[:SLOTS], narrow_ref[...], NN_DIMS).astype(BF)
+    behind_picked_ref[...] = dot(one_hot_ref[SLOTS:], narrow_ref[...], NN_DIMS).astype(BF)
+
+
+def pack_kernel(place_ref, rows_ref, packed_ref):
+    rows = rows_ref[...].astype(F32)
+    before = jnp.concatenate([rows[-1:], rows[:-1]], axis=0)
+    packed_ref[:, :, :D] = jnp.concatenate([rows, before], axis=1).astype(BF)
+    slot = lax.broadcasted_iota(jnp.int32, (8, 128), 0)
+    peers = rows_ref.shape[0]
+    for peer in range(peers):
+        places = jnp.zeros((8, 128), jnp.int32)
+        for at in range(8):
+            source = peer if at < 4 else (peer - 1) % peers
+            places = jnp.where(slot == at, place_ref[source, at % 4], places)
+        packed_ref[peer, :, D:] = places.astype(F32).astype(BF)
+
+
+def target_kernel(pixel_ref, own_ref, row_ref, time_ref, corner_ref):
+    for frame in range(4):
+        for row in range(4):
+            for part in range(3):
+                cols = slice(part * GROUP, part * GROUP + GROUP)
+                raw = pixel_ref[frame, row, :, cols].astype(F32)
+                center = raw - lane_mean(raw)
+                spread = jnp.sqrt(jnp.sum(center * center, axis=-1, keepdims=True) * (1.0 / (GROUP - 1)))
+                target = (center * (1.0 / (spread + 1e-06))).astype(BF)
+                own_ref[frame, row, :, cols] = target
+                if row > 0:
+                    row_ref[frame, row - 1, :, cols] = target
+                if frame == 3:
+                    time_ref[0, row, :, cols] = target
+                if frame == 3 and row > 0:
+                    corner_ref[0, row - 1, :, cols] = target
+
+
+def unpack_kernel(scale, back_ref, rows_ref, total_ref):
+    rows = back_ref[:, :4, :D].astype(F32)
+    after = back_ref[:, 4:, :D].astype(F32)
+    after = jnp.concatenate([after[1:], after[:1]], axis=0)
+    rows_ref[...] = (rows + after).astype(BF)
+    sums = jnp.sum(back_ref[:, :, D:].astype(F32), axis=0)
+    total_ref[...] = (sums[:, :128] + sums[:, 128:]) * scale
 
 
 def forward_part(*operands):
@@ -318,11 +358,12 @@
     return pl.pallas_call(
         backward_kernel,
         name="backward_part",
-        in_specs=[smem] + [vmem] * 6 + [hbm] + [vmem] * 3 + [hbm] * 3,
-        out_specs=[vmem] * 2,
+        in_specs=[smem] + [vmem] * 10 + [hbm] * 3,
+        out_specs=[vmem] * 3,
         out_shape=[
-            jax.ShapeDtypeStruct((2 * SLOTS, D), BF),
-            jax.ShapeDtypeStruct((8, D), F32),
+            jax.ShapeDtypeStruct((SLOTS, D), BF),
+            jax.ShapeDtypeStruct((SLOTS, D), BF),
+            jax.ShapeDtypeStruct((8, 128), F32),
         ],
         scratch_shapes=[
             pltpu.VMEM((5, 7, 16, PIX), BF),
@@ -337,7 +378,7 @@
             pltpu.VMEM((TOK, D), F32),
             pltpu.VMEM((TOK, D), F32),
             pltpu.VMEM((TOK, 3 * D), BF),
-            pltpu.SemaphoreType.DMA((4,)),
+            pltpu.SemaphoreType.DMA((3,)),
         ],
         compiler_params=pltpu.CompilerParams(vmem_limit_bytes=36 << 20),
     )(*operands)
@@ -369,16 +410,32 @@
 def per_device(visible, slot_pos, window_shift, mask_token, w_qkv, w_out, w_head, pixels):
     frame_count, row_count = pixels.shape[:2]
     peers, slots = slot_pos.shape[2:]
-    rows = visible.reshape(peers, slots, D)
-    places = slot_pos.reshape(peers, slots).astype(BF)
-    packed = jnp.concatenate([rows, jnp.broadcast_to(places[..., None], (peers, slots, 128))], axis=-1)
-    packed = jnp.concatenate([packed, jnp.roll(packed, 1, axis=0)], axis=1)
+    vmem = pl.BlockSpec(memory_space=VMEM)
+    smem = pl.BlockSpec(memory_space=SMEM)
+    packed = pl.pallas_call(
+        pack_kernel,
+        name="pack_part",
+        in_specs=[smem, vmem],
+        out_specs=vmem,
+        out_shape=jax.ShapeDtypeStruct((peers, 2 * slots, D + 128), BF),
+        compiler_params=pltpu.CompilerParams(vmem_limit_bytes=8 << 20),
+    )(slot_pos.reshape(peers, slots), visible.reshape(peers, slots, D))
     own = lax.all_to_all(packed, ROW, split_axis=0, concat_axis=0, tiled=True).reshape(SLOTS, D + 128)
     behind = move(own, TM, 1)
-
-    row_px = move(pixels[:, 1:], ROW, 1)
-    time_px = move(pixels[3:], TM, 1)
-    corner_px = move_corner(pixels[3:, 1:])
+    own_target, row_target, time_target, corner_target = pl.pallas_call(
+        target_kernel,
+        name="target_part",
+        in_specs=[vmem],
+        out_specs=[vmem] * 4,
+        out_shape=[
+            jax.ShapeDtypeStruct((frames, rows, 16, PIX), BF)
+            for frames, rows in ((4, 4), (4, 3), (1, 4), (1, 3))
+        ],
+        compiler_params=pltpu.CompilerParams(vmem_limit_bytes=8 << 20),
+    )(pixels)
+    row_target = move(row_target, ROW, 1)
+    corner_target = move_corner(corner_target)
+    time_target = move(time_target, TM, 1)
 
     local = jnp.arange(4, dtype=jnp.int32)
     frame_total = frame_count * lax.axis_size(TM)
@@ -389,20 +446,18 @@
     row_table = sinusoid(band.reshape(-1), 384)
     column_table = sinusoid(jnp.arange(16, dtype=jnp.int32), 384)
 
-    w_qkv, w_out, w_head, own_px = (
-        pltpu.with_memory_space_constraint(value, pltpu.MemorySpace.HBM)
-        for value in (w_qkv, w_out, w_head, pixels)
+    w_qkv, w_out, w_head = (
+        pltpu.with_memory_space_constraint(value, pltpu.MemorySpace.HBM) for value in (w_qkv, w_out, w_head)
     )
     kept = forward_part(
         window_shift, own, behind, mask_token.reshape(1, D), frame_table, row_table, column_table,
         w_qkv, w_out,
     )
-    picked, total = backward_part(
-        window_shift, *kept, own_px, row_px, time_px, corner_px, w_head, w_out, w_qkv
+    own_picked, behind_picked, local_total = backward_part(
+        window_shift, *kept, own_target, row_target, time_target, corner_target, w_head, w_out, w_qkv
     )
-    from_next = move(picked[SLOTS:], TM, -1)
-    mine = picked[:SLOTS] + from_next
-    local_total = jnp.sum(total, axis=0).reshape(8, 128)
+    from_next = move(behind_picked, TM, -1)
+    mine = own_picked + from_next
     other = move(local_total, "tm_1", 1)
     local_total = local_total + other
     turned = [move(local_total, "tm_0", step) for step in (1, 2, 3)]
@@ -412,11 +467,16 @@
     sums = jnp.broadcast_to(jnp.concatenate([high, low], axis=1)[None], (peers, 8, 256))
     sent = jnp.concatenate([mine.reshape(peers, 2 * slots, D), sums], axis=-1)
     back = lax.all_to_all(sent, ROW, split_axis=0, concat_axis=0, tiled=True)
-    d_visible = back[:, :slots, :D] + jnp.roll(back[:, slots:, :D], -1, axis=0)
-    halves = jnp.sum(back[:, :, D:].astype(F32), axis=0)
     grad_scale = (frame_total * row_total * pixels.shape[2]) ** (-0.5)
-    d_mask = (halves[:, :128] + halves[:, 128:]).reshape(D) * grad_scale
-    return (d_visible.reshape(visible.shape), d_mask)
+    d_visible, d_mask = pl.pallas_call(
+        functools.partial(unpack_kernel, grad_scale),
+        name="unpack_part",
+        in_specs=[vmem],
+        out_specs=[vmem] * 2,
+        out_shape=[jax.ShapeDtypeStruct((peers, slots, D), BF), jax.ShapeDtypeStruct((8, 128), F32)],
+        compiler_params=pltpu.CompilerParams(vmem_limit_bytes=8 << 20),
+    )(back)
+    return (d_visible.reshape(visible.shape), d_mask.reshape(D))
 
 
 def solution(mesh):

time: 75 us -> 73.8 us (0.984)
  other arithmetic: 4.64 us -> 0.72 us
  Pallas kernels: 16.9 us -> 19.6 us
  waiting for transfers between devices: 14.8 us -> 15.6 us
    slice x6 -> x0, local copies, waits for them, and re-layouts: 3.07 us -> none  [the longest x1 1.11 us: per_device(): row_px = move(pixels[:, 1:], ROW, 1)]
    pallas_call x0 -> x3, Pallas kernels: none -> 2.98 us  [the longest x1 1.46 us: per_device(): pl.pallas_call(pack_kernel, name='pack_part', in_specs=[smem, vmem], out_...]
    unnamed x2 -> x8, local copies, waits for them, and re-layouts: 0.01 us -> 2.71 us
    concatenate x1 -> x0, other arithmetic: 1.83 us -> none  [per_device(): packed = jnp.concatenate([packed, jnp.roll(packed, 1, axis=0)], axis=1)]
    reshape x0 -> x1, local copies, waits for them, and re-layouts: none -> 0.76 us  [per_device(): slot_pos.reshape(peers, slots)]
    reshape x1 -> x0, other arithmetic: 0.76 us -> none  [per_device(): return (d_visible.reshape(visible.shape), d_mask)]
  transfers between devices with their start and end apart: 10 -> 10, of which waited for: 7 -> 7; matrix products, arithmetic and copies ran while one was open for 7% -> 3% of each run, Pallas kernels for 9% -> 11%
where the time goes in v3:
time: 73.8 us; the launch traced here: 72.5 us
  Pallas kernels  19.6 us (27%)
  starting transfers between devices  16 us (22%)
  waiting for transfers between devices  15.6 us (21%)
  blocking collectives  14.8 us (20%)
  local copies, waits for them, and re-layouts  5.09 us (7%)
  between operations  0.77 us (1%)
    all_to_all x1, blocking collectives, per_device(): back = lax.all_to_all(sent, ROW, split_axis=0, concat_axis=0, tiled=True)  14.8 us
    ppermute x8, waiting for transfers between devices, move(): lax.ppermute(value, axis, [(at, (at + steps) % count) for at in range(cou...  11.6 us
    pallas_call x1, Pallas kernels, backward_part(): pl.pallas_call(backward_kernel, name='backward_part', in_specs=[smem] + [...  9.62 us
    all_to_all x1, starting transfers between devices, per_device(): lax.all_to_all(packed, ROW, split_axis=0, concat_axis=0, tiled=True)  7.15 us
    pallas_call x1, Pallas kernels, forward_part(): pl.pallas_call(forward_kernel, name='forward_part', in_specs=[smem] + [vm...  6.99 us
    ppermute x8, starting transfers between devices, move(): lax.ppermute(value, axis, [(at, (at + steps) % count) for at in range(cou...  5.74 us
    ppermute x1, starting transfers between devices, move_corner(): return lax.ppermute(value, ALL, pairs)  3.1 us
    ppermute x1, waiting for transfers between devices, move_corner(): return lax.ppermute(value, ALL, pairs)  2.94 us
  transfers between devices with their start and end apart: 10, of which 7 were waited for; matrix products, arithmetic and copies ran while one was open for 3% of the time, Pallas kernels for 11%

profile of v3, /device:TPU:0, one launch (start us, length us, event | category | flops | bytes accessed | tf_op | source)
XLA Modules:
  0.0 72.5 jit_solution(17433895125668502519)
XLA Ops:
  0.6 0.8 %copy.10.place_ref = s32[16,4]{1,0:T(8,128)S(1)} copy(s32[16,4]{0,1:T(4,128)} %bitcast.14) | data formatting | bytes 512 | tf_op jit(solution)/shard_map/reshape | solution.py:422
  1.4 0.9 %copy-done.1 = bf16[1,1,16,4,1024]{4,3,2,1,0:T(4,128)(2,1)S(1)} copy-done((bf16[1,1,16,4,1024]{4,3,2,1,0:T(4,128)(2,1)S(1)}, bf16[1,1,16,4,1024]{4,3,2,1,0:T(4,128)(2,1)}, u32[]{:S(2)}) %copy-start.1) | copy-done | bytes 131096
  2.3 1.5 %pack_part.1 = bf16[16,8,1152]{2,1,0:T(8,128)(2,1)} custom-call(s32[16,4]{1,0:T(8,128)S(1)} %copy.10.place_ref, bf16[16,4,1024]{2,1,0:T(4,128)(2,1)S(1)} %bitcast.13), custom_call_target="tpu_custom_call" | custom-call | tf_op jit(solution)/shard_map/pack_part/pallas_call | solution.py:415
  3.8 7.1 %all-to-all-start = ((bf16[16,8,1152]{2,1,0:T(8,128)(2,1)}), bf16[16,8,1152]{2,1,0:T(8,128)(2,1)S(1)}, u32[]{:S(2)}, u32[]{:S(2)}) async-start(bf16[16,8,1152]{2,1,0:T(8,128)(2,1)} %pack_part.1), calls=%async_computation | async-start | bytes 589824 | tf_op jit(solution)/shard_map/all_to_all | solution.py:423
  10.9 1.1 %copy-done = bf16[4,4,16,1536]{3,2,1,0:T(8,128)(2,1)S(1)} copy-done((bf16[4,4,16,1536]{3,2,1,0:T(8,128)(2,1)S(1)}, bf16[4,4,16,1536]{3,2,1,0:T(8,128)(2,1)}, u32[]{:S(2)}) %copy-start) | copy-done | bytes 786456
  12.0 0.8 %target_part.1 = (bf16[4,4,16,1536]{3,2,1,0:T(8,128)(2,1)S(1)}, bf16[4,3,16,1536]{3,2,1,0:T(8,128)(2,1)S(1)}, bf16[1,4,16,1536]{3,2,1,0:T(8,128)(2,1)S(1)}, bf16[1,3,16,1536]{3,2,1,0:T(8,128)(2,1)S(1)}) custom-call(bf16[4,4,16,1536]{3,2,1,0:T(8,128)(2,1)S(1)} %copy-done), custom_call_target="tpu_custom_call" | custom-call | tf_op jit(solution)/shard_map/target_part/pallas_call | solution.py:425
  12.8 2.0 %collective-permute-start.1 = (bf16[4,3,16,1536]{3,2,1,0:T(8,128)(2,1)S(1)}, bf16[4,3,16,1536]{3,2,1,0:T(8,128)(2,1)S(1)}, u32[]{:S(2)}, u32[]{:S(2)}) collective-permute-start(bf16[4,3,16,1536]{3,2,1,0:T(8,128)(2,1)S(1)} %get-tuple-element.24), channel_id=1, source_target_pairs={{0,1},{1,2},{2,3},{3,4},{4,5},{5,6},{6,7},{7,8},{8,9},{9,10},{10,1... | collective-permute-start | bytes 1769480 | tf_op jit(solution)/shard_map/ppermute | solution.py:396
  14.8 3.1 %collective-permute-start.3 = (bf16[1,3,16,1536]{3,2,1,0:T(8,128)(2,1)S(1)}, bf16[1,3,16,1536]{3,2,1,0:T(8,128)(2,1)S(1)}, u32[]{:S(2)}, u32[]{:S(2)}) collective-permute-start(bf16[1,3,16,1536]{3,2,1,0:T(8,128)(2,1)S(1)} %get-tuple-element.26), channel_id=1, source_target_pairs={{0,17},{1,18},{2,19},{3,20},{4,21},{5,22},{6,23},{7,24},{8,25},{9,... | collective-permute-start | bytes 442376 | tf_op jit(solution)/shard_map/ppermute | solution.py:407
  18.0 0.8 %slice_bitcast_fusion = (s32[2]{0:T(128)S(1)}, s32[2]{0:T(128)S(1)}) fusion(s32[2,2]{1,0:T(2,128)} %shift_ref.3), kind=kLoop, calls=%fused_computation.26 | loop fusion | bytes 32 | tf_op jit(solution)/shard_map/sub | solution.py:444
  18.7 0.1 broadcast_subtract_fusion
  18.8 0.1 sub.58
  18.9 0.1 sub.53
  19.0 0.1 multiply_sine_fusion.1
  19.1 0.1 multiply_sine_fusion.2
  19.2 0.1 multiply_sine_fusion
  19.4 1.1 %all-to-all-done = bf16[16,8,1152]{2,1,0:T(8,128)(2,1)S(1)} async-done(((bf16[16,8,1152]{2,1,0:T(8,128)(2,1)}), bf16[16,8,1152]{2,1,0:T(8,128)(2,1)S(1)}, u32[]{:S(2)}, u32[]{:S(2)}) %all-to-all-start) | async-done | bytes 294944 | tf_op jit(solution)/shard_map/all_to_all | solution.py:423
  20.5 0.7 reshape.105.mask_ref
  21.3 6.5 %collective-permute-done.behind_ref = bf16[128,1152]{1,0:T(8,128)(2,1)S(1)} collective-permute-done((bf16[128,1152]{1,0:T(8,128)(2,1)S(1)}, bf16[128,1152]{1,0:T(8,128)(2,1)S(1)}, u32[]{:S(2)}, u32[]{:S(2)}) %collective-permute-start) | collective-permute-done | bytes 294944 | tf_op jit(solution)/shard_map/ppermute | solution.py:396
  27.8 0.7 copy-done.2
  28.5 7.0 %forward_part.1 = (bf16[256,1024]{1,0:T(8,128)(2,1)S(1)}, f32[256,1024]{1,0:T(8,128)S(1)}, bf16[256,3072]{1,0:T(8,128)(2,1)S(1)}, bf16[4,8,64,128]{3,2,1,0:T(8,1...) custom-call(s32[2,2]{1,0:T(2,128)S(1)} %copy-done.2, bf16[128,1152]{1,0:T(8,128)(2,1)S(1)} %bitcast.12, ...), custom_call_target="tpu_custom_call" | custom-call | tf_op jit(solution)/shard_map/forward_part/pallas_call | solution.py:329
  35.5 2.9 %collective-permute-done.3.corner_target = bf16[1,3,16,1536]{3,2,1,0:T(8,128)(2,1)S(1)} collective-permute-done((bf16[1,3,16,1536]{3,2,1,0:T(8,128)(2,1)S(1)}, bf16[1,3,16,1536]{3,2,1,0:T(8,128)(2,1)S(1)}, u32[]{:S(2)}, u32[]{:S(2)}) %collective-permute-start.3) | collective-permute-done | bytes 147488 | tf_op jit(solution)/shard_map/ppermute | solution.py:407
  38.4 9.6 %backward_part.1 = (bf16[128,1024]{1,0:T(8,128)(2,1)S(1)}, bf16[128,1024]{1,0:T(8,128)(2,1)S(1)}, f32[8,128]{1,0:T(8,128)S(1)}) custom-call(s32[2,2]{1,0:T(2,128)S(1)} %copy-done.3, bf16[256,1024]{1,0:T(8,128)(2,1)S(1)} %get-tuple-element.17.embedded_ref, f32[256,1024]{1,0:T(8,128)S(1)} %get-tuple-element.18.residual_ref, ...), custom_call_target="tpu_custom_call" | custom-call | tf_op jit(solution)/shard_map/backward_part/pallas_call | solution.py:358
  48.1 0.1 collective-permute-start.5
  48.2 1.2 %collective-permute-done.5 = f32[8,128]{1,0:T(8,128)S(1)} collective-permute-done((f32[8,128]{1,0:T(8,128)S(1)}, f32[8,128]{1,0:T(8,128)S(1)}, u32[]{:S(2)}, u32[]{:S(2)}) %collective-permute-start.5) | collective-permute-done | bytes 4128 | tf_op jit(solution)/shard_map/ppermute | solution.py:396
  49.3 0.4 collective-permute-start.6
  49.7 1.0 %collective-permute-start.7 = (f32[8,128]{1,0:T(8,128)S(1)}, f32[8,128]{1,0:T(8,128)S(1)}, u32[]{:S(2)}, u32[]{:S(2)}) collective-permute-start(f32[8,128]{1,0:T(8,128)S(1)} %add.72), channel_id=1, source_target_pairs={{0,32},{32,64},{64,96},{96,0},{1,33},{33,65},{65,97},{97,1},{2,34}... | collective-permute-start | bytes 12296 | tf_op jit(solution)/shard_map/ppermute | solution.py:396
  50.7 2.2 %collective-permute-start.8 = (f32[8,128]{1,0:T(8,128)S(1)}, f32[8,128]{1,0:T(8,128)S(1)}, u32[]{:S(2)}, u32[]{:S(2)}) collective-permute-start(f32[8,128]{1,0:T(8,128)S(1)} %add.72), channel_id=1, source_target_pairs={{0,96},{32,0},{64,32},{96,64},{1,97},{33,1},{65,33},{97,65},{2,98}... | collective-permute-start | bytes 12296 | tf_op jit(solution)/shard_map/ppermute | solution.py:396
  53.0 1.5 %collective-permute-done.6 = f32[8,128]{1,0:T(8,128)S(1)} collective-permute-done((f32[8,128]{1,0:T(8,128)S(1)}, f32[8,128]{1,0:T(8,128)S(1)}, u32[]{:S(2)}, u32[]{:S(2)}) %collective-permute-start.6) | collective-permute-done | bytes 4128 | tf_op jit(solution)/shard_map/ppermute | solution.py:396
  54.4 0.1 collective-permute-done.7
  54.6 2.3 %collective-permute-done.4 = bf16[128,1024]{1,0:T(8,128)(2,1)S(1)} collective-permute-done((bf16[128,1024]{1,0:T(8,128)(2,1)S(1)}, bf16[128,1024]{1,0:T(8,128)(2,1)S(1)}, u32[]{:S(2)}, u32[]{:S(2)}) %collective-permute-start.4) | collective-permute-done | bytes 262176 | tf_op jit(solution)/shard_map/ppermute | solution.py:396
  57.0 14.8 %all_to_all.10.back_ref = bf16[16,8,1280]{2,1,0:T(8,128)(2,1)S(1)} all-to-all(bf16[16,8,1280]{2,1,0:T(8,128)(2,1)S(1)} %pad_maximum_fusion), channel_id=1, replica_groups=mesh['tm_0'=4,'tm_1'=2,'row_0'=4,'row_1'=4] {'row_0','row_1'}, dimensions={0} | all-to-all | bytes 655360 | tf_op jit(solution)/shard_map/all_to_all | solution.py:469
  71.7 0.8 %unpack_part.1 = (bf16[16,4,1024]{2,1,0:T(4,128)(2,1)}, f32[8,128]{1,0:T(8,128)}) custom-call(bf16[16,8,1280]{2,1,0:T(8,128)(2,1)S(1)} %all_to_all.10.back_ref), custom_call_target="tpu_custom_call" | custom-call | tf_op jit(solution)/shard_map/unpack_part/pallas_call | solution.py:471
  (27 shorter events, 0.3 us)
Async XLA Ops:
  1.4 0.9 %copy-start.1 = (bf16[1,1,16,4,1024]{4,3,2,1,0:T(4,128)(2,1)S(1)}, bf16[1,1,16,4,1024]{4,3,2,1,0:T(4,128)(2,1)}, u32[]{:S(2)}) copy-start(bf16[1,1,16,4,1024]{4,3,2,1,0:T(4,128)(2,1)} %param.8) | copy-start | bytes 393220
  3.8 16.7 %all-to-all-start = ((bf16[16,8,1152]{2,1,0:T(8,128)(2,1)}), bf16[16,8,1152]{2,1,0:T(8,128)(2,1)S(1)}, u32[]{:S(2)}, u32[]{:S(2)}) async-start(bf16[16,8,1152]{2,1,0:T(8,128)(2,1)} %pack_part.1), calls=%async_computation | async-start | bytes 589824 | tf_op jit(solution)/shard_map/all_to_all | solution.py:423
  10.9 1.1 %copy-start = (bf16[4,4,16,1536]{3,2,1,0:T(8,128)(2,1)S(1)}, bf16[4,4,16,1536]{3,2,1,0:T(8,128)(2,1)}, u32[]{:S(2)}) copy-start(bf16[4,4,16,1536]{3,2,1,0:T(8,128)(2,1)} %pixel_ref.1) | copy-start | bytes 2359300
  12.8 25.6 %collective-permute-start.1 = (bf16[4,3,16,1536]{3,2,1,0:T(8,128)(2,1)S(1)}, bf16[4,3,16,1536]{3,2,1,0:T(8,128)(2,1)S(1)}, u32[]{:S(2)}, u32[]{:S(2)}) collective-permute-start(bf16[4,3,16,1536]{3,2,1,0:T(8,128)(2,1)S(1)} %get-tuple-element.24), channel_id=1, source_target_pairs={{0,1},{1,2},{2,3},{3,4},{4,5},{5,6},{6,7},{7,8},{8,9},{9,10},{10,1... | collective-permute-start | bytes 1769480 | tf_op jit(solution)/shard_map/ppermute | solution.py:396
  14.8 23.6 %collective-permute-start.2 = (bf16[1,4,16,1536]{3,2,1,0:T(8,128)(2,1)S(1)}, bf16[1,4,16,1536]{3,2,1,0:T(8,128)(2,1)S(1)}, u32[]{:S(2)}, u32[]{:S(2)}) collective-permute-start(bf16[1,4,16,1536]{3,2,1,0:T(8,128)(2,1)S(1)} %get-tuple-element.25), channel_id=1, source_target_pairs={{0,16},{16,32},{32,48},{48,64},{64,80},{80,96},{96,112},{112,0},{1... | collective-permute-start | bytes 589832 | tf_op jit(solution)/shard_map/ppermute | solution.py:396
  14.8 23.6 %collective-permute-start.3 = (bf16[1,3,16,1536]{3,2,1,0:T(8,128)(2,1)S(1)}, bf16[1,3,16,1536]{3,2,1,0:T(8,128)(2,1)S(1)}, u32[]{:S(2)}, u32[]{:S(2)}) collective-permute-start(bf16[1,3,16,1536]{3,2,1,0:T(8,128)(2,1)S(1)} %get-tuple-element.26), channel_id=1, source_target_pairs={{0,17},{1,18},{2,19},{3,20},{4,21},{5,22},{6,23},{7,24},{8,25},{9,... | collective-permute-start | bytes 442376 | tf_op jit(solution)/shard_map/ppermute | solution.py:407
  20.4 7.4 %collective-permute-start = (bf16[128,1152]{1,0:T(8,128)(2,1)S(1)}, bf16[128,1152]{1,0:T(8,128)(2,1)S(1)}, u32[]{:S(2)}, u32[]{:S(2)}) collective-permute-start(bf16[128,1152]{1,0:T(8,128)(2,1)S(1)} %bitcast.11), channel_id=1, source_target_pairs={{0,16},{16,32},{32,48},{48,64},{64,80},{80,96},{96,112},{112,0},{1... | collective-permute-start | bytes 884744 | tf_op jit(solution)/shard_map/ppermute | solution.py:396
  27.8 0.7 copy-start.2
  28.5 10.0 %copy-start.3 = (s32[2,2]{1,0:T(2,128)S(1)}, s32[2,2]{1,0:T(2,128)}, u32[]{:S(2)}) copy-start(s32[2,2]{1,0:T(2,128)} %shift_ref.3) | copy-start | bytes 52
  48.1 1.2 %collective-permute-start.5 = (f32[8,128]{1,0:T(8,128)S(1)}, f32[8,128]{1,0:T(8,128)S(1)}, u32[]{:S(2)}, u32[]{:S(2)}) collective-permute-start(f32[8,128]{1,0:T(8,128)S(1)} %get-tuple-element.29), channel_id=1, source_target_pairs={{0,16},{16,0},{1,17},{17,1},{2,18},{18,2},{3,19},{19,3},{4,20},{20... | collective-permute-start | bytes 12296 | tf_op jit(solution)/shard_map/ppermute | solution.py:396
  49.3 5.1 %collective-permute-start.6 = (f32[8,128]{1,0:T(8,128)S(1)}, f32[8,128]{1,0:T(8,128)S(1)}, u32[]{:S(2)}, u32[]{:S(2)}) collective-permute-start(f32[8,128]{1,0:T(8,128)S(1)} %add.72), channel_id=1, source_target_pairs={{0,64},{32,96},{64,0},{96,32},{1,65},{33,97},{65,1},{97,33},{2,66}... | collective-permute-start | bytes 12296 | tf_op jit(solution)/shard_map/ppermute | solution.py:396
  49.7 4.8 %collective-permute-start.7 = (f32[8,128]{1,0:T(8,128)S(1)}, f32[8,128]{1,0:T(8,128)S(1)}, u32[]{:S(2)}, u32[]{:S(2)}) collective-permute-start(f32[8,128]{1,0:T(8,128)S(1)} %add.72), channel_id=1, source_target_pairs={{0,32},{32,64},{64,96},{96,0},{1,33},{33,65},{65,97},{97,1},{2,34}... | collective-permute-start | bytes 12296 | tf_op jit(solution)/shard_map/ppermute | solution.py:396
  50.7 3.8 %collective-permute-start.8 = (f32[8,128]{1,0:T(8,128)S(1)}, f32[8,128]{1,0:T(8,128)S(1)}, u32[]{:S(2)}, u32[]{:S(2)}) collective-permute-start(f32[8,128]{1,0:T(8,128)S(1)} %add.72), channel_id=1, source_target_pairs={{0,96},{32,0},{64,32},{96,64},{1,97},{33,1},{65,33},{97,65},{2,98}... | collective-permute-start | bytes 12296 | tf_op jit(solution)/shard_map/ppermute | solution.py:396
  53.0 3.9 %collective-permute-start.4 = (bf16[128,1024]{1,0:T(8,128)(2,1)S(1)}, bf16[128,1024]{1,0:T(8,128)(2,1)S(1)}, u32[]{:S(2)}, u32[]{:S(2)}) collective-permute-start(bf16[128,1024]{1,0:T(8,128)(2,1)S(1)} %get-tuple-element.28), channel_id=1, source_target_pairs={{0,112},{16,0},{32,16},{48,32},{64,48},{80,64},{96,80},{112,96},{1... | collective-permute-start | bytes 786440 | tf_op jit(solution)/shard_map/ppermute | solution.py:396

commit v4 on v3

v4 whole, which is shorter than its diff:
```python
import functools
import math

import jax
import jax.numpy as jnp
from jax import lax
from jax.experimental import pallas as pl
from jax.experimental.pallas import tpu as pltpu
from jax.sharding import Mesh
from jax.sharding import PartitionSpec as P

WT = 2
WH = 4
WW = 8
D = 1024
PIX = 1536
GROUP = PIX // 3
TOK = 256
HALF = TOK // 2
WIN = WT * WH * WW
PAIRS = D // 128
SLOTS = 128
TM = ("tm_0", "tm_1")
ROW = ("row_0", "row_1")
ALL = TM + ROW
BF = jnp.bfloat16
F32 = jnp.float32
NT_DIMS = (((1,), (1,)), ((), ()))
TN_DIMS = (((0,), (0,)), ((), ()))
NN_DIMS = (((1,), (0,)), ((), ()))
VMEM = pltpu.MemorySpace.VMEM
SMEM = pltpu.MemorySpace.SMEM
HBM = pltpu.MemorySpace.HBM


def dot(a, b, dims):
    return lax.dot_general(a, b, dims, preferred_element_type=F32)


def lane_mean(values):
    return jnp.sum(values, axis=-1, keepdims=True) * (1.0 / values.shape[-1])


def normalise(values):
    center = values - lane_mean(values)
    scale = lax.rsqrt(lane_mean(center * center) + 1e-05)
    return center * scale, scale


def normalise_back(cotangent, normed, scale):
    return scale * (cotangent - lane_mean(cotangent) - normed * lane_mean(cotangent * normed))


def two_heads(rows):
    first = lax.broadcasted_iota(jnp.int32, rows.shape, 1) < 64
    zero = jnp.zeros_like(rows)
    return jnp.concatenate([jnp.where(first, rows, zero), jnp.where(first, zero, rows)], axis=0)


def own_head(rows):
    first = lax.broadcasted_iota(jnp.int32, (WIN, 128), 1) < 64
    return jnp.where(first, rows[:WIN], rows[WIN:])


def slot_one_hot(shift_ref, rows_ref, behind, frame_pair):
    place = rows_ref[:, D : D + 128].astype(F32).astype(jnp.int32)
    frame = place >> 6
    row = (place >> 4) & 3
    column = place & 15
    group = column >> 3
    slot = lax.broadcasted_iota(jnp.int32, (SLOTS, 128), 0) & 7
    lane = lax.broadcasted_iota(jnp.int32, (SLOTS, 128), 1)
    frame = frame + jnp.where(group == 0, shift_ref[0:1], shift_ref[1:2]) - 4 * behind
    row = row + jnp.where(group == 0, shift_ref[2:3], shift_ref[3:4]) - jnp.where(slot >= 4, 4, 0)
    inside = (place >= 0) & ((frame >> 1) == frame_pair) & (row >= 0) & (row < 4)
    token = group * 64 + ((frame & 1) * 32) + row * 8 + (column & 7)
    token = jnp.where(inside, token, -1)
    return jnp.where(token == lane, 1.0, 0.0).astype(BF)


def embed(frame_pair, mask_ref, frames_ref, rows_ref, columns_ref, chosen_ref, seen_ref, embedded_ref, normed_ref):
    mask = mask_ref[...].astype(F32)
    mask = jnp.concatenate([mask[at : at + 1] for at in range(8)], axis=1)
    for block in range(HALF // 16):
        group, half = divmod(block, 4)
        at_frame = group * 4 + frame_pair * 2 + half // 2
        rows = slice(block * 16, block * 16 + 16)
        start = jnp.where(jnp.concatenate([seen_ref[rows]] * 8, axis=1) > 0, chosen_ref[rows], mask)
        position = []
        for at in range(2):
            at_row = group * 4 + (half % 2) * 2 + at
            position.append(
                jnp.concatenate(
                    [
                        jnp.broadcast_to(frames_ref[at_frame : at_frame + 1], (8, 256)),
                        jnp.broadcast_to(rows_ref[at_row : at_row + 1], (8, 384)),
                        columns_ref[group * 8 : group * 8 + 8],
                    ],
                    axis=1,
                )
            )
        embedded = (start + jnp.concatenate(position, axis=0)).astype(BF)
        embedded_ref[rows] = embedded
        normed_ref[rows] = normalise(embedded.astype(F32))[0].astype(BF)


def project(at, normed_ref, w_qkv_ref, qkv_ref):
    for part in range(2):
        cols = slice(at * D + part * 512, at * D + part * 512 + 512)
        qkv_ref[:, cols] = dot(normed_ref[...], w_qkv_ref[:, cols], NN_DIMS).astype(BF)


def attend(qkv_ref, probs_ref, heads_ref):
    for window in range(HALF // WIN):
        rows = slice(window * WIN, window * WIN + WIN)
        scores = []
        for pair in range(PAIRS):
            q = qkv_ref[rows, pair * 128 : pair * 128 + 128]
            k = qkv_ref[rows, D + pair * 128 : D + pair * 128 + 128]
            scores.append(dot(k, two_heads(q), NT_DIMS) * 0.125)
        probs = []
        for pair in range(PAIRS):
            weights = jnp.exp(scores[pair] - jnp.max(scores[pair], axis=0, keepdims=True))
            probs.append((weights * (1.0 / jnp.sum(weights, axis=0, keepdims=True))).astype(BF))
            probs_ref[window, pair] = probs[pair]
        for pair in range(PAIRS):
            v = qkv_ref[rows, 2 * D + pair * 128 : 2 * D + pair * 128 + 128]
            heads_ref[rows, pair * 128 : pair * 128 + 128] = own_head(dot(probs[pair], v, TN_DIMS)).astype(BF)


def early_kernel(
    shift_ref, own_ref, mask_ref, frames_ref, rows_ref, columns_ref, w_qkv_hbm, w_out_hbm, w_head_hbm,
    embedded_ref, qkv_ref, probs_ref, seen_ref, one_hot_ref, heads_ref, w_qkv_ref, w_out_ref, w_head_ref,
    chosen_ref, normed_ref, sems,
):
    copies = [
        pltpu.make_async_copy(
            w_qkv_hbm.at[:, pl.ds(at * D, D)], w_qkv_ref.at[:, pl.ds(at * D, D)], sems.at[at]
        )
        for at in range(3)
    ]
    copies.append(pltpu.make_async_copy(w_out_hbm, w_out_ref, sems.at[3]))
    copies.append(pltpu.make_async_copy(w_head_hbm, w_head_ref, sems.at[4]))
    for copy in copies:
        copy.start()
    one_hot_ref[...] = slot_one_hot(shift_ref, own_ref, 0, 1)
    chosen_ref[...] = dot(one_hot_ref[...], own_ref[:, :D], TN_DIMS)
    seen_ref[...] = dot(one_hot_ref[...], jnp.ones((SLOTS, 128), BF), TN_DIMS)
    embed(1, mask_ref, frames_ref, rows_ref, columns_ref, chosen_ref, seen_ref, embedded_ref, normed_ref)
    for at in range(3):
        copies[at].wait()
        project(at, normed_ref, w_qkv_ref, qkv_ref)
    attend(qkv_ref, probs_ref, heads_ref)
    copies[3].wait()
    copies[4].wait()


def late_kernel(
    shift_ref, own_ref, behind_ref, mask_ref, frames_ref, rows_ref, columns_ref, embedded_1_ref, heads_1_ref,
    w_qkv_ref, w_out_ref, w_head_ref,
    embedded_ref, qkv_ref, probs_ref, seen_ref, one_hot_ref, head_normed_ref, scale_ref, predicted_ref,
    chosen_ref, normed_ref, heads_ref, residual_ref, narrow_ref,
):
    one_hot_ref[:SLOTS] = slot_one_hot(shift_ref, own_ref, 0, 0)
    one_hot_ref[SLOTS:] = slot_one_hot(shift_ref, behind_ref, 1, 0)
    own_hot = one_hot_ref[:SLOTS]
    behind_hot = one_hot_ref[SLOTS:]
    chosen_ref[...] = dot(own_hot, own_ref[:, :D], TN_DIMS) + dot(behind_hot, behind_ref[:, :D], TN_DIMS)
    seen_ref[...] = dot(one_hot_ref[...], jnp.ones((2 * SLOTS, 128), BF), TN_DIMS)
    embed(0, mask_ref, frames_ref, rows_ref, columns_ref, chosen_ref, seen_ref, embedded_ref, normed_ref)
    for at in range(3):
        project(at, normed_ref, w_qkv_ref, qkv_ref)
    heads_ref[HALF:] = heads_1_ref[...]
    attend(qkv_ref, probs_ref, heads_ref)
    for part in range(2):
        cols = slice(part * 512, part * 512 + 512)
        attn = dot(heads_ref[...], w_out_ref[:, cols], NN_DIMS).astype(BF).astype(F32)
        residual_ref[:HALF, cols] = embedded_ref[:, cols].astype(F32) + attn[:HALF]
        residual_ref[HALF:, cols] = embedded_1_ref[:, cols].astype(F32) + attn[HALF:]
    for block in range(TOK // 16):
        rows = slice(block * 16, block * 16 + 16)
        normed, scale = normalise(residual_ref[rows])
        head_normed_ref[rows] = normed
        scale_ref[rows] = jnp.broadcast_to(scale, (16, 128))
        narrow_ref[rows] = normed.astype(BF)
    for part in range(3):
        cols = slice(part * GROUP, part * GROUP + GROUP)
        predicted_ref[:, cols] = dot(narrow_ref[...], w_head_ref[:, cols], NN_DIMS)


def backward_kernel(
    shift_ref, embedded_0_ref, qkv_0_ref, probs_0_ref, seen_0_ref, one_hot_0_ref,
    embedded_1_ref, qkv_1_ref, probs_1_ref, seen_1_ref, one_hot_1_ref,
    normed_ref, scale_ref, predicted_ref, w_qkv_ref, w_out_ref, w_head_ref,
    own_target, row_target, last_row_target, time_target, corner_target,
    own_picked_ref, behind_picked_ref, total_ref,
    target_ref, error_ref, narrow_ref, wide_ref, stream_ref, dqkv_ref,
):
    embedded_refs = (embedded_0_ref, embedded_1_ref)
    qkv_refs = (qkv_0_ref, qkv_1_ref)
    probs_refs = (probs_0_ref, probs_1_ref)
    seen_refs = (seen_0_ref, seen_1_ref)
    target_ref[1:, 3:] = own_target[...]
    target_ref[1:4, :3] = row_target[...]
    target_ref[4:, :3] = last_row_target[...]
    target_ref[:1, 3:] = time_target[...]
    target_ref[:1, :3] = corner_target[...]

    for block in range(TOK // 16):
        frame_pair, rest = divmod(block, 8)
        group, half = divmod(rest, 4)
        rows = slice(block * 16, block * 16 + 16)
        local = slice(rest * 16, rest * 16 + 16)
        masked = 1.0 - jnp.concatenate([seen_refs[frame_pair][local]] * 12, axis=1)
        target = jnp.concatenate(
            [
                target_ref[
                    frame_pair * 2 + half // 2 - shift_ref[0, group] + 1,
                    (half % 2) * 2 + at - shift_ref[1, group] + 3,
                    group * 8 : group * 8 + 8,
                ].astype(F32)
                for at in range(2)
            ],
            axis=0,
        )
        error_ref[rows] = (masked * (predicted_ref[rows] - target)).astype(BF)

    for part in range(2):
        cols = slice(part * 512, part * 512 + 512)
        wide_ref[:, cols] = dot(error_ref[...], w_head_ref[cols, :], NT_DIMS)

    for block in range(TOK // 16):
        rows = slice(block * 16, block * 16 + 16)
        scale = jnp.concatenate([scale_ref[rows]] * 8, axis=1)
        cotangent = wide_ref[rows].astype(BF).astype(F32)
        grad = normalise_back(cotangent, normed_ref[rows], scale)
        stream_ref[rows] = grad
        narrow_ref[rows] = grad.astype(BF)

    narrow_ref[...] = dot(narrow_ref[...], w_out_ref[...], NT_DIMS).astype(BF)

    for window in range(TOK // WIN):
        rows = slice(window * WIN, window * WIN + WIN)
        frame_pair, group = divmod(window, 2)
        local = slice(group * WIN, group * WIN + WIN)
        qkv_ref = qkv_refs[frame_pair]
        probs_ref = probs_refs[frame_pair]
        cols = [[slice(at * D + pair * 128, at * D + pair * 128 + 128) for at in range(3)] for pair in range(PAIRS)]
        d_probs = []
        out_heads = []
        for pair in range(PAIRS):
            out_heads.append(two_heads(narrow_ref[rows, cols[pair][0]]))
            d_probs.append(dot(qkv_ref[local, cols[pair][2]], out_heads[pair], NT_DIMS))
        for pair in range(PAIRS):
            dqkv_ref[rows, cols[pair][2]] = dot(probs_ref[group, pair], out_heads[pair], NN_DIMS).astype(BF)
        d_scores = []
        for pair in range(PAIRS):
            probs = probs_ref[group, pair].astype(F32)
            cotangent = d_probs[pair].astype(BF).astype(F32)
            mean = jnp.sum(cotangent * probs, axis=0, keepdims=True)
            d_scores.append((probs * (cotangent - mean) * 0.125).astype(BF))
        for pair in range(PAIRS):
            q_heads = two_heads(qkv_ref[local, cols[pair][0]])
            dqkv_ref[rows, cols[pair][1]] = dot(d_scores[pair], q_heads, NN_DIMS).astype(BF)
        for pair in range(PAIRS):
            d_q = own_head(dot(d_scores[pair], qkv_ref[local, cols[pair][1]], TN_DIMS))
            dqkv_ref[rows, cols[pair][0]] = d_q.astype(BF)

    for part in range(2):
        cols = slice(part * 512, part * 512 + 512)
        wide_ref[:, cols] = dot(dqkv_ref[...], w_qkv_ref[cols, :], NT_DIMS)

    total = jnp.zeros((8, D), F32)
    for block in range(TOK // 16):
        frame_pair, rest = divmod(block, 8)
        rows = slice(block * 16, block * 16 + 16)
        local = slice(rest * 16, rest * 16 + 16)
        normed, scale = normalise(embedded_refs[frame_pair][local].astype(F32))
        cotangent = wide_ref[rows].astype(BF).astype(F32)
        grad = stream_ref[rows] + normalise_back(cotangent, normed, scale)
        narrow_ref[rows] = grad.astype(BF)
        part = (1.0 - jnp.concatenate([seen_refs[frame_pair][local]] * 8, axis=1)) * grad
        total = total + part[:8] + part[8:]
    total = jnp.sum(total, axis=0, keepdims=True)
    total_ref[...] = jnp.concatenate([total[:, at * 128 : at * 128 + 128] for at in range(8)], axis=0)
    behind_picked_ref[...] = dot(one_hot_0_ref[SLOTS:], narrow_ref[:HALF], NN_DIMS).astype(BF)
    own_picked = dot(one_hot_0_ref[:SLOTS], narrow_ref[:HALF], NN_DIMS)
    own_picked_ref[...] = (own_picked + dot(one_hot_1_ref[...], narrow_ref[HALF:], NN_DIMS)).astype(BF)


def pack_kernel(
    place_hbm, shift_hbm, rows_hbm, packed_ref, shift_rows_ref, place_ref, shift_ref, rows_ref, sems
):
    copies = [
        pltpu.make_async_copy(rows_hbm, rows_ref, sems.at[0]),
        pltpu.make_async_copy(place_hbm, place_ref, sems.at[1]),
        pltpu.make_async_copy(shift_hbm, shift_ref, sems.at[2]),
    ]
    for copy in copies:
        copy.start()
    copies[1].wait()
    slot = lax.broadcasted_iota(jnp.int32, (8, 128), 0)
    peers = rows_ref.shape[0]
    for peer in range(peers):
        places = jnp.zeros((8, 128), jnp.int32)
        for at in range(8):
            source = peer if at < 4 else (peer - 1) % peers
            places = jnp.where(slot == at, place_ref[source, at % 4], places)
        packed_ref[peer, :, D:] = places.astype(F32).astype(BF)
    copies[2].wait()
    shifts = jnp.zeros((8, 128), jnp.int32)
    for at in range(4):
        shifts = jnp.where(slot == at, shift_ref[at // 2, at % 2], shifts)
    shift_rows_ref[...] = shifts
    copies[0].wait()
    rows = rows_ref[...].astype(F32)
    before = jnp.concatenate([rows[-1:], rows[:-1]], axis=0)
    packed_ref[:, :, :D] = jnp.concatenate([rows, before], axis=1).astype(BF)


def target_kernel(pixel_hbm, own_ref, row_ref, last_row_ref, time_ref, pixel_ref, sems):
    copies = [pltpu.make_async_copy(pixel_hbm.at[at], pixel_ref.at[at], sems.at[at]) for at in range(4)]
    for frame in (3, 0, 1, 2):
        copies[frame].start()
    for frame in (3, 0, 1, 2):
        copies[frame].wait()
        for row in range(4):
            for part in range(3):
                cols = slice(part * GROUP, part * GROUP + GROUP)
                raw = pixel_ref[frame, row, :, cols].astype(F32)
                center = raw - lane_mean(raw)
                spread = jnp.sqrt(jnp.sum(center * center, axis=-1, keepdims=True) * (1.0 / (GROUP - 1)))
                target = (center * (1.0 / (spread + 1e-06))).astype(BF)
                own_ref[frame, row, :, cols] = target
                if row > 0 and frame < 3:
                    row_ref[frame, row - 1, :, cols] = target
                if row > 0 and frame == 3:
                    last_row_ref[0, row - 1, :, cols] = target
                if frame == 3:
                    time_ref[0, row, :, cols] = target


def unpack_kernel(scale, back_ref, rows_ref, total_ref):
    rows = back_ref[:, :4, :D].astype(F32)
    after = back_ref[:, 4:, :D].astype(F32)
    after = jnp.concatenate([after[1:], after[:1]], axis=0)
    rows_ref[...] = (rows + after).astype(BF)
    sums = jnp.sum(back_ref[:, :, D:].astype(F32), axis=0)
    total_ref[...] = (sums[:, :128] + sums[:, 128:]) * scale


def shapes(*items):
    return [jax.ShapeDtypeStruct(dims, kind) for dims, kind in items]


def call(kernel, outputs, scratch, in_specs, limit):
    return pl.pallas_call(
        kernel,
        in_specs=in_specs,
        out_specs=[pl.BlockSpec(memory_space=VMEM)] * len(outputs),
        out_shape=shapes(*outputs),
        scratch_shapes=scratch,
        compiler_params=pltpu.CompilerParams(vmem_limit_bytes=limit << 20),
    )


def in_space(space, count):
    return [pl.BlockSpec(memory_space=space)] * count


def half_outputs(slots):
    return [
        ((HALF, D), BF),
        ((HALF, 3 * D), BF),
        ((HALF // WIN, PAIRS, WIN, 128), BF),
        ((HALF, 128), F32),
        ((slots, HALF), BF),
    ]


def pack_part(*operands):
    outputs = [((16, 8, D + 128), BF), ((8, 128), jnp.int32)]
    scratch = [
        pltpu.SMEM((16, 4), jnp.int32),
        pltpu.SMEM((2, 2), jnp.int32),
        pltpu.VMEM((16, 4, D), BF),
        pltpu.SemaphoreType.DMA((3,)),
    ]
    return call(pack_kernel, outputs, scratch, in_space(HBM, 3), 8)(*operands)


def target_part(*operands):
    outputs = [((frames, rows, 16, PIX), BF) for frames, rows in ((4, 4), (3, 3), (1, 3), (1, 4))]
    scratch = [pltpu.VMEM((4, 4, 16, PIX), BF), pltpu.SemaphoreType.DMA((4,))]
    return call(target_kernel, outputs, scratch, in_space(HBM, 1), 8)(*operands)


def early_part(*operands):
    outputs = half_outputs(SLOTS) + [((HALF, D), BF), ((D, 3 * D), BF), ((D, D), BF), ((D, PIX), BF)]
    scratch = [pltpu.VMEM((HALF, D), F32), pltpu.VMEM((HALF, D), BF), pltpu.SemaphoreType.DMA((5,))]
    return call(early_kernel, outputs, scratch, in_space(VMEM, 6) + in_space(HBM, 3), 20)(*operands)


def late_part(*operands):
    outputs = half_outputs(2 * SLOTS) + [((TOK, D), F32), ((TOK, 128), F32), ((TOK, PIX), F32)]
    scratch = [
        pltpu.VMEM((HALF, D), F32),
        pltpu.VMEM((HALF, D), BF),
        pltpu.VMEM((TOK, D), BF),
        pltpu.VMEM((TOK, D), F32),
        pltpu.VMEM((TOK, D), BF),
    ]
    return call(late_kernel, outputs, scratch, in_space(VMEM, 12), 26)(*operands)


def backward_part(*operands):
    outputs = [((SLOTS, D), BF), ((SLOTS, D), BF), ((8, 128), F32)]
    scratch = [
        pltpu.VMEM((5, 7, 16, PIX), BF),
        pltpu.VMEM((TOK, PIX), BF),
        pltpu.VMEM((TOK, D), BF),
        pltpu.VMEM((TOK, D), F32),
        pltpu.VMEM((TOK, D), F32),
        pltpu.VMEM((TOK, 3 * D), BF),
    ]
    return call(backward_kernel, outputs, scratch, in_space(SMEM, 1) + in_space(VMEM, 21), 34)(*operands)


def sinusoid(coordinate, channel_count):
    half_count = channel_count // 2
    frequency = jnp.exp(-math.log(10000.0) * jnp.arange(half_count, dtype=F32) / half_count)
    angles = coordinate.astype(F32)[..., None] * frequency
    return jnp.concatenate([jnp.sin(angles), jnp.cos(angles)], axis=-1)


def move(value, axis, steps):
    count = lax.axis_size(axis)
    return lax.ppermute(value, axis, [(at, (at + steps) % count) for at in range(count)])


def per_device(visible, slot_pos, window_shift, mask_token, w_qkv, w_out, w_head, pixels):
    frame_count, row_count = pixels.shape[:2]
    peers, slots = slot_pos.shape[2:]
    hold = functools.partial(pltpu.with_memory_space_constraint, memory_space=HBM)
    packed, shift_rows = pack_part(
        hold(slot_pos.reshape(peers, slots)), hold(window_shift), hold(visible.reshape(peers, slots, D))
    )
    own = lax.all_to_all(packed, ROW, split_axis=0, concat_axis=0, tiled=True).reshape(SLOTS, D + 128)
    behind = move(own, TM, 1)
    own_target, row_target, last_row_target, time_target = target_part(hold(pixels))
    last_row_target = move(last_row_target, ROW, 1)
    row_target = move(row_target, ROW, 1)
    time_target = move(time_target, TM, 1)
    corner_target = move(last_row_target, TM, 1)

    local = jnp.arange(4, dtype=jnp.int32)
    frame_total = frame_count * lax.axis_size(TM)
    row_total = row_count * lax.axis_size(ROW)
    frames = (lax.axis_index(TM) * frame_count + local[None] - window_shift[0][:, None]) % frame_total
    band = (lax.axis_index(ROW) * row_count + local[None] - window_shift[1][:, None]) % row_total
    frame_table = sinusoid(frames.reshape(-1), 256)
    row_table = sinusoid(band.reshape(-1), 384)
    column_table = sinusoid(jnp.arange(16, dtype=jnp.int32), 384)

    tables = (mask_token.reshape(8, 128), frame_table, row_table, column_table)
    *half_1, heads_1, w_qkv, w_out, w_head = early_part(
        shift_rows, own, *tables, hold(w_qkv), hold(w_out), hold(w_head)
    )
    *half_0, head_normed, head_scale, predicted = late_part(
        shift_rows, own, behind, *tables, half_1[0], heads_1, w_qkv, w_out, w_head
    )
    own_picked, behind_picked, local_total = backward_part(
        window_shift, *half_0, *half_1, head_normed, head_scale, predicted, w_qkv, w_out, w_head,
        own_target, row_target, last_row_target, time_target, corner_target,
    )
    from_next = move(behind_picked, TM, -1)
    mine = own_picked + from_next
    other = move(local_total, "tm_1", 1)
    local_total = local_total + other
    turned = [move(local_total, "tm_0", step) for step in (1, 2, 3)]
    local_total = (local_total + turned[1]) + (turned[0] + turned[2])
    high = local_total.astype(BF)
    low = (local_total - high.astype(F32)).astype(BF)
    sums = jnp.broadcast_to(jnp.concatenate([high, low], axis=1)[None], (peers, 8, 256))
    sent = jnp.concatenate([mine.reshape(peers, 2 * slots, D), sums], axis=-1)
    back = lax.all_to_all(sent, ROW, split_axis=0, concat_axis=0, tiled=True)
    grad_scale = (frame_total * row_total * pixels.shape[2]) ** (-0.5)
    outputs = [((peers, slots, D), BF), ((8, 128), F32)]
    unpack = call(functools.partial(unpack_kernel, grad_scale), outputs, [], in_space(VMEM, 1), 8)
    d_visible, d_mask = unpack(back)
    return (d_visible.reshape(visible.shape), d_mask.reshape(D))


def solution(mesh):
    torus = Mesh(mesh.devices.reshape(4, 2, 4, 4), ALL)
    return jax.shard_map(
        per_device,
        mesh=torus,
        in_specs=(
            P(TM, ROW, None, None, None),
            P(TM, ROW, None, None),
            P(),
            P(),
            P(),
            P(),
            P(),
            P(TM, ROW, None, None),
        ),
        out_specs=(P(TM, ROW, None, None, None), P()),
        check_vma=False,
    )
```

time: 73.8 us -> 69.5 us (0.942)
  waiting for transfers between devices: 15.6 us -> 10.3 us
  starting transfers between devices: 16 us -> 19.5 us
  local copies, waits for them, and re-layouts: 5.09 us -> 2.98 us
  blocking collectives: 14.8 us -> 14 us
    ppermute x8 -> x10, starting transfers between devices: 5.74 us -> 12.4 us  [move(): lax.ppermute(value, axis, [(at, (at + steps) % count) for at in range(cou...]
    ppermute x8 -> x10, waiting for transfers between devices: 11.6 us -> 7.61 us  [move(): lax.ppermute(value, axis, [(at, (at + steps) % count) for at in range(cou...]
    ppermute x1 -> x0, starting transfers between devices: 3.1 us -> none  [move_corner(): return lax.ppermute(value, ALL, pairs)]
    ppermute x1 -> x0, waiting for transfers between devices: 2.94 us -> none  [move_corner(): return lax.ppermute(value, ALL, pairs)]
    unnamed x8 -> x6, local copies, waits for them, and re-layouts: 2.71 us -> 0.69 us
    all_to_all x1, waiting for transfers between devices: 1.06 us -> 2.67 us  [per_device(): lax.all_to_all(packed, ROW, split_axis=0, concat_axis=0, tiled=True)]
    all_to_all x1, blocking collectives: 14.8 us -> 14 us  [per_device(): back = lax.all_to_all(sent, ROW, split_axis=0, concat_axis=0, tiled=True)]
    pallas_call x5 -> x6, Pallas kernels: 19.6 us -> 19.9 us  [the longest x1 6.72 us: backward_part(): call(backward_kernel, outputs, scratch, in_space(SMEM, 1) + in_space(VMEM...]
  transfers between devices with their start and end apart: 10 -> 11, of which waited for: 7 -> 5; matrix products, arithmetic and copies ran while one was open for 3% -> 2% of each run, Pallas kernels for 11% -> 16%
where the time goes in v4:
time: 69.5 us; the launch traced here: 68.2 us
  Pallas kernels  19.9 us (29%)
  starting transfers between devices  19.5 us (28%)
  blocking collectives  14 us (20%)
  waiting for transfers between devices  10.3 us (15%)
  local copies, waits for them, and re-layouts  2.98 us (4%)
  between operations  0.83 us (1%)
  other arithmetic  0.72 us (1%)
    all_to_all x1, blocking collectives, per_device(): back = lax.all_to_all(sent, ROW, split_axis=0, concat_axis=0, tiled=True)  14 us
    ppermute x10, starting transfers between devices, move(): lax.ppermute(value, axis, [(at, (at + steps) % count) for at in range(cou...  12.4 us
    ppermute x10, waiting for transfers between devices, move(): lax.ppermute(value, axis, [(at, (at + steps) % count) for at in range(cou...  7.61 us
    all_to_all x1, starting transfers between devices, per_device(): lax.all_to_all(packed, ROW, split_axis=0, concat_axis=0, tiled=True)  7.16 us
    pallas_call x1, Pallas kernels, backward_part(): call(backward_kernel, outputs, scratch, in_space(SMEM, 1) + in_space(VMEM...  6.72 us
    pallas_call x1, Pallas kernels, early_part(): call(early_kernel, outputs, scratch, in_space(VMEM, 6) + in_space(HBM, 3)...  4.55 us
    pallas_call x1, Pallas kernels, late_part(): call(late_kernel, outputs, scratch, in_space(VMEM, 12), 26)(*operands)  4.17 us
    all_to_all x1, waiting for transfers between devices, per_device(): lax.all_to_all(packed, ROW, split_axis=0, concat_axis=0, tiled=True)  2.67 us
  transfers between devices with their start and end apart: 11, of which 5 were waited for; matrix products, arithmetic and copies ran while one was open for 2% of the time, Pallas kernels for 16%

profile of v4, /device:TPU:0, one launch (start us, length us, event | category | flops | bytes accessed | tf_op | source)
XLA Modules:
  0.0 68.2 jit_solution(13253539104243723679)
XLA Ops:
  0.6 1.4 %copy.10.place_hbm = s32[16,4]{1,0:T(8,128)} copy(s32[16,4]{0,1:T(4,128)} %bitcast.18) | data formatting | bytes 512 | tf_op jit(solution)/shard_map/reshape | solution.py:446
  2.0 1.8 %shard_map.95 = (bf16[16,8,1152]{2,1,0:T(8,128)(2,1)}, s32[8,128]{1,0:T(8,128)S(1)}) custom-call(s32[16,4]{1,0:T(8,128)} %copy.10.place_hbm, s32[2,2]{1,0:T(2,128)} %shift_ref.1, bf16[16,4,1024]{2,1,0:T(4,128)(2,1)} %bitcast.17), custom_call_target="tpu_custom_call" | custom-call | tf_op jit(solution)/shard_map/pallas_call | solution.py:389
  3.8 7.2 %all-to-all-start = ((bf16[16,8,1152]{2,1,0:T(8,128)(2,1)}), bf16[16,8,1152]{2,1,0:T(8,128)(2,1)S(1)}, u32[]{:S(2)}, u32[]{:S(2)}) async-start(bf16[16,8,1152]{2,1,0:T(8,128)(2,1)} %get-tuple-element.31), calls=%async_computation | async-start | bytes 589824 | tf_op jit(solution)/shard_map/all_to_all | solution.py:448
  10.9 1.9 %shard_map.98 = (bf16[4,4,16,1536]{3,2,1,0:T(8,128)(2,1)S(1)}, bf16[3,3,16,1536]{3,2,1,0:T(8,128)(2,1)S(1)}, bf16[1,3,16,1536]{3,2,1,0:T(8,128)(2,1)S(1)}, bf16[1,4,16,1536]{3,2,1,0:T(8,128)(2,1)S(1)}) custom-call(bf16[4,4,16,1536]{3,2,1,0:T(8,128)(2,1)} %pixel_hbm.1), custom_call_target="tpu_custom_call" | custom-call | tf_op jit(solution)/shard_map/pallas_call | solution.py:395
  12.8 2.0 %collective-permute-start.2 = (bf16[1,3,16,1536]{3,2,1,0:T(8,128)(2,1)S(1)}, bf16[1,3,16,1536]{3,2,1,0:T(8,128)(2,1)S(1)}, u32[]{:S(2)}, u32[]{:S(2)}) collective-permute-start(bf16[1,3,16,1536]{3,2,1,0:T(8,128)(2,1)S(1)} %get-tuple-element.51), channel_id=1, source_target_pairs={{0,1},{1,2},{2,3},{3,4},{4,5},{5,6},{6,7},{7,8},{8,9},{9,10},{10,1... | collective-permute-start | bytes 442376 | tf_op jit(solution)/shard_map/ppermute | solution.py:438
  14.8 1.5 %collective-permute-start.1 = (bf16[3,3,16,1536]{3,2,1,0:T(8,128)(2,1)S(1)}, bf16[3,3,16,1536]{3,2,1,0:T(8,128)(2,1)S(1)}, u32[]{:S(2)}, u32[]{:S(2)}) collective-permute-start(bf16[3,3,16,1536]{3,2,1,0:T(8,128)(2,1)S(1)} %get-tuple-element.50), channel_id=1, source_target_pairs={{0,1},{1,2},{2,3},{3,4},{4,5},{5,6},{6,7},{7,8},{8,9},{9,10},{10,1... | collective-permute-start | bytes 1327112 | tf_op jit(solution)/shard_map/ppermute | solution.py:438
  16.3 0.0 collective-permute-start.3
  16.3 0.8 %slice_bitcast_fusion = (s32[2]{0:T(128)S(1)}, s32[2]{0:T(128)S(1)}) fusion(s32[2,2]{1,0:T(2,128)} %shift_ref.1), kind=kLoop, calls=%fused_computation.26 | loop fusion | bytes 32 | tf_op jit(solution)/shard_map/sub | solution.py:460
  17.1 0.1 broadcast_subtract_fusion
  17.2 0.1 sub.58
  17.3 0.1 sub.53
  17.4 0.1 multiply_sine_fusion.1
  17.5 0.1 multiply_sine_fusion
  17.7 0.1 multiply_sine_fusion.2
  17.8 2.7 %all-to-all-done = bf16[16,8,1152]{2,1,0:T(8,128)(2,1)S(1)} async-done(((bf16[16,8,1152]{2,1,0:T(8,128)(2,1)}), bf16[16,8,1152]{2,1,0:T(8,128)(2,1)S(1)}, u32[]{:S(2)}, u32[]{:S(2)}) %all-to-all-start) | async-done | bytes 294944 | tf_op jit(solution)/shard_map/all_to_all | solution.py:448
  20.4 0.0 collective-permute-start
  20.4 0.1 pad_maximum_fusion.2.rows_ref
  20.5 2.9 %collective-permute-done.2.last_row_target = bf16[1,3,16,1536]{3,2,1,0:T(8,128)(2,1)S(1)} collective-permute-done((bf16[1,3,16,1536]{3,2,1,0:T(8,128)(2,1)S(1)}, bf16[1,3,16,1536]{3,2,1,0:T(8,128)(2,1)S(1)}, u32[]{:S(2)}, u32[]{:S(2)}) %collective-permute-start.2) | collective-permute-done | bytes 147488 | tf_op jit(solution)/shard_map/ppermute | solution.py:438
  23.4 0.1 pad_maximum_fusion.1.columns_ref
  23.5 0.7 copy-done.1
  24.2 4.5 %shard_map.96 = (bf16[128,1024]{1,0:T(8,128)(2,1)S(1)}, bf16[128,3072]{1,0:T(8,128)(2,1)S(1)}, bf16[2,8,64,128]{3,2,1,0:T(8,128)(2,1)S(1)}, f32[128,128]{1,0:T(8...) custom-call(s32[8,128]{1,0:T(8,128)S(1)} %get-tuple-element.30.shift, ...), custom_call_target="tpu_custom_call" | custom-call | tf_op jit(solution)/shard_map/pallas_call | solution.py:401
  28.7 0.0 copy-start
  28.7 4.2 %shard_map.97 = (bf16[128,1024]{1,0:T(8,128)(2,1)S(1)}, bf16[128,3072]{1,0:T(8,128)(2,1)S(1)}, bf16[2,8,64,128]{3,2,1,0:T(8,128)(2,1)S(1)}, f32[128,128]{1,0:T(8...) custom-call(s32[8,128]{1,0:T(8,128)S(1)} %get-tuple-element.30.shift, ...), custom_call_target="tpu_custom_call" | custom-call | tf_op jit(solution)/shard_map/pallas_call | solution.py:413
  33.0 6.7 %shard_map.99 = (bf16[128,1024]{1,0:T(8,128)(2,1)S(1)}, bf16[128,1024]{1,0:T(8,128)(2,1)S(1)}, f32[8,128]{1,0:T(8,128)S(1)}) custom-call(s32[2,2]{1,0:T(2,128)S(1)} %copy-done, bf16[128,1024]{1,0:T(8,128)(2,1)S(1)} %get-tuple-element.37.embedded_0_ref, bf16[128,3072]{1,0:T(8,128)(2,1)S(1)} %get-tuple-element.38.qkv_0_ref, ...), custom_call_target="tpu_custom_call" | custom-call | tf_op jit(solution)/shard_map/pallas_call | solution.py:426
  39.7 2.1 %collective-permute-start.6 = (f32[8,128]{1,0:T(8,128)S(1)}, f32[8,128]{1,0:T(8,128)S(1)}, u32[]{:S(2)}, u32[]{:S(2)}) collective-permute-start(f32[8,128]{1,0:T(8,128)S(1)} %get-tuple-element.55), channel_id=1, source_target_pairs={{0,16},{16,0},{1,17},{17,1},{2,18},{18,2},{3,19},{19,3},{4,20},{20... | collective-permute-start | bytes 12296 | tf_op jit(solution)/shard_map/ppermute | solution.py:438
  41.8 0.8 %collective-permute-done.6 = f32[8,128]{1,0:T(8,128)S(1)} collective-permute-done((f32[8,128]{1,0:T(8,128)S(1)}, f32[8,128]{1,0:T(8,128)S(1)}, u32[]{:S(2)}, u32[]{:S(2)}) %collective-permute-start.6) | collective-permute-done | bytes 4128 | tf_op jit(solution)/shard_map/ppermute | solution.py:438
  42.6 3.6 %collective-permute-start.7 = (f32[8,128]{1,0:T(8,128)S(1)}, f32[8,128]{1,0:T(8,128)S(1)}, u32[]{:S(2)}, u32[]{:S(2)}) collective-permute-start(f32[8,128]{1,0:T(8,128)S(1)} %add.72), channel_id=1, source_target_pairs={{0,64},{32,96},{64,0},{96,32},{1,65},{33,97},{65,1},{97,33},{2,66}... | collective-permute-start | bytes 12296 | tf_op jit(solution)/shard_map/ppermute | solution.py:438
  46.2 3.2 %collective-permute-start.9 = (f32[8,128]{1,0:T(8,128)S(1)}, f32[8,128]{1,0:T(8,128)S(1)}, u32[]{:S(2)}, u32[]{:S(2)}) collective-permute-start(f32[8,128]{1,0:T(8,128)S(1)} %add.72), channel_id=1, source_target_pairs={{0,96},{32,0},{64,32},{96,64},{1,97},{33,1},{65,33},{97,65},{2,98}... | collective-permute-start | bytes 12296 | tf_op jit(solution)/shard_map/ppermute | solution.py:438
  49.5 1.6 %collective-permute-done.8 = f32[8,128]{1,0:T(8,128)S(1)} collective-permute-done((f32[8,128]{1,0:T(8,128)S(1)}, f32[8,128]{1,0:T(8,128)S(1)}, u32[]{:S(2)}, u32[]{:S(2)}) %collective-permute-start.8) | collective-permute-done | bytes 4128 | tf_op jit(solution)/shard_map/ppermute | solution.py:438
  51.1 2.3 %collective-permute-done.5 = bf16[128,1024]{1,0:T(8,128)(2,1)S(1)} collective-permute-done((bf16[128,1024]{1,0:T(8,128)(2,1)S(1)}, bf16[128,1024]{1,0:T(8,128)(2,1)S(1)}, u32[]{:S(2)}, u32[]{:S(2)}) %collective-permute-start.5) | collective-permute-done | bytes 262176 | tf_op jit(solution)/shard_map/ppermute | solution.py:438
  53.5 14.0 %all_to_all.10.back_ref = bf16[16,8,1280]{2,1,0:T(8,128)(2,1)S(1)} all-to-all(bf16[16,8,1280]{2,1,0:T(8,128)(2,1)S(1)} %pad_maximum_fusion), channel_id=1, replica_groups=mesh['tm_0'=4,'tm_1'=2,'row_0'=4,'row_1'=4] {'row_0','row_1'}, dimensions={0} | all-to-all | bytes 655360 | tf_op jit(solution)/shard_map/all_to_all | solution.py:486
  67.4 0.8 %shard_map.100 = (bf16[16,4,1024]{2,1,0:T(4,128)(2,1)}, f32[8,128]{1,0:T(8,128)}) custom-call(bf16[16,8,1280]{2,1,0:T(8,128)(2,1)S(1)} %all_to_all.10.back_ref), custom_call_target="tpu_custom_call" | custom-call | tf_op jit(solution)/shard_map/pallas_call | solution.py:490
  (27 shorter events, 0.2 us)
Async XLA Ops:
  3.8 16.7 %all-to-all-start = ((bf16[16,8,1152]{2,1,0:T(8,128)(2,1)}), bf16[16,8,1152]{2,1,0:T(8,128)(2,1)S(1)}, u32[]{:S(2)}, u32[]{:S(2)}) async-start(bf16[16,8,1152]{2,1,0:T(8,128)(2,1)} %get-tuple-element.31), calls=%async_computation | async-start | bytes 589824 | tf_op jit(solution)/shard_map/all_to_all | solution.py:448
  12.8 10.5 %collective-permute-start.2 = (bf16[1,3,16,1536]{3,2,1,0:T(8,128)(2,1)S(1)}, bf16[1,3,16,1536]{3,2,1,0:T(8,128)(2,1)S(1)}, u32[]{:S(2)}, u32[]{:S(2)}) collective-permute-start(bf16[1,3,16,1536]{3,2,1,0:T(8,128)(2,1)S(1)} %get-tuple-element.51), channel_id=1, source_target_pairs={{0,1},{1,2},{2,3},{3,4},{4,5},{5,6},{6,7},{7,8},{8,9},{9,10},{10,1... | collective-permute-start | bytes 442376 | tf_op jit(solution)/shard_map/ppermute | solution.py:438
  14.8 18.1 %collective-permute-start.1 = (bf16[3,3,16,1536]{3,2,1,0:T(8,128)(2,1)S(1)}, bf16[3,3,16,1536]{3,2,1,0:T(8,128)(2,1)S(1)}, u32[]{:S(2)}, u32[]{:S(2)}) collective-permute-start(bf16[3,3,16,1536]{3,2,1,0:T(8,128)(2,1)S(1)} %get-tuple-element.50), channel_id=1, source_target_pairs={{0,1},{1,2},{2,3},{3,4},{4,5},{5,6},{6,7},{7,8},{8,9},{9,10},{10,1... | collective-permute-start | bytes 1327112 | tf_op jit(solution)/shard_map/ppermute | solution.py:438
  16.3 16.6 %collective-permute-start.3 = (bf16[1,4,16,1536]{3,2,1,0:T(8,128)(2,1)S(1)}, bf16[1,4,16,1536]{3,2,1,0:T(8,128)(2,1)S(1)}, u32[]{:S(2)}, u32[]{:S(2)}) collective-permute-start(bf16[1,4,16,1536]{3,2,1,0:T(8,128)(2,1)S(1)} %get-tuple-element.52), channel_id=1, source_target_pairs={{0,16},{16,32},{32,48},{48,64},{64,80},{80,96},{96,112},{112,0},{1... | collective-permute-start | bytes 589832 | tf_op jit(solution)/shard_map/ppermute | solution.py:438
  20.4 8.3 %collective-permute-start = (bf16[128,1152]{1,0:T(8,128)(2,1)S(1)}, bf16[128,1152]{1,0:T(8,128)(2,1)S(1)}, u32[]{:S(2)}, u32[]{:S(2)}) collective-permute-start(bf16[128,1152]{1,0:T(8,128)(2,1)S(1)} %bitcast.12), channel_id=1, source_target_pairs={{0,16},{16,32},{32,48},{48,64},{64,80},{80,96},{96,112},{112,0},{1... | collective-permute-start | bytes 884744 | tf_op jit(solution)/shard_map/ppermute | solution.py:438
  23.4 9.5 %collective-permute-start.4 = (bf16[1,3,16,1536]{3,2,1,0:T(8,128)(2,1)S(1)}, bf16[1,3,16,1536]{3,2,1,0:T(8,128)(2,1)S(1)}, u32[]{:S(2)}, u32[]{:S(2)}) collective-permute-start(bf16[1,3,16,1536]{3,2,1,0:T(8,128)(2,1)S(1)} %collective-permute-done.2.last_row_target), channel_id=1, source_target_pairs={{0,16},{16,32},{32,48},{48,64},{64,80},{80,96},{96,112},{112,0},{1... | collective-permute-start | bytes 442376 | tf_op jit(solution)/shard_map/ppermute | solution.py:438
  23.5 0.7 %copy-start.1 = (bf16[1024]{0:T(1024)(128)(2,1)S(1)}, bf16[1024]{0:T(1024)(128)(2,1)}, u32[]{:S(2)}) copy-start(bf16[1024]{0:T(1024)(128)(2,1)} %param.11) | copy-start | bytes 6148
  24.2 4.6 %copy-start.2 = (bf16[1024]{0:T(1024)(128)(2,1)S(1)}, bf16[1024]{0:T(1024)(128)(2,1)}, u32[]{:S(2)}) copy-start(bf16[1024]{0:T(1024)(128)(2,1)} %param.11) | copy-start | bytes 6148
  28.7 4.2 %copy-start = (s32[2,2]{1,0:T(2,128)S(1)}, s32[2,2]{1,0:T(2,128)}, u32[]{:S(2)}) copy-start(s32[2,2]{1,0:T(2,128)} %shift_ref.1) | copy-start | bytes 52
  39.7 2.9 %collective-permute-start.6 = (f32[8,128]{1,0:T(8,128)S(1)}, f32[8,128]{1,0:T(8,128)S(1)}, u32[]{:S(2)}, u32[]{:S(2)}) collective-permute-start(f32[8,128]{1,0:T(8,128)S(1)} %get-tuple-element.55), channel_id=1, source_target_pairs={{0,16},{16,0},{1,17},{17,1},{2,18},{18,2},{3,19},{19,3},{4,20},{20... | collective-permute-start | bytes 12296 | tf_op jit(solution)/shard_map/ppermute | solution.py:438
  42.6 6.8 %collective-permute-start.7 = (f32[8,128]{1,0:T(8,128)S(1)}, f32[8,128]{1,0:T(8,128)S(1)}, u32[]{:S(2)}, u32[]{:S(2)}) collective-permute-start(f32[8,128]{1,0:T(8,128)S(1)} %add.72), channel_id=1, source_target_pairs={{0,64},{32,96},{64,0},{96,32},{1,65},{33,97},{65,1},{97,33},{2,66}... | collective-permute-start | bytes 12296 | tf_op jit(solution)/shard_map/ppermute | solution.py:438
  46.2 4.8 %collective-permute-start.8 = (f32[8,128]{1,0:T(8,128)S(1)}, f32[8,128]{1,0:T(8,128)S(1)}, u32[]{:S(2)}, u32[]{:S(2)}) collective-permute-start(f32[8,128]{1,0:T(8,128)S(1)} %add.72), channel_id=1, source_target_pairs={{0,32},{32,64},{64,96},{96,0},{1,33},{33,65},{65,97},{97,1},{2,34}... | collective-permute-start | bytes 12296 | tf_op jit(solution)/shard_map/ppermute | solution.py:438
  46.2 4.8 %collective-permute-start.9 = (f32[8,128]{1,0:T(8,128)S(1)}, f32[8,128]{1,0:T(8,128)S(1)}, u32[]{:S(2)}, u32[]{:S(2)}) collective-permute-start(f32[8,128]{1,0:T(8,128)S(1)} %add.72), channel_id=1, source_target_pairs={{0,96},{32,0},{64,32},{96,64},{1,97},{33,1},{65,33},{97,65},{2,98}... | collective-permute-start | bytes 12296 | tf_op jit(solution)/shard_map/ppermute | solution.py:438
  49.4 3.9 %collective-permute-start.5 = (bf16[128,1024]{1,0:T(8,128)(2,1)S(1)}, bf16[128,1024]{1,0:T(8,128)(2,1)S(1)}, u32[]{:S(2)}, u32[]{:S(2)}) collective-permute-start(bf16[128,1024]{1,0:T(8,128)(2,1)S(1)} %get-tuple-element.54), channel_id=1, source_target_pairs={{0,112},{16,0},{32,16},{48,32},{64,48},{80,64},{96,80},{112,96},{1... | collective-permute-start | bytes 786440 | tf_op jit(solution)/shard_map/ppermute | solution.py:438

commit v5 on v4

--- a/solution.py
+++ b/solution.py
@@ -289,12 +289,21 @@
 
 
 def pack_kernel(
-    place_hbm, shift_hbm, rows_hbm, packed_ref, shift_rows_ref, place_ref, shift_ref, rows_ref, sems
+    place_hbm, shift_hbm, mask_hbm, rows_hbm, pixel_hbm,
+    packed_ref, shift_rows_ref, mask_ref, pixel_ref,
+    place_ref, shift_ref, rows_ref, sems,
 ):
     copies = [
-        pltpu.make_async_copy(rows_hbm, rows_ref, sems.at[0]),
-        pltpu.make_async_copy(place_hbm, place_ref, sems.at[1]),
-        pltpu.make_async_copy(shift_hbm, shift_ref, sems.at[2]),
+        pltpu.make_async_copy(source, target, sems.at[at])
+        for at, (source, target) in enumerate(
+            [
+                (rows_hbm, rows_ref),
+                (place_hbm, place_ref),
+                (shift_hbm, shift_ref),
+                (mask_hbm, mask_ref),
+                (pixel_hbm, pixel_ref),
+            ]
+        )
     ]
     for copy in copies:
         copy.start()
@@ -305,7 +314,7 @@
         places = jnp.zeros((8, 128), jnp.int32)
         for at in range(8):
             source = peer if at < 4 else (peer - 1) % peers
-            places = jnp.where(slot == at, place_ref[source, at % 4], places)
+            places = jnp.where(slot == at, place_ref[at % 4, source], places)
         packed_ref[peer, :, D:] = places.astype(F32).astype(BF)
     copies[2].wait()
     shifts = jnp.zeros((8, 128), jnp.int32)
@@ -316,14 +325,12 @@
     rows = rows_ref[...].astype(F32)
     before = jnp.concatenate([rows[-1:], rows[:-1]], axis=0)
     packed_ref[:, :, :D] = jnp.concatenate([rows, before], axis=1).astype(BF)
-
-
-def target_kernel(pixel_hbm, own_ref, row_ref, last_row_ref, time_ref, pixel_ref, sems):
-    copies = [pltpu.make_async_copy(pixel_hbm.at[at], pixel_ref.at[at], sems.at[at]) for at in range(4)]
-    for frame in (3, 0, 1, 2):
-        copies[frame].start()
-    for frame in (3, 0, 1, 2):
-        copies[frame].wait()
+    copies[3].wait()
+    copies[4].wait()
+
+
+def target_kernel(pixel_ref, own_ref, row_ref, last_row_ref, time_ref):
+    for frame in range(4):
         for row in range(4):
             for part in range(3):
                 cols = slice(part * GROUP, part * GROUP + GROUP)
@@ -379,20 +386,19 @@
 
 
 def pack_part(*operands):
-    outputs = [((16, 8, D + 128), BF), ((8, 128), jnp.int32)]
+    outputs = [((16, 8, D + 128), BF), ((8, 128), jnp.int32), ((8, 128), BF), ((4, 4, 16, PIX), BF)]
     scratch = [
-        pltpu.SMEM((16, 4), jnp.int32),
+        pltpu.SMEM((4, 16), jnp.int32),
         pltpu.SMEM((2, 2), jnp.int32),
         pltpu.VMEM((16, 4, D), BF),
-        pltpu.SemaphoreType.DMA((3,)),
+        pltpu.SemaphoreType.DMA((5,)),
     ]
-    return call(pack_kernel, outputs, scratch, in_space(HBM, 3), 8)(*operands)
+    return call(pack_kernel, outputs, scratch, in_space(HBM, 5), 8)(*operands)
 
 
 def target_part(*operands):
     outputs = [((frames, rows, 16, PIX), BF) for frames, rows in ((4, 4), (3, 3), (1, 3), (1, 4))]
-    scratch = [pltpu.VMEM((4, 4, 16, PIX), BF), pltpu.SemaphoreType.DMA((4,))]
-    return call(target_kernel, outputs, scratch, in_space(HBM, 1), 8)(*operands)
+    return call(target_kernel, outputs, [], in_space(VMEM, 1), 8)(*operands)
 
 
 def early_part(*operands):
@@ -442,12 +448,16 @@
     frame_count, row_count = pixels.shape[:2]
     peers, slots = slot_pos.shape[2:]
     hold = functools.partial(pltpu.with_memory_space_constraint, memory_space=HBM)
-    packed, shift_rows = pack_part(
-        hold(slot_pos.reshape(peers, slots)), hold(window_shift), hold(visible.reshape(peers, slots, D))
+    packed, shift_rows, mask_rows, near_pixels = pack_part(
+        hold(slot_pos.reshape(peers, slots).T),
+        hold(window_shift),
+        hold(mask_token.reshape(8, 128)),
+        hold(visible.reshape(peers, slots, D)),
+        hold(pixels),
     )
     own = lax.all_to_all(packed, ROW, split_axis=0, concat_axis=0, tiled=True).reshape(SLOTS, D + 128)
     behind = move(own, TM, 1)
-    own_target, row_target, last_row_target, time_target = target_part(hold(pixels))
+    own_target, row_target, last_row_target, time_target = target_part(near_pixels)
     last_row_target = move(last_row_target, ROW, 1)
     row_target = move(row_target, ROW, 1)
     time_target = move(time_target, TM, 1)
@@ -462,7 +472,7 @@
     row_table = sinusoid(band.reshape(-1), 384)
     column_table = sinusoid(jnp.arange(16, dtype=jnp.int32), 384)
 
-    tables = (mask_token.reshape(8, 128), frame_table, row_table, column_table)
+    tables = (mask_rows, frame_table, row_table, column_table)
     *half_1, heads_1, w_qkv, w_out, w_head = early_part(
         shift_rows, own, *tables, hold(w_qkv), hold(w_out), hold(w_head)
     )
@@ -477,8 +487,9 @@
     mine = own_picked + from_next
     other = move(local_total, "tm_1", 1)
     local_total = local_total + other
-    turned = [move(local_total, "tm_0", step) for step in (1, 2, 3)]
-    local_total = (local_total + turned[1]) + (turned[0] + turned[2])
+    for bit in (1, 2):
+        pairs = [(at, at ^ bit) for at in range(lax.axis_size("tm_0"))]
+        local_total = local_total + lax.ppermute(local_total, "tm_0", pairs)
     high = local_total.astype(BF)
     low = (local_total - high.astype(F32)).astype(BF)
     sums = jnp.broadcast_to(jnp.concatenate([high, low], axis=1)[None], (peers, 8, 256))

time: 69.5 us -> 66.8 us (0.961); the launches traced: 68.2 us -> 66.2 us
  waiting for transfers between devices: 10.3 us -> 13.8 us
  local copies, waits for them, and re-layouts: 2.98 us -> 0.93 us
  starting transfers between devices: 19.5 us -> 17.8 us
  Pallas kernels: 19.9 us -> 18.9 us
  blocking collectives: 14 us -> 13.3 us
    ppermute x10 -> x7, starting transfers between devices: 12.4 us -> 5.15 us  [move(): lax.ppermute(value, axis, [(at, (at + steps) % count) for at in range(cou...]
    ppermute x0 -> x2, starting transfers between devices: none -> 5.48 us  [per_device(): local_total = local_total + lax.ppermute(local_total, 'tm_0', pairs)]
    ppermute x0 -> x2, waiting for transfers between devices: none -> 3.27 us  [per_device(): local_total = local_total + lax.ppermute(local_total, 'tm_0', pairs)]
    all_to_all x1, waiting for transfers between devices: 2.67 us -> 4.73 us  [per_device(): lax.all_to_all(packed, ROW, split_axis=0, concat_axis=0, tiled=True)]
    ppermute x10 -> x7, waiting for transfers between devices: 7.61 us -> 5.78 us  [move(): lax.ppermute(value, axis, [(at, (at + steps) % count) for at in range(cou...]
    reshape x1 -> x0, local copies, waits for them, and re-layouts: 1.36 us -> none  [per_device(): slot_pos.reshape(peers, slots)]
    pallas_call x2, Pallas kernels: 3.67 us -> 2.76 us  [the longest x1 1.99 us: pack_part(): return call(pack_kernel, outputs, scratch, in_space(HBM, 5), 8)(*operands)]
    all_to_all x1, blocking collectives: 14 us -> 13.3 us  [per_device(): back = lax.all_to_all(sent, ROW, split_axis=0, concat_axis=0, tiled=True)]
  transfers between devices with their start and end apart: 11 -> 10, of which waited for: 5 -> 7; matrix products, arithmetic and copies ran while one was open for 2% -> 2% of each run, Pallas kernels for 16% -> 14%
where the time goes in v5:
time: 66.8 us; the launch traced here: 66.2 us
  Pallas kernels  18.9 us (28%)
  starting transfers between devices  17.8 us (27%)
  waiting for transfers between devices  13.8 us (21%)
  blocking collectives  13.3 us (20%)
  local copies, waits for them, and re-layouts  0.93 us (1%)
  between operations  0.79 us (1%)
  other arithmetic  0.72 us (1%)
    all_to_all x1, blocking collectives, per_device(): back = lax.all_to_all(sent, ROW, split_axis=0, concat_axis=0, tiled=True)  13.3 us
    all_to_all x1, starting transfers between devices, per_device(): lax.all_to_all(packed, ROW, split_axis=0, concat_axis=0, tiled=True)  7.16 us
    pallas_call x1, Pallas kernels, backward_part(): call(backward_kernel, outputs, scratch, in_space(SMEM, 1) + in_space(VMEM...  6.72 us
    ppermute x7, waiting for transfers between devices, move(): lax.ppermute(value, axis, [(at, (at + steps) % count) for at in range(cou...  5.78 us
    ppermute x2, starting transfers between devices, per_device(): local_total = local_total + lax.ppermute(local_total, 'tm_0', pairs)  5.48 us
    ppermute x7, starting transfers between devices, move(): lax.ppermute(value, axis, [(at, (at + steps) % count) for at in range(cou...  5.15 us
    all_to_all x1, waiting for transfers between devices, per_device(): lax.all_to_all(packed, ROW, split_axis=0, concat_axis=0, tiled=True)  4.73 us
    pallas_call x1, Pallas kernels, early_part(): call(early_kernel, outputs, scratch, in_space(VMEM, 6) + in_space(HBM, 3)...  4.54 us
  transfers between devices with their start and end apart: 10, of which 7 were waited for; matrix products, arithmetic and copies ran while one was open for 2% of the time, Pallas kernels for 14%

profile of v5, /device:TPU:0, one launch (start us, length us, event | category | flops | bytes accessed | tf_op | source)
XLA Modules:
  0.0 66.2 jit_solution(17314167472568146495)
XLA Ops:
  0.6 2.0 %shard_map.95 = (bf16[16,8,1152]{2,1,0:T(8,128)(2,1)}, s32[8,128]{1,0:T(8,128)S(1)}, bf16[8,128]{1,0:T(8,128)(2,1)S(1)}, bf16[4,4,16,1536]{3,2,1,0:T(8,128)(2,1)S(1)}) custom-call(s32[4,16]{1,0:T(4,128)} %bitcast.18, s32[2,2]{1,0:T(2,128)} %shift_ref.1, bf16[8,128]{1,0:T(8,128)(2,1)} %bitcast.19, bf16[16,4,1024]{2,1,0:T(4,128)(2,1)} %bitcast.17, ...), custom_call_target="tpu_custom_call" | custom-call | tf_op jit(solution)/shard_map/pallas_call | solution.py:396
  2.6 7.2 %all-to-all-start = ((bf16[16,8,1152]{2,1,0:T(8,128)(2,1)}), bf16[16,8,1152]{2,1,0:T(8,128)(2,1)S(1)}, u32[]{:S(2)}, u32[]{:S(2)}) async-start(bf16[16,8,1152]{2,1,0:T(8,128)(2,1)} %get-tuple-element.33), calls=%async_computation | async-start | bytes 589824 | tf_op jit(solution)/shard_map/all_to_all | solution.py:458
  9.8 0.8 %shard_map.98 = (bf16[4,4,16,1536]{3,2,1,0:T(8,128)(2,1)S(1)}, bf16[3,3,16,1536]{3,2,1,0:T(8,128)(2,1)S(1)}, bf16[1,3,16,1536]{3,2,1,0:T(8,128)(2,1)S(1)}, bf16[1,4,16,1536]{3,2,1,0:T(8,128)(2,1)S(1)}) custom-call(bf16[4,4,16,1536]{3,2,1,0:T(8,128)(2,1)S(1)} %get-tuple-element.52.pixel_ref), custom_call_target="tpu_custom_call" | custom-call | tf_op jit(solution)/shard_map/pallas_call | solution.py:401
  10.6 2.0 %collective-permute-start.2 = (bf16[1,3,16,1536]{3,2,1,0:T(8,128)(2,1)S(1)}, bf16[1,3,16,1536]{3,2,1,0:T(8,128)(2,1)S(1)}, u32[]{:S(2)}, u32[]{:S(2)}) collective-permute-start(bf16[1,3,16,1536]{3,2,1,0:T(8,128)(2,1)S(1)} %get-tuple-element.55), channel_id=1, source_target_pairs={{0,1},{1,2},{2,3},{3,4},{4,5},{5,6},{6,7},{7,8},{8,9},{9,10},{10,1... | collective-permute-start | bytes 442376 | tf_op jit(solution)/shard_map/ppermute | solution.py:444
  12.6 1.5 %collective-permute-start.1 = (bf16[3,3,16,1536]{3,2,1,0:T(8,128)(2,1)S(1)}, bf16[3,3,16,1536]{3,2,1,0:T(8,128)(2,1)S(1)}, u32[]{:S(2)}, u32[]{:S(2)}) collective-permute-start(bf16[3,3,16,1536]{3,2,1,0:T(8,128)(2,1)S(1)} %get-tuple-element.54), channel_id=1, source_target_pairs={{0,1},{1,2},{2,3},{3,4},{4,5},{5,6},{6,7},{7,8},{8,9},{9,10},{10,1... | collective-permute-start | bytes 1327112 | tf_op jit(solution)/shard_map/ppermute | solution.py:444
  14.0 0.8 %slice_bitcast_fusion = (s32[2]{0:T(128)S(1)}, s32[2]{0:T(128)S(1)}) fusion(s32[2,2]{1,0:T(2,128)} %shift_ref.1), kind=kLoop, calls=%fused_computation.26 | loop fusion | bytes 32 | tf_op jit(solution)/shard_map/sub | solution.py:470
  14.8 0.1 broadcast_subtract_fusion
  14.9 0.1 sub.58
  15.0 0.1 sub.53
  15.1 0.1 multiply_sine_fusion.1
  15.2 0.1 multiply_sine_fusion
  15.4 0.1 multiply_sine_fusion.2
  15.5 4.7 %all-to-all-done = bf16[16,8,1152]{2,1,0:T(8,128)(2,1)S(1)} async-done(((bf16[16,8,1152]{2,1,0:T(8,128)(2,1)}), bf16[16,8,1152]{2,1,0:T(8,128)(2,1)S(1)}, u32[]{:S(2)}, u32[]{:S(2)}) %all-to-all-start) | async-done | bytes 294944 | tf_op jit(solution)/shard_map/all_to_all | solution.py:458
  20.2 0.0 collective-permute-start
  20.2 0.1 pad_maximum_fusion.2.rows_ref
  20.3 2.2 %collective-permute-done.2.last_row_target = bf16[1,3,16,1536]{3,2,1,0:T(8,128)(2,1)S(1)} collective-permute-done((bf16[1,3,16,1536]{3,2,1,0:T(8,128)(2,1)S(1)}, bf16[1,3,16,1536]{3,2,1,0:T(8,128)(2,1)S(1)}, u32[]{:S(2)}, u32[]{:S(2)}) %collective-permute-start.2) | collective-permute-done | bytes 147488 | tf_op jit(solution)/shard_map/ppermute | solution.py:444
  22.5 0.1 pad_maximum_fusion.1.columns_ref
  22.6 4.5 %shard_map.96 = (bf16[128,1024]{1,0:T(8,128)(2,1)S(1)}, bf16[128,3072]{1,0:T(8,128)(2,1)S(1)}, bf16[2,8,64,128]{3,2,1,0:T(8,128)(2,1)S(1)}, f32[128,128]{1,0:T(8...) custom-call(s32[8,128]{1,0:T(8,128)S(1)} %get-tuple-element.32.shift, ...), custom_call_target="tpu_custom_call" | custom-call | tf_op jit(solution)/shard_map/pallas_call | solution.py:407
  27.1 0.5 collective-permute-done.behind_ref
  27.6 4.2 %shard_map.97 = (bf16[128,1024]{1,0:T(8,128)(2,1)S(1)}, bf16[128,3072]{1,0:T(8,128)(2,1)S(1)}, bf16[2,8,64,128]{3,2,1,0:T(8,128)(2,1)S(1)}, f32[128,128]{1,0:T(8...) custom-call(s32[8,128]{1,0:T(8,128)S(1)} %get-tuple-element.32.shift, ...), custom_call_target="tpu_custom_call" | custom-call | tf_op jit(solution)/shard_map/pallas_call | solution.py:419
  31.8 0.0 collective-permute-done.3.time_target
  31.8 0.0 collective-permute-done.1.row_target
  31.8 6.7 %shard_map.99 = (bf16[128,1024]{1,0:T(8,128)(2,1)S(1)}, bf16[128,1024]{1,0:T(8,128)(2,1)S(1)}, f32[8,128]{1,0:T(8,128)S(1)}) custom-call(s32[2,2]{1,0:T(2,128)S(1)} %copy-done, bf16[128,1024]{1,0:T(8,128)(2,1)S(1)} %get-tuple-element.40.embedded_0_ref, bf16[128,3072]{1,0:T(8,128)(2,1)S(1)} %get-tuple-element.41.qkv_0_ref, ...), custom_call_target="tpu_custom_call" | custom-call | tf_op jit(solution)/shard_map/pallas_call | solution.py:432
  38.5 1.7 %collective-permute-start.6 = (f32[8,128]{1,0:T(8,128)S(1)}, f32[8,128]{1,0:T(8,128)S(1)}, u32[]{:S(2)}, u32[]{:S(2)}) collective-permute-start(f32[8,128]{1,0:T(8,128)S(1)} %get-tuple-element.59), channel_id=1, source_target_pairs={{0,16},{16,0},{1,17},{17,1},{2,18},{18,2},{3,19},{19,3},{4,20},{20... | collective-permute-start | bytes 12296 | tf_op jit(solution)/shard_map/ppermute | solution.py:444
  40.2 0.8 %collective-permute-done.6 = f32[8,128]{1,0:T(8,128)S(1)} collective-permute-done((f32[8,128]{1,0:T(8,128)S(1)}, f32[8,128]{1,0:T(8,128)S(1)}, u32[]{:S(2)}, u32[]{:S(2)}) %collective-permute-start.6) | collective-permute-done | bytes 4128 | tf_op jit(solution)/shard_map/ppermute | solution.py:444
  41.0 1.9 %collective-permute-start.7 = (f32[8,128]{1,0:T(8,128)S(1)}, f32[8,128]{1,0:T(8,128)S(1)}, u32[]{:S(2)}, u32[]{:S(2)}) collective-permute-start(f32[8,128]{1,0:T(8,128)S(1)} %add.69), channel_id=1, source_target_pairs={{0,32},{32,0},{64,96},{96,64},{1,33},{33,1},{65,97},{97,65},{2,34}... | collective-permute-start | bytes 12296 | tf_op jit(solution)/shard_map/ppermute | solution.py:492
  43.0 1.7 %collective-permute-done.7 = f32[8,128]{1,0:T(8,128)S(1)} collective-permute-done((f32[8,128]{1,0:T(8,128)S(1)}, f32[8,128]{1,0:T(8,128)S(1)}, u32[]{:S(2)}, u32[]{:S(2)}) %collective-permute-start.7) | collective-permute-done | bytes 4128 | tf_op jit(solution)/shard_map/ppermute | solution.py:492
  44.7 3.6 %collective-permute-start.8 = (f32[8,128]{1,0:T(8,128)S(1)}, f32[8,128]{1,0:T(8,128)S(1)}, u32[]{:S(2)}, u32[]{:S(2)}) collective-permute-start(f32[8,128]{1,0:T(8,128)S(1)} %add.70), channel_id=1, source_target_pairs={{0,64},{32,96},{64,0},{96,32},{1,65},{33,97},{65,1},{97,33},{2,66}... | collective-permute-start | bytes 12296 | tf_op jit(solution)/shard_map/ppermute | solution.py:492
  48.2 1.6 %collective-permute-done.8 = f32[8,128]{1,0:T(8,128)S(1)} collective-permute-done((f32[8,128]{1,0:T(8,128)S(1)}, f32[8,128]{1,0:T(8,128)S(1)}, u32[]{:S(2)}, u32[]{:S(2)}) %collective-permute-start.8) | collective-permute-done | bytes 4128 | tf_op jit(solution)/shard_map/ppermute | solution.py:492
  49.8 2.3 %collective-permute-done.5 = bf16[128,1024]{1,0:T(8,128)(2,1)S(1)} collective-permute-done((bf16[128,1024]{1,0:T(8,128)(2,1)S(1)}, bf16[128,1024]{1,0:T(8,128)(2,1)S(1)}, u32[]{:S(2)}, u32[]{:S(2)}) %collective-permute-start.5) | collective-permute-done | bytes 262176 | tf_op jit(solution)/shard_map/ppermute | solution.py:444
  52.2 13.3 %all_to_all.10.back_ref = bf16[16,8,1280]{2,1,0:T(8,128)(2,1)S(1)} all-to-all(bf16[16,8,1280]{2,1,0:T(8,128)(2,1)S(1)} %pad_maximum_fusion), channel_id=1, replica_groups=mesh['tm_0'=4,'tm_1'=2,'row_0'=4,'row_1'=4] {'row_0','row_1'}, dimensions={0} | all-to-all | bytes 655360 | tf_op jit(solution)/shard_map/all_to_all | solution.py:497
  65.5 0.8 %shard_map.100 = (bf16[16,4,1024]{2,1,0:T(4,128)(2,1)}, f32[8,128]{1,0:T(8,128)}) custom-call(bf16[16,8,1280]{2,1,0:T(8,128)(2,1)S(1)} %all_to_all.10.back_ref), custom_call_target="tpu_custom_call" | custom-call | tf_op jit(solution)/shard_map/pallas_call | solution.py:501
  (21 shorter events, 0.1 us)
Async XLA Ops:
  2.6 17.6 %all-to-all-start = ((bf16[16,8,1152]{2,1,0:T(8,128)(2,1)}), bf16[16,8,1152]{2,1,0:T(8,128)(2,1)S(1)}, u32[]{:S(2)}, u32[]{:S(2)}) async-start(bf16[16,8,1152]{2,1,0:T(8,128)(2,1)} %get-tuple-element.33), calls=%async_computation | async-start | bytes 589824 | tf_op jit(solution)/shard_map/all_to_all | solution.py:458
  10.6 11.9 %collective-permute-start.2 = (bf16[1,3,16,1536]{3,2,1,0:T(8,128)(2,1)S(1)}, bf16[1,3,16,1536]{3,2,1,0:T(8,128)(2,1)S(1)}, u32[]{:S(2)}, u32[]{:S(2)}) collective-permute-start(bf16[1,3,16,1536]{3,2,1,0:T(8,128)(2,1)S(1)} %get-tuple-element.55), channel_id=1, source_target_pairs={{0,1},{1,2},{2,3},{3,4},{4,5},{5,6},{6,7},{7,8},{8,9},{9,10},{10,1... | collective-permute-start | bytes 442376 | tf_op jit(solution)/shard_map/ppermute | solution.py:444
  12.6 19.2 %collective-permute-start.1 = (bf16[3,3,16,1536]{3,2,1,0:T(8,128)(2,1)S(1)}, bf16[3,3,16,1536]{3,2,1,0:T(8,128)(2,1)S(1)}, u32[]{:S(2)}, u32[]{:S(2)}) collective-permute-start(bf16[3,3,16,1536]{3,2,1,0:T(8,128)(2,1)S(1)} %get-tuple-element.54), channel_id=1, source_target_pairs={{0,1},{1,2},{2,3},{3,4},{4,5},{5,6},{6,7},{7,8},{8,9},{9,10},{10,1... | collective-permute-start | bytes 1327112 | tf_op jit(solution)/shard_map/ppermute | solution.py:444
  14.0 17.7 %collective-permute-start.3 = (bf16[1,4,16,1536]{3,2,1,0:T(8,128)(2,1)S(1)}, bf16[1,4,16,1536]{3,2,1,0:T(8,128)(2,1)S(1)}, u32[]{:S(2)}, u32[]{:S(2)}) collective-permute-start(bf16[1,4,16,1536]{3,2,1,0:T(8,128)(2,1)S(1)} %get-tuple-element.56), channel_id=1, source_target_pairs={{0,16},{16,32},{32,48},{48,64},{64,80},{80,96},{96,112},{112,0},{1... | collective-permute-start | bytes 589832 | tf_op jit(solution)/shard_map/ppermute | solution.py:444
  20.2 7.4 %collective-permute-start = (bf16[128,1152]{1,0:T(8,128)(2,1)S(1)}, bf16[128,1152]{1,0:T(8,128)(2,1)S(1)}, u32[]{:S(2)}, u32[]{:S(2)}) collective-permute-start(bf16[128,1152]{1,0:T(8,128)(2,1)S(1)} %bitcast.14), channel_id=1, source_target_pairs={{0,16},{16,32},{32,48},{48,64},{64,80},{80,96},{96,112},{112,0},{1... | collective-permute-start | bytes 884744 | tf_op jit(solution)/shard_map/ppermute | solution.py:444
  22.5 9.3 %collective-permute-start.4 = (bf16[1,3,16,1536]{3,2,1,0:T(8,128)(2,1)S(1)}, bf16[1,3,16,1536]{3,2,1,0:T(8,128)(2,1)S(1)}, u32[]{:S(2)}, u32[]{:S(2)}) collective-permute-start(bf16[1,3,16,1536]{3,2,1,0:T(8,128)(2,1)S(1)} %collective-permute-done.2.last_row_target), channel_id=1, source_target_pairs={{0,16},{16,32},{32,48},{48,64},{64,80},{80,96},{96,112},{112,0},{1... | collective-permute-start | bytes 442376 | tf_op jit(solution)/shard_map/ppermute | solution.py:444
  27.6 4.2 %copy-start = (s32[2,2]{1,0:T(2,128)S(1)}, s32[2,2]{1,0:T(2,128)}, u32[]{:S(2)}) copy-start(s32[2,2]{1,0:T(2,128)} %shift_ref.1) | copy-start | bytes 52
  38.5 2.5 %collective-permute-start.6 = (f32[8,128]{1,0:T(8,128)S(1)}, f32[8,128]{1,0:T(8,128)S(1)}, u32[]{:S(2)}, u32[]{:S(2)}) collective-permute-start(f32[8,128]{1,0:T(8,128)S(1)} %get-tuple-element.59), channel_id=1, source_target_pairs={{0,16},{16,0},{1,17},{17,1},{2,18},{18,2},{3,19},{19,3},{4,20},{20... | collective-permute-start | bytes 12296 | tf_op jit(solution)/shard_map/ppermute | solution.py:444
  41.0 3.6 %collective-permute-start.7 = (f32[8,128]{1,0:T(8,128)S(1)}, f32[8,128]{1,0:T(8,128)S(1)}, u32[]{:S(2)}, u32[]{:S(2)}) collective-permute-start(f32[8,128]{1,0:T(8,128)S(1)} %add.69), channel_id=1, source_target_pairs={{0,32},{32,0},{64,96},{96,64},{1,33},{33,1},{65,97},{97,65},{2,34}... | collective-permute-start | bytes 12296 | tf_op jit(solution)/shard_map/ppermute | solution.py:492
  44.7 5.2 %collective-permute-start.8 = (f32[8,128]{1,0:T(8,128)S(1)}, f32[8,128]{1,0:T(8,128)S(1)}, u32[]{:S(2)}, u32[]{:S(2)}) collective-permute-start(f32[8,128]{1,0:T(8,128)S(1)} %add.70), channel_id=1, source_target_pairs={{0,64},{32,96},{64,0},{96,32},{1,65},{33,97},{65,1},{97,33},{2,66}... | collective-permute-start | bytes 12296 | tf_op jit(solution)/shard_map/ppermute | solution.py:492
  48.2 3.9 %collective-permute-start.5 = (bf16[128,1024]{1,0:T(8,128)(2,1)S(1)}, bf16[128,1024]{1,0:T(8,128)(2,1)S(1)}, u32[]{:S(2)}, u32[]{:S(2)}) collective-permute-start(bf16[128,1024]{1,0:T(8,128)(2,1)S(1)} %get-tuple-element.58), channel_id=1, source_target_pairs={{0,112},{16,0},{32,16},{48,32},{64,48},{80,64},{96,80},{112,96},{1... | collective-permute-start | bytes 786440 | tf_op jit(solution)/shard_map/ppermute | solution.py:444

commit v6 on v5

--- a/solution.py
+++ b/solution.py
@@ -193,7 +193,7 @@
     embedded_1_ref, qkv_1_ref, probs_1_ref, seen_1_ref, one_hot_1_ref,
     normed_ref, scale_ref, predicted_ref, w_qkv_ref, w_out_ref, w_head_ref,
     own_target, row_target, last_row_target, time_target, corner_target,
-    own_picked_ref, behind_picked_ref, total_ref,
+    own_picked_ref, behind_rows_ref, total_ref,
     target_ref, error_ref, narrow_ref, wide_ref, stream_ref, dqkv_ref,
 ):
     embedded_refs = (embedded_0_ref, embedded_1_ref)
@@ -283,9 +283,35 @@
         total = total + part[:8] + part[8:]
     total = jnp.sum(total, axis=0, keepdims=True)
     total_ref[...] = jnp.concatenate([total[:, at * 128 : at * 128 + 128] for at in range(8)], axis=0)
-    behind_picked_ref[...] = dot(one_hot_0_ref[SLOTS:], narrow_ref[:HALF], NN_DIMS).astype(BF)
+    behind_rows_ref[...] = jnp.where(
+        shift_ref[0, 1] == 1, narrow_ref[WIN : WIN + 32].astype(F32), narrow_ref[:32].astype(F32)
+    ).astype(BF)
     own_picked = dot(one_hot_0_ref[:SLOTS], narrow_ref[:HALF], NN_DIMS)
     own_picked_ref[...] = (own_picked + dot(one_hot_1_ref[...], narrow_ref[HALF:], NN_DIMS)).astype(BF)
+
+
+def give_kernel(
+    shift_ref, own_ref, picked_ref, next_ref, total_ref, turned_1_ref, turned_2_ref, turned_3_ref, sent_ref
+):
+    place = own_ref[:, D : D + 128].astype(F32).astype(jnp.int32)
+    row = (place >> 4) & 3
+    column = place & 15
+    slot = lax.broadcasted_iota(jnp.int32, (SLOTS, 128), 0) & 7
+    lane = lax.broadcasted_iota(jnp.int32, (SLOTS, 128), 1)
+    late = jnp.where(column < 8, shift_ref[0:1], shift_ref[1:2])
+    row = row + jnp.where(column < 8, shift_ref[2:3], shift_ref[3:4]) - jnp.where(slot >= 4, 4, 0)
+    inside = (place >= 192) & (late == 1) & (row >= 0) & (row < 4)
+    token = jnp.where(inside, row * 8 + (column & 7), -1)
+    one_hot = jnp.where(token == lane, 1.0, 0.0).astype(BF)
+    rows = jnp.concatenate([next_ref[...], jnp.zeros((SLOTS - 32, D), BF)], axis=0)
+    picked = picked_ref[...].astype(F32) + dot(one_hot, rows, NN_DIMS)
+    sent_ref[:, :, :D] = picked.reshape(16, 8, D).astype(BF)
+    total = (total_ref[...] + turned_2_ref[...]) + (turned_1_ref[...] + turned_3_ref[...])
+    high = total.astype(BF)
+    low = (total - high.astype(F32)).astype(BF)
+    for peer in range(16):
+        sent_ref[peer, :, D : D + 128] = high
+        sent_ref[peer, :, D + 128 :] = low
 
 
 def pack_kernel(
@@ -329,7 +355,30 @@
     copies[4].wait()
 
 
-def target_kernel(pixel_ref, own_ref, row_ref, last_row_ref, time_ref):
+def sinusoid(coordinate, channel_count):
+    half_count = channel_count // 2
+    lane = lax.broadcasted_iota(jnp.int32, (coordinate.shape[0], channel_count), 1)
+    channel = jnp.where(lane < half_count, lane, lane - half_count).astype(F32)
+    angles = coordinate.astype(F32) * jnp.exp(-math.log(10000.0) * channel / half_count)
+    return jnp.where(lane < half_count, jnp.sin(angles), jnp.cos(angles))
+
+
+def grid_coordinates(start, offsets_ref, first, total, channel_count):
+    row = lax.broadcasted_iota(jnp.int32, (8, 128), 0)
+    offset = jnp.where(row < 4, offsets_ref[first : first + 1], offsets_ref[first + 1 : first + 2])
+    coordinate = start + (row & 3) - offset
+    coordinate = jnp.where(coordinate < 0, coordinate + total, coordinate)
+    return jnp.concatenate([coordinate] * (channel_count // 128), axis=1)
+
+
+def target_kernel(
+    totals, shift_rows_ref, pixel_ref, own_ref, row_ref, last_row_ref, time_ref, frames_ref, rows_ref, columns_ref
+):
+    frames = grid_coordinates(lax.axis_index(TM) * 4, shift_rows_ref, 0, totals[0], 256)
+    rows = grid_coordinates(lax.axis_index(ROW) * 4, shift_rows_ref, 2, totals[1], 384)
+    frames_ref[...] = sinusoid(frames, 256)
+    rows_ref[...] = sinusoid(rows, 384)
+    columns_ref[...] = sinusoid(lax.broadcasted_iota(jnp.int32, (16, 384), 0), 384)
     for frame in range(4):
         for row in range(4):
             for part in range(3):
@@ -396,9 +445,11 @@
     return call(pack_kernel, outputs, scratch, in_space(HBM, 5), 8)(*operands)
 
 
-def target_part(*operands):
+def target_part(totals, *operands):
     outputs = [((frames, rows, 16, PIX), BF) for frames, rows in ((4, 4), (3, 3), (1, 3), (1, 4))]
-    return call(target_kernel, outputs, [], in_space(VMEM, 1), 8)(*operands)
+    outputs += [((8, 256), F32), ((8, 384), F32), ((16, 384), F32)]
+    kernel = functools.partial(target_kernel, totals)
+    return call(kernel, outputs, [], in_space(VMEM, 2), 8)(*operands)
 
 
 def early_part(*operands):
@@ -420,7 +471,7 @@
 
 
 def backward_part(*operands):
-    outputs = [((SLOTS, D), BF), ((SLOTS, D), BF), ((8, 128), F32)]
+    outputs = [((SLOTS, D), BF), ((32, D), BF), ((8, 128), F32)]
     scratch = [
         pltpu.VMEM((5, 7, 16, PIX), BF),
         pltpu.VMEM((TOK, PIX), BF),
@@ -430,13 +481,6 @@
         pltpu.VMEM((TOK, 3 * D), BF),
     ]
     return call(backward_kernel, outputs, scratch, in_space(SMEM, 1) + in_space(VMEM, 21), 34)(*operands)
-
-
-def sinusoid(coordinate, channel_count):
-    half_count = channel_count // 2
-    frequency = jnp.exp(-math.log(10000.0) * jnp.arange(half_count, dtype=F32) / half_count)
-    angles = coordinate.astype(F32)[..., None] * frequency
-    return jnp.concatenate([jnp.sin(angles), jnp.cos(angles)], axis=-1)
 
 
 def move(value, axis, steps):
@@ -457,43 +501,33 @@
     )
     own = lax.all_to_all(packed, ROW, split_axis=0, concat_axis=0, tiled=True).reshape(SLOTS, D + 128)
     behind = move(own, TM, 1)
-    own_target, row_target, last_row_target, time_target = target_part(near_pixels)
+    frame_total = frame_count * lax.axis_size(TM)
+    row_total = row_count * lax.axis_size(ROW)
+    own_target, row_target, last_row_target, time_target, *positions = target_part(
+        (frame_total, row_total), shift_rows, near_pixels
+    )
     last_row_target = move(last_row_target, ROW, 1)
     row_target = move(row_target, ROW, 1)
     time_target = move(time_target, TM, 1)
     corner_target = move(last_row_target, TM, 1)
 
-    local = jnp.arange(4, dtype=jnp.int32)
-    frame_total = frame_count * lax.axis_size(TM)
-    row_total = row_count * lax.axis_size(ROW)
-    frames = (lax.axis_index(TM) * frame_count + local[None] - window_shift[0][:, None]) % frame_total
-    band = (lax.axis_index(ROW) * row_count + local[None] - window_shift[1][:, None]) % row_total
-    frame_table = sinusoid(frames.reshape(-1), 256)
-    row_table = sinusoid(band.reshape(-1), 384)
-    column_table = sinusoid(jnp.arange(16, dtype=jnp.int32), 384)
-
-    tables = (mask_rows, frame_table, row_table, column_table)
+    tables = (mask_rows, *positions)
     *half_1, heads_1, w_qkv, w_out, w_head = early_part(
         shift_rows, own, *tables, hold(w_qkv), hold(w_out), hold(w_head)
     )
     *half_0, head_normed, head_scale, predicted = late_part(
         shift_rows, own, behind, *tables, half_1[0], heads_1, w_qkv, w_out, w_head
     )
-    own_picked, behind_picked, local_total = backward_part(
+    own_picked, behind_rows, local_total = backward_part(
         window_shift, *half_0, *half_1, head_normed, head_scale, predicted, w_qkv, w_out, w_head,
         own_target, row_target, last_row_target, time_target, corner_target,
     )
-    from_next = move(behind_picked, TM, -1)
-    mine = own_picked + from_next
     other = move(local_total, "tm_1", 1)
+    from_next = move(behind_rows, TM, -1)
     local_total = local_total + other
-    for bit in (1, 2):
-        pairs = [(at, at ^ bit) for at in range(lax.axis_size("tm_0"))]
-        local_total = local_total + lax.ppermute(local_total, "tm_0", pairs)
-    high = local_total.astype(BF)
-    low = (local_total - high.astype(F32)).astype(BF)
-    sums = jnp.broadcast_to(jnp.concatenate([high, low], axis=1)[None], (peers, 8, 256))
-    sent = jnp.concatenate([mine.reshape(peers, 2 * slots, D), sums], axis=-1)
+    turned = [move(local_total, "tm_0", step) for step in (1, 2, 3)]
+    give = call(give_kernel, [((peers, 8, D + 256), BF)], [], in_space(VMEM, 8), 8)
+    (sent,) = give(shift_rows, own, own_picked, from_next, local_total, *turned)
     back = lax.all_to_all(sent, ROW, split_axis=0, concat_axis=0, tiled=True)
     grad_scale = (frame_total * row_total * pixels.shape[2]) ** (-0.5)
     outputs = [((peers, slots, D), BF), ((8, 128), F32)]

time: 66.8 us -> 71.6 us (1.072)
  waiting for transfers between devices: 13.8 us -> 20 us
  starting transfers between devices: 17.8 us -> 19.6 us
  blocking collectives: 13.3 us -> 11.6 us
  local copies, waits for them, and re-layouts: 0.93 us -> 0.01 us
    ppermute x7 -> x10, starting transfers between devices: 5.15 us -> 12.5 us  [move(): lax.ppermute(value, axis, [(at, (at + steps) % count) for at in range(cou...]
    ppermute x7 -> x10, waiting for transfers between devices: 5.78 us -> 12.5 us  [move(): lax.ppermute(value, axis, [(at, (at + steps) % count) for at in range(cou...]
    ppermute x2 -> x0, starting transfers between devices: 5.48 us -> none  [per_device(): local_total = local_total + lax.ppermute(local_total, 'tm_0', pairs)]
    ppermute x2 -> x0, waiting for transfers between devices: 3.27 us -> none  [per_device(): local_total = local_total + lax.ppermute(local_total, 'tm_0', pairs)]
    all_to_all x1, waiting for transfers between devices: 4.73 us -> 7.52 us  [per_device(): lax.all_to_all(packed, ROW, split_axis=0, concat_axis=0, tiled=True)]
    all_to_all x1, blocking collectives: 13.3 us -> 11.6 us  [per_device(): back = lax.all_to_all(sent, ROW, split_axis=0, concat_axis=0, tiled=True)]
    sub x3 -> x0, local copies, waits for them, and re-layouts: 0.92 us -> none  [the longest x2 0.84 us: per_device(): lax.axis_index(ROW) * row_count + local[None] - window_shift[1][:, None]]
  transfers between devices with their start and end apart: 10 -> 11, of which waited for: 7 -> 5; matrix products, arithmetic and copies ran while one was open for 2% -> 0% of each run, Pallas kernels for 14% -> 13%
where the time goes in v6:
time: 71.6 us; the launch traced here: 71.3 us
  waiting for transfers between devices  20 us (28%)
  starting transfers between devices  19.6 us (27%)
  Pallas kernels  19.3 us (27%)
  blocking collectives  11.6 us (16%)
  between operations  0.74 us (1%)
    ppermute x10, waiting for transfers between devices, move(): lax.ppermute(value, axis, [(at, (at + steps) % count) for at in range(cou...  12.5 us
    ppermute x10, starting transfers between devices, move(): lax.ppermute(value, axis, [(at, (at + steps) % count) for at in range(cou...  12.5 us
    all_to_all x1, blocking collectives, per_device(): back = lax.all_to_all(sent, ROW, split_axis=0, concat_axis=0, tiled=True)  11.6 us
    all_to_all x1, waiting for transfers between devices, per_device(): lax.all_to_all(packed, ROW, split_axis=0, concat_axis=0, tiled=True)  7.52 us
    all_to_all x1, starting transfers between devices, per_device(): lax.all_to_all(packed, ROW, split_axis=0, concat_axis=0, tiled=True)  7.16 us
    pallas_call x1, Pallas kernels, backward_part(): call(backward_kernel, outputs, scratch, in_space(SMEM, 1) + in_space(VMEM...  6.68 us
    pallas_call x1, Pallas kernels, early_part(): call(early_kernel, outputs, scratch, in_space(VMEM, 6) + in_space(HBM, 3)...  4.54 us
    pallas_call x1, Pallas kernels, late_part(): call(late_kernel, outputs, scratch, in_space(VMEM, 12), 26)(*operands)  4.17 us
  transfers between devices with their start and end apart: 11, of which 5 were waited for; matrix products, arithmetic and copies ran while one was open for 0% of the time, Pallas kernels for 13%

profile of v6, /device:TPU:0, one launch (start us, length us, event | category | flops | bytes accessed | tf_op | source)
XLA Modules:
  0.0 71.3 jit_solution(16128356857819320049)
XLA Ops:
  0.6 2.0 %shard_map.95 = (bf16[16,8,1152]{2,1,0:T(8,128)(2,1)}, s32[8,128]{1,0:T(8,128)S(1)}, bf16[8,128]{1,0:T(8,128)(2,1)S(1)}, bf16[4,4,16,1536]{3,2,1,0:T(8,128)(2,1)S(1)}) custom-call(s32[4,16]{1,0:T(4,128)} %bitcast.13, s32[2,2]{1,0:T(2,128)} %shift_ref.1, bf16[8,128]{1,0:T(8,128)(2,1)} %bitcast.14, bf16[16,4,1024]{2,1,0:T(4,128)(2,1)} %bitcast.12, ...), custom_call_target="tpu_custom_call" | custom-call | tf_op jit(solution)/shard_map/pallas_call | solution.py:445
  2.6 7.2 %all-to-all-start = ((bf16[16,8,1152]{2,1,0:T(8,128)(2,1)}), bf16[16,8,1152]{2,1,0:T(8,128)(2,1)S(1)}, u32[]{:S(2)}, u32[]{:S(2)}) async-start(bf16[16,8,1152]{2,1,0:T(8,128)(2,1)} %get-tuple-element.36), calls=%async_computation | async-start | bytes 589824 | tf_op jit(solution)/shard_map/all_to_all | solution.py:502
  9.8 0.9 %shard_map.96 = (bf16[4,4,16,1536]{3,2,1,0:T(8,128)(2,1)S(1)}, bf16[3,3,16,1536]{3,2,1,0:T(8,128)(2,1)S(1)}, bf16[1,3,16,1536]{3,2,1,0:T(8,128)(2,1)S(1)}, bf16[...) custom-call(s32[8,128]{1,0:T(8,128)S(1)} %get-tuple-element.35.shift_rows_, ...), custom_call_target="tpu_custom_call" | custom-call | tf_op jit(solution)/shard_map/pallas_call | solution.py:452
  10.7 2.0 %collective-permute-start.1 = (bf16[3,3,16,1536]{3,2,1,0:T(8,128)(2,1)S(1)}, bf16[3,3,16,1536]{3,2,1,0:T(8,128)(2,1)S(1)}, u32[]{:S(2)}, u32[]{:S(2)}) collective-permute-start(bf16[3,3,16,1536]{3,2,1,0:T(8,128)(2,1)S(1)} %get-tuple-element.60), channel_id=1, source_target_pairs={{0,1},{1,2},{2,3},{3,4},{4,5},{5,6},{6,7},{7,8},{8,9},{9,10},{10,1... | collective-permute-start | bytes 1327112 | tf_op jit(solution)/shard_map/ppermute | solution.py:488
  12.7 7.5 %all-to-all-done = bf16[16,8,1152]{2,1,0:T(8,128)(2,1)S(1)} async-done(((bf16[16,8,1152]{2,1,0:T(8,128)(2,1)}), bf16[16,8,1152]{2,1,0:T(8,128)(2,1)S(1)}, u32[]{:S(2)}, u32[]{:S(2)}) %all-to-all-start) | async-done | bytes 294944 | tf_op jit(solution)/shard_map/all_to_all | solution.py:502
  20.2 0.0 collective-permute-start
  20.2 0.0 collective-permute-start.2
  20.2 2.0 %collective-permute-start.3 = (bf16[1,4,16,1536]{3,2,1,0:T(8,128)(2,1)S(1)}, bf16[1,4,16,1536]{3,2,1,0:T(8,128)(2,1)S(1)}, u32[]{:S(2)}, u32[]{:S(2)}) collective-permute-start(bf16[1,4,16,1536]{3,2,1,0:T(8,128)(2,1)S(1)} %get-tuple-element.62), channel_id=1, source_target_pairs={{0,16},{16,32},{32,48},{48,64},{64,80},{80,96},{96,112},{112,0},{1... | collective-permute-start | bytes 589832 | tf_op jit(solution)/shard_map/ppermute | solution.py:488
  22.3 8.7 %collective-permute-done.2.last_row_target = bf16[1,3,16,1536]{3,2,1,0:T(8,128)(2,1)S(1)} collective-permute-done((bf16[1,3,16,1536]{3,2,1,0:T(8,128)(2,1)S(1)}, bf16[1,3,16,1536]{3,2,1,0:T(8,128)(2,1)S(1)}, u32[]{:S(2)}, u32[]{:S(2)}) %collective-permute-start.2) | collective-permute-done | bytes 147488 | tf_op jit(solution)/shard_map/ppermute | solution.py:488
  31.0 0.1 collective-permute-start.4
  31.1 4.5 %shard_map.97 = (bf16[128,1024]{1,0:T(8,128)(2,1)S(1)}, bf16[128,3072]{1,0:T(8,128)(2,1)S(1)}, bf16[2,8,64,128]{3,2,1,0:T(8,128)(2,1)S(1)}, f32[128,128]{1,0:T(8...) custom-call(s32[8,128]{1,0:T(8,128)S(1)} %get-tuple-element.35.shift, ...), custom_call_target="tpu_custom_call" | custom-call | tf_op jit(solution)/shard_map/pallas_call | solution.py:458
  35.7 0.0 collective-permute-done.behind_ref
  35.7 0.0 copy-start
  35.7 4.2 %shard_map.98 = (bf16[128,1024]{1,0:T(8,128)(2,1)S(1)}, bf16[128,3072]{1,0:T(8,128)(2,1)S(1)}, bf16[2,8,64,128]{3,2,1,0:T(8,128)(2,1)S(1)}, f32[128,128]{1,0:T(8...) custom-call(s32[8,128]{1,0:T(8,128)S(1)} %get-tuple-element.35.shift, ...), custom_call_target="tpu_custom_call" | custom-call | tf_op jit(solution)/shard_map/pallas_call | solution.py:470
  39.9 0.0 collective-permute-done.3.time_target
  39.9 0.0 collective-permute-done.4.corner_target
  39.9 0.0 collective-permute-done.1.row_target
  39.9 0.0 copy-done
  39.9 6.7 %shard_map.99 = (bf16[128,1024]{1,0:T(8,128)(2,1)S(1)}, bf16[32,1024]{1,0:T(8,128)(2,1)S(1)}, f32[8,128]{1,0:T(8,128)S(1)}) custom-call(s32[2,2]{1,0:T(2,128)S(1)} %copy-done, bf16[128,1024]{1,0:T(8,128)(2,1)S(1)} %get-tuple-element.47.embedded_0_ref, bf16[128,3072]{1,0:T(8,128)(2,1)S(1)} %get-tuple-element.48.qkv_0_ref, ...), custom_call_target="tpu_custom_call" | custom-call | tf_op jit(solution)/shard_map/pallas_call | solution.py:483
  46.6 3.0 %collective-permute-start.5 = (bf16[32,1024]{1,0:T(8,128)(2,1)S(1)}, bf16[32,1024]{1,0:T(8,128)(2,1)S(1)}, u32[]{:S(2)}, u32[]{:S(2)}) collective-permute-start(bf16[32,1024]{1,0:T(8,128)(2,1)S(1)} %get-tuple-element.64), channel_id=1, source_target_pairs={{0,112},{16,0},{32,16},{48,32},{64,48},{80,64},{96,80},{112,96},{1... | collective-permute-start | bytes 196616 | tf_op jit(solution)/shard_map/ppermute | solution.py:488
  49.6 0.0 collective-permute-start.6
  49.6 1.2 %collective-permute-done.6 = f32[8,128]{1,0:T(8,128)S(1)} collective-permute-done((f32[8,128]{1,0:T(8,128)S(1)}, f32[8,128]{1,0:T(8,128)S(1)}, u32[]{:S(2)}, u32[]{:S(2)}) %collective-permute-start.6) | collective-permute-done | bytes 4128 | tf_op jit(solution)/shard_map/ppermute | solution.py:488
  50.8 0.8 %collective-permute-start.7 = (f32[8,128]{1,0:T(8,128)S(1)}, f32[8,128]{1,0:T(8,128)S(1)}, u32[]{:S(2)}, u32[]{:S(2)}) collective-permute-start(f32[8,128]{1,0:T(8,128)S(1)} %add.3.total_ref), channel_id=1, source_target_pairs={{0,32},{32,64},{64,96},{96,0},{1,33},{33,65},{65,97},{97,1},{2,34}... | collective-permute-start | bytes 12296 | tf_op jit(solution)/shard_map/ppermute | solution.py:488
  51.5 3.5 %collective-permute-start.8 = (f32[8,128]{1,0:T(8,128)S(1)}, f32[8,128]{1,0:T(8,128)S(1)}, u32[]{:S(2)}, u32[]{:S(2)}) collective-permute-start(f32[8,128]{1,0:T(8,128)S(1)} %add.3.total_ref), channel_id=1, source_target_pairs={{0,64},{32,96},{64,0},{96,32},{1,65},{33,97},{65,1},{97,33},{2,66}... | collective-permute-start | bytes 12296 | tf_op jit(solution)/shard_map/ppermute | solution.py:488
  55.1 1.0 %collective-permute-start.9 = (f32[8,128]{1,0:T(8,128)S(1)}, f32[8,128]{1,0:T(8,128)S(1)}, u32[]{:S(2)}, u32[]{:S(2)}) collective-permute-start(f32[8,128]{1,0:T(8,128)S(1)} %add.3.total_ref), channel_id=1, source_target_pairs={{0,96},{32,0},{64,32},{96,64},{1,97},{33,1},{65,33},{97,65},{2,98}... | collective-permute-start | bytes 12296 | tf_op jit(solution)/shard_map/ppermute | solution.py:488
  56.1 0.0 collective-permute-done.7.turned_1_ref
  56.1 0.6 collective-permute-done.8.turned_2_ref
  56.7 2.0 %collective-permute-done.9.turned_3_ref = f32[8,128]{1,0:T(8,128)S(1)} collective-permute-done((f32[8,128]{1,0:T(8,128)S(1)}, f32[8,128]{1,0:T(8,128)S(1)}, u32[]{:S(2)}, u32[]{:S(2)}) %collective-permute-start.9) | collective-permute-done | bytes 4128 | tf_op jit(solution)/shard_map/ppermute | solution.py:488
  58.7 0.0 collective-permute-done.5.next_ref
  58.7 0.2 shard_map.100
  58.9 11.6 %all_to_all.10.back_ref = bf16[16,8,1280]{2,1,0:T(8,128)(2,1)S(1)} all-to-all(bf16[16,8,1280]{2,1,0:T(8,128)(2,1)S(1)} %shard_map.100), channel_id=1, replica_groups=mesh['tm_0'=4,'tm_1'=2,'row_0'=4,'row_1'=4] {'row_0','row_1'}, dimensions={0} | all-to-all | bytes 655360 | tf_op jit(solution)/shard_map/all_to_all | solution.py:531
  70.6 0.8 %shard_map.101 = (bf16[16,4,1024]{2,1,0:T(4,128)(2,1)}, f32[8,128]{1,0:T(8,128)}) custom-call(bf16[16,8,1280]{2,1,0:T(8,128)(2,1)S(1)} %all_to_all.10.back_ref), custom_call_target="tpu_custom_call" | custom-call | tf_op jit(solution)/shard_map/pallas_call | solution.py:535
  (1 shorter events, 0.0 us)
Async XLA Ops:
  2.6 17.6 %all-to-all-start = ((bf16[16,8,1152]{2,1,0:T(8,128)(2,1)}), bf16[16,8,1152]{2,1,0:T(8,128)(2,1)S(1)}, u32[]{:S(2)}, u32[]{:S(2)}) async-start(bf16[16,8,1152]{2,1,0:T(8,128)(2,1)} %get-tuple-element.36), calls=%async_computation | async-start | bytes 589824 | tf_op jit(solution)/shard_map/all_to_all | solution.py:502
  10.7 29.2 %collective-permute-start.1 = (bf16[3,3,16,1536]{3,2,1,0:T(8,128)(2,1)S(1)}, bf16[3,3,16,1536]{3,2,1,0:T(8,128)(2,1)S(1)}, u32[]{:S(2)}, u32[]{:S(2)}) collective-permute-start(bf16[3,3,16,1536]{3,2,1,0:T(8,128)(2,1)S(1)} %get-tuple-element.60), channel_id=1, source_target_pairs={{0,1},{1,2},{2,3},{3,4},{4,5},{5,6},{6,7},{7,8},{8,9},{9,10},{10,1... | collective-permute-start | bytes 1327112 | tf_op jit(solution)/shard_map/ppermute | solution.py:488
  20.2 15.4 %collective-permute-start = (bf16[128,1152]{1,0:T(8,128)(2,1)S(1)}, bf16[128,1152]{1,0:T(8,128)(2,1)S(1)}, u32[]{:S(2)}, u32[]{:S(2)}) collective-permute-start(bf16[128,1152]{1,0:T(8,128)(2,1)S(1)} %bitcast.8), channel_id=1, source_target_pairs={{0,16},{16,32},{32,48},{48,64},{64,80},{80,96},{96,112},{112,0},{1... | collective-permute-start | bytes 884744 | tf_op jit(solution)/shard_map/ppermute | solution.py:488
  20.2 10.8 %collective-permute-start.2 = (bf16[1,3,16,1536]{3,2,1,0:T(8,128)(2,1)S(1)}, bf16[1,3,16,1536]{3,2,1,0:T(8,128)(2,1)S(1)}, u32[]{:S(2)}, u32[]{:S(2)}) collective-permute-start(bf16[1,3,16,1536]{3,2,1,0:T(8,128)(2,1)S(1)} %get-tuple-element.61), channel_id=1, source_target_pairs={{0,1},{1,2},{2,3},{3,4},{4,5},{5,6},{6,7},{7,8},{8,9},{9,10},{10,1... | collective-permute-start | bytes 442376 | tf_op jit(solution)/shard_map/ppermute | solution.py:488
  20.2 19.6 %collective-permute-start.3 = (bf16[1,4,16,1536]{3,2,1,0:T(8,128)(2,1)S(1)}, bf16[1,4,16,1536]{3,2,1,0:T(8,128)(2,1)S(1)}, u32[]{:S(2)}, u32[]{:S(2)}) collective-permute-start(bf16[1,4,16,1536]{3,2,1,0:T(8,128)(2,1)S(1)} %get-tuple-element.62), channel_id=1, source_target_pairs={{0,16},{16,32},{32,48},{48,64},{64,80},{80,96},{96,112},{112,0},{1... | collective-permute-start | bytes 589832 | tf_op jit(solution)/shard_map/ppermute | solution.py:488
  31.0 8.9 %collective-permute-start.4 = (bf16[1,3,16,1536]{3,2,1,0:T(8,128)(2,1)S(1)}, bf16[1,3,16,1536]{3,2,1,0:T(8,128)(2,1)S(1)}, u32[]{:S(2)}, u32[]{:S(2)}) collective-permute-start(bf16[1,3,16,1536]{3,2,1,0:T(8,128)(2,1)S(1)} %collective-permute-done.2.last_row_target), channel_id=1, source_target_pairs={{0,16},{16,32},{32,48},{48,64},{64,80},{80,96},{96,112},{112,0},{1... | collective-permute-start | bytes 442376 | tf_op jit(solution)/shard_map/ppermute | solution.py:488
  35.7 4.2 %copy-start = (s32[2,2]{1,0:T(2,128)S(1)}, s32[2,2]{1,0:T(2,128)}, u32[]{:S(2)}) copy-start(s32[2,2]{1,0:T(2,128)} %shift_ref.1) | copy-start | bytes 52
  46.6 12.1 %collective-permute-start.5 = (bf16[32,1024]{1,0:T(8,128)(2,1)S(1)}, bf16[32,1024]{1,0:T(8,128)(2,1)S(1)}, u32[]{:S(2)}, u32[]{:S(2)}) collective-permute-start(bf16[32,1024]{1,0:T(8,128)(2,1)S(1)} %get-tuple-element.64), channel_id=1, source_target_pairs={{0,112},{16,0},{32,16},{48,32},{64,48},{80,64},{96,80},{112,96},{1... | collective-permute-start | bytes 196616 | tf_op jit(solution)/shard_map/ppermute | solution.py:488
  49.6 1.2 %collective-permute-start.6 = (f32[8,128]{1,0:T(8,128)S(1)}, f32[8,128]{1,0:T(8,128)S(1)}, u32[]{:S(2)}, u32[]{:S(2)}) collective-permute-start(f32[8,128]{1,0:T(8,128)S(1)} %get-tuple-element.65), channel_id=1, source_target_pairs={{0,16},{16,0},{1,17},{17,1},{2,18},{18,2},{3,19},{19,3},{4,20},{20... | collective-permute-start | bytes 12296 | tf_op jit(solution)/shard_map/ppermute | solution.py:488
  50.8 5.3 %collective-permute-start.7 = (f32[8,128]{1,0:T(8,128)S(1)}, f32[8,128]{1,0:T(8,128)S(1)}, u32[]{:S(2)}, u32[]{:S(2)}) collective-permute-start(f32[8,128]{1,0:T(8,128)S(1)} %add.3.total_ref), channel_id=1, source_target_pairs={{0,32},{32,64},{64,96},{96,0},{1,33},{33,65},{65,97},{97,1},{2,34}... | collective-permute-start | bytes 12296 | tf_op jit(solution)/shard_map/ppermute | solution.py:488
  51.5 5.2 %collective-permute-start.8 = (f32[8,128]{1,0:T(8,128)S(1)}, f32[8,128]{1,0:T(8,128)S(1)}, u32[]{:S(2)}, u32[]{:S(2)}) collective-permute-start(f32[8,128]{1,0:T(8,128)S(1)} %add.3.total_ref), channel_id=1, source_target_pairs={{0,64},{32,96},{64,0},{96,32},{1,65},{33,97},{65,1},{97,33},{2,66}... | collective-permute-start | bytes 12296 | tf_op jit(solution)/shard_map/ppermute | solution.py:488
  55.1 3.6 %collective-permute-start.9 = (f32[8,128]{1,0:T(8,128)S(1)}, f32[8,128]{1,0:T(8,128)S(1)}, u32[]{:S(2)}, u32[]{:S(2)}) collective-permute-start(f32[8,128]{1,0:T(8,128)S(1)} %add.3.total_ref), channel_id=1, source_target_pairs={{0,96},{32,0},{64,32},{96,64},{1,97},{33,1},{65,33},{97,65},{2,98}... | collective-permute-start | bytes 12296 | tf_op jit(solution)/shard_map/ppermute | solution.py:488

commit v7 on v6

--- a/solution.py
+++ b/solution.py
@@ -129,8 +129,8 @@
 
 
 def early_kernel(
-    shift_ref, own_ref, mask_ref, frames_ref, rows_ref, columns_ref, w_qkv_hbm, w_out_hbm, w_head_hbm,
-    embedded_ref, qkv_ref, probs_ref, seen_ref, one_hot_ref, heads_ref, w_qkv_ref, w_out_ref, w_head_ref,
+    shift_ref, own_ref, mask_ref, frames_ref, rows_ref, columns_ref, w_qkv_hbm, w_out_hbm,
+    embedded_ref, qkv_ref, probs_ref, seen_ref, one_hot_ref, heads_ref, w_qkv_ref, w_out_ref,
     chosen_ref, normed_ref, sems,
 ):
     copies = [
@@ -140,7 +140,6 @@
         for at in range(3)
     ]
     copies.append(pltpu.make_async_copy(w_out_hbm, w_out_ref, sems.at[3]))
-    copies.append(pltpu.make_async_copy(w_head_hbm, w_head_ref, sems.at[4]))
     for copy in copies:
         copy.start()
     one_hot_ref[...] = slot_one_hot(shift_ref, own_ref, 0, 1)
@@ -152,15 +151,16 @@
         project(at, normed_ref, w_qkv_ref, qkv_ref)
     attend(qkv_ref, probs_ref, heads_ref)
     copies[3].wait()
-    copies[4].wait()
 
 
 def late_kernel(
     shift_ref, own_ref, behind_ref, mask_ref, frames_ref, rows_ref, columns_ref, embedded_1_ref, heads_1_ref,
-    w_qkv_ref, w_out_ref, w_head_ref,
-    embedded_ref, qkv_ref, probs_ref, seen_ref, one_hot_ref, head_normed_ref, scale_ref, predicted_ref,
-    chosen_ref, normed_ref, heads_ref, residual_ref, narrow_ref,
+    w_qkv_ref, w_out_ref, w_head_hbm,
+    embedded_ref, qkv_ref, probs_ref, seen_ref, one_hot_ref, head_normed_ref, scale_ref, predicted_ref, w_head_ref,
+    chosen_ref, normed_ref, heads_ref, residual_ref, narrow_ref, sem,
 ):
+    head_copy = pltpu.make_async_copy(w_head_hbm, w_head_ref, sem)
+    head_copy.start()
     one_hot_ref[:SLOTS] = slot_one_hot(shift_ref, own_ref, 0, 0)
     one_hot_ref[SLOTS:] = slot_one_hot(shift_ref, behind_ref, 1, 0)
     own_hot = one_hot_ref[:SLOTS]
@@ -183,6 +183,7 @@
         head_normed_ref[rows] = normed
         scale_ref[rows] = jnp.broadcast_to(scale, (16, 128))
         narrow_ref[rows] = normed.astype(BF)
+    head_copy.wait()
     for part in range(3):
         cols = slice(part * GROUP, part * GROUP + GROUP)
         predicted_ref[:, cols] = dot(narrow_ref[...], w_head_ref[:, cols], NN_DIMS)
@@ -192,7 +193,7 @@
     shift_ref, embedded_0_ref, qkv_0_ref, probs_0_ref, seen_0_ref, one_hot_0_ref,
     embedded_1_ref, qkv_1_ref, probs_1_ref, seen_1_ref, one_hot_1_ref,
     normed_ref, scale_ref, predicted_ref, w_qkv_ref, w_out_ref, w_head_ref,
-    own_target, row_target, last_row_target, time_target, corner_target,
+    own_target, first_row_target, row_target, last_row_target, time_target, corner_target,
     own_picked_ref, behind_rows_ref, total_ref,
     target_ref, error_ref, narrow_ref, wide_ref, stream_ref, dqkv_ref,
 ):
@@ -201,7 +202,8 @@
     probs_refs = (probs_0_ref, probs_1_ref)
     seen_refs = (seen_0_ref, seen_1_ref)
     target_ref[1:, 3:] = own_target[...]
-    target_ref[1:4, :3] = row_target[...]
+    target_ref[1:2, :3] = first_row_target[...]
+    target_ref[2:4, :3] = row_target[...]
     target_ref[4:, :3] = last_row_target[...]
     target_ref[:1, 3:] = time_target[...]
     target_ref[:1, :3] = corner_target[...]
@@ -291,7 +293,7 @@
 
 
 def give_kernel(
-    shift_ref, own_ref, picked_ref, next_ref, total_ref, turned_1_ref, turned_2_ref, turned_3_ref, sent_ref
+    shift_ref, own_ref, picked_ref, next_ref, total_ref, far_ref, sent_ref
 ):
     place = own_ref[:, D : D + 128].astype(F32).astype(jnp.int32)
     row = (place >> 4) & 3
@@ -306,7 +308,7 @@
     rows = jnp.concatenate([next_ref[...], jnp.zeros((SLOTS - 32, D), BF)], axis=0)
     picked = picked_ref[...].astype(F32) + dot(one_hot, rows, NN_DIMS)
     sent_ref[:, :, :D] = picked.reshape(16, 8, D).astype(BF)
-    total = (total_ref[...] + turned_2_ref[...]) + (turned_1_ref[...] + turned_3_ref[...])
+    total = total_ref[...] + far_ref[...]
     high = total.astype(BF)
     low = (total - high.astype(F32)).astype(BF)
     for peer in range(16):
@@ -372,7 +374,7 @@
 
 
 def target_kernel(
-    totals, shift_rows_ref, pixel_ref, own_ref, row_ref, last_row_ref, time_ref, frames_ref, rows_ref, columns_ref
+    totals, shift_rows_ref, pixel_ref, own_ref, first_row_ref, row_ref, last_row_ref, time_ref, frames_ref, rows_ref, columns_ref
 ):
     frames = grid_coordinates(lax.axis_index(TM) * 4, shift_rows_ref, 0, totals[0], 256)
     rows = grid_coordinates(lax.axis_index(ROW) * 4, shift_rows_ref, 2, totals[1], 384)
@@ -388,8 +390,10 @@
                 spread = jnp.sqrt(jnp.sum(center * center, axis=-1, keepdims=True) * (1.0 / (GROUP - 1)))
                 target = (center * (1.0 / (spread + 1e-06))).astype(BF)
                 own_ref[frame, row, :, cols] = target
-                if row > 0 and frame < 3:
-                    row_ref[frame, row - 1, :, cols] = target
+                if row > 0 and frame == 0:
+                    first_row_ref[0, row - 1, :, cols] = target
+                if row > 0 and 0 < frame < 3:
+                    row_ref[frame - 1, row - 1, :, cols] = target
                 if row > 0 and frame == 3:
                     last_row_ref[0, row - 1, :, cols] = target
                 if frame == 3:
@@ -446,28 +450,29 @@
 
 
 def target_part(totals, *operands):
-    outputs = [((frames, rows, 16, PIX), BF) for frames, rows in ((4, 4), (3, 3), (1, 3), (1, 4))]
+    outputs = [((frames, rows, 16, PIX), BF) for frames, rows in ((4, 4), (1, 3), (2, 3), (1, 3), (1, 4))]
     outputs += [((8, 256), F32), ((8, 384), F32), ((16, 384), F32)]
     kernel = functools.partial(target_kernel, totals)
     return call(kernel, outputs, [], in_space(VMEM, 2), 8)(*operands)
 
 
 def early_part(*operands):
-    outputs = half_outputs(SLOTS) + [((HALF, D), BF), ((D, 3 * D), BF), ((D, D), BF), ((D, PIX), BF)]
-    scratch = [pltpu.VMEM((HALF, D), F32), pltpu.VMEM((HALF, D), BF), pltpu.SemaphoreType.DMA((5,))]
-    return call(early_kernel, outputs, scratch, in_space(VMEM, 6) + in_space(HBM, 3), 20)(*operands)
+    outputs = half_outputs(SLOTS) + [((HALF, D), BF), ((D, 3 * D), BF), ((D, D), BF)]
+    scratch = [pltpu.VMEM((HALF, D), F32), pltpu.VMEM((HALF, D), BF), pltpu.SemaphoreType.DMA((4,))]
+    return call(early_kernel, outputs, scratch, in_space(VMEM, 6) + in_space(HBM, 2), 20)(*operands)
 
 
 def late_part(*operands):
-    outputs = half_outputs(2 * SLOTS) + [((TOK, D), F32), ((TOK, 128), F32), ((TOK, PIX), F32)]
+    outputs = half_outputs(2 * SLOTS) + [((TOK, D), F32), ((TOK, 128), F32), ((TOK, PIX), F32), ((D, PIX), BF)]
     scratch = [
         pltpu.VMEM((HALF, D), F32),
         pltpu.VMEM((HALF, D), BF),
         pltpu.VMEM((TOK, D), BF),
         pltpu.VMEM((TOK, D), F32),
         pltpu.VMEM((TOK, D), BF),
+        pltpu.SemaphoreType.DMA,
     ]
-    return call(late_kernel, outputs, scratch, in_space(VMEM, 12), 26)(*operands)
+    return call(late_kernel, outputs, scratch, in_space(VMEM, 11) + in_space(HBM, 1), 28)(*operands)
 
 
 def backward_part(*operands):
@@ -480,7 +485,7 @@
         pltpu.VMEM((TOK, D), F32),
         pltpu.VMEM((TOK, 3 * D), BF),
     ]
-    return call(backward_kernel, outputs, scratch, in_space(SMEM, 1) + in_space(VMEM, 21), 34)(*operands)
+    return call(backward_kernel, outputs, scratch, in_space(SMEM, 1) + in_space(VMEM, 22), 34)(*operands)
 
 
 def move(value, axis, steps):
@@ -503,31 +508,32 @@
     behind = move(own, TM, 1)
     frame_total = frame_count * lax.axis_size(TM)
     row_total = row_count * lax.axis_size(ROW)
-    own_target, row_target, last_row_target, time_target, *positions = target_part(
+    own_target, first_row_target, row_target, last_row_target, time_target, *positions = target_part(
         (frame_total, row_total), shift_rows, near_pixels
     )
     last_row_target = move(last_row_target, ROW, 1)
+    first_row_target = move(first_row_target, ROW, 1)
     row_target = move(row_target, ROW, 1)
     time_target = move(time_target, TM, 1)
     corner_target = move(last_row_target, TM, 1)
 
     tables = (mask_rows, *positions)
-    *half_1, heads_1, w_qkv, w_out, w_head = early_part(
-        shift_rows, own, *tables, hold(w_qkv), hold(w_out), hold(w_head)
-    )
-    *half_0, head_normed, head_scale, predicted = late_part(
-        shift_rows, own, behind, *tables, half_1[0], heads_1, w_qkv, w_out, w_head
+    *half_1, heads_1, w_qkv, w_out = early_part(shift_rows, own, *tables, hold(w_qkv), hold(w_out))
+    *half_0, head_normed, head_scale, predicted, w_head = late_part(
+        shift_rows, own, behind, *tables, half_1[0], heads_1, w_qkv, w_out, hold(w_head)
     )
     own_picked, behind_rows, local_total = backward_part(
         window_shift, *half_0, *half_1, head_normed, head_scale, predicted, w_qkv, w_out, w_head,
-        own_target, row_target, last_row_target, time_target, corner_target,
+        own_target, first_row_target, row_target, last_row_target, time_target, corner_target,
     )
     other = move(local_total, "tm_1", 1)
     from_next = move(behind_rows, TM, -1)
     local_total = local_total + other
-    turned = [move(local_total, "tm_0", step) for step in (1, 2, 3)]
-    give = call(give_kernel, [((peers, 8, D + 256), BF)], [], in_space(VMEM, 8), 8)
-    (sent,) = give(shift_rows, own, own_picked, from_next, local_total, *turned)
+    pairs = [(at, at ^ 1) for at in range(lax.axis_size("tm_0"))]
+    local_total = local_total + lax.ppermute(local_total, "tm_0", pairs)
+    far = move(local_total, "tm_0", 2)
+    give = call(give_kernel, [((peers, 8, D + 256), BF)], [], in_space(VMEM, 6), 8)
+    (sent,) = give(shift_rows, own, own_picked, from_next, local_total, far)
     back = lax.all_to_all(sent, ROW, split_axis=0, concat_axis=0, tiled=True)
     grad_scale = (frame_total * row_total * pixels.shape[2]) ** (-0.5)
     outputs = [((peers, slots, D), BF), ((8, 128), F32)]

time: 71.6 us -> 69.3 us (0.968)
  blocking collectives: 11.6 us -> 27.6 us
  waiting for transfers between devices: 20 us -> 10.5 us
  starting transfers between devices: 19.6 us -> 11.4 us
    all_to_all x0 -> x1, blocking collectives: none -> 16 us  [per_device(): lax.all_to_all(packed, ROW, split_axis=0, concat_axis=0, tiled=True)]
    all_to_all x1 -> x0, waiting for transfers between devices: 7.52 us -> none  [per_device(): lax.all_to_all(packed, ROW, split_axis=0, concat_axis=0, tiled=True)]
    all_to_all x1 -> x0, starting transfers between devices: 7.16 us -> none  [per_device(): lax.all_to_all(packed, ROW, split_axis=0, concat_axis=0, tiled=True)]
    ppermute x10 -> x9, waiting for transfers between devices: 12.5 us -> 8.23 us  [move(): lax.ppermute(value, axis, [(at, (at + steps) % count) for at in range(cou...]
    ppermute x10 -> x9, starting transfers between devices: 12.5 us -> 10.1 us  [move(): lax.ppermute(value, axis, [(at, (at + steps) % count) for at in range(cou...]
    ppermute x0 -> x1, waiting for transfers between devices: none -> 2.24 us  [per_device(): local_total = local_total + lax.ppermute(local_total, 'tm_0', pairs)]
    ppermute x0 -> x1, starting transfers between devices: none -> 1.37 us  [per_device(): local_total = local_total + lax.ppermute(local_total, 'tm_0', pairs)]
  transfers between devices with their start and end apart: 11 -> 10, of which waited for: 5 -> 4; matrix products, arithmetic and copies ran while one was open for 0% -> 0% of each run, Pallas kernels for 13% -> 14%
where the time goes in v7:
time: 69.3 us; the launch traced here: 69.1 us
  blocking collectives  27.6 us (40%)
  Pallas kernels  18.8 us (27%)
  starting transfers between devices  11.4 us (16%)
  waiting for transfers between devices  10.5 us (15%)
  between operations  0.74 us (1%)
    all_to_all x1, blocking collectives, per_device(): lax.all_to_all(packed, ROW, split_axis=0, concat_axis=0, tiled=True)  16 us
    all_to_all x1, blocking collectives, per_device(): back = lax.all_to_all(sent, ROW, split_axis=0, concat_axis=0, tiled=True)  11.6 us
    ppermute x9, starting transfers between devices, move(): lax.ppermute(value, axis, [(at, (at + steps) % count) for at in range(cou...  10.1 us
    ppermute x9, waiting for transfers between devices, move(): lax.ppermute(value, axis, [(at, (at + steps) % count) for at in range(cou...  8.23 us
    pallas_call x1, Pallas kernels, backward_part(): call(backward_kernel, outputs, scratch, in_space(SMEM, 1) + in_space(VMEM...  6.67 us
    pallas_call x1, Pallas kernels, early_part(): call(early_kernel, outputs, scratch, in_space(VMEM, 6) + in_space(HBM, 2)...  4.58 us
    pallas_call x1, Pallas kernels, late_part(): call(late_kernel, outputs, scratch, in_space(VMEM, 11) + in_space(HBM, 1)...  4.35 us
    ppermute x1, waiting for transfers between devices, per_device(): local_total = local_total + lax.ppermute(local_total, 'tm_0', pairs)  2.24 us
  transfers between devices with their start and end apart: 10, of which 4 were waited for; matrix products, arithmetic and copies ran while one was open for 0% of the time, Pallas kernels for 14%

profile of v7, /device:TPU:0, one launch (start us, length us, event | category | flops | bytes accessed | tf_op | source)
XLA Modules:
  0.0 69.1 jit_solution(2202564035366132191)
XLA Ops:
  0.6 1.3 %shard_map.95 = (bf16[16,8,1152]{2,1,0:T(8,128)(2,1)S(1)}, s32[8,128]{1,0:T(8,128)S(1)}, bf16[8,128]{1,0:T(8,128)(2,1)S(1)}, bf16[4,4,16,1536]{3,2,1,0:T(8,128)(2,1)S(1)}) custom-call(s32[4,16]{1,0:T(4,128)} %bitcast.13, s32[2,2]{1,0:T(2,128)} %shift_ref.1, bf16[8,128]{1,0:T(8,128)(2,1)} %bitcast.14, bf16[16,4,1024]{2,1,0:T(4,128)(2,1)} %bitcast.12, ...), custom_call_target="tpu_custom_call" | custom-call | tf_op jit(solution)/shard_map/pallas_call | solution.py:449
  1.9 16.0 %all_to_all.10 = bf16[16,8,1152]{2,1,0:T(8,128)(2,1)S(1)} all-to-all(bf16[16,8,1152]{2,1,0:T(8,128)(2,1)S(1)} %get-tuple-element.37), channel_id=1, replica_groups=mesh['tm_0'=4,'tm_1'=2,'row_0'=4,'row_1'=4] {'row_0','row_1'}, dimensions={0} | all-to-all | bytes 589824 | tf_op jit(solution)/shard_map/all_to_all | solution.py:507
  17.9 0.0 collective-permute-start
  17.9 0.9 %shard_map.96 = (bf16[4,4,16,1536]{3,2,1,0:T(8,128)(2,1)S(1)}, bf16[1,3,16,1536]{3,2,1,0:T(8,128)(2,1)S(1)}, bf16[2,3,16,1536]{3,2,1,0:T(8,128)(2,1)S(1)}, bf16[...) custom-call(s32[8,128]{1,0:T(8,128)S(1)} %get-tuple-element.36.shift, ...), custom_call_target="tpu_custom_call" | custom-call | tf_op jit(solution)/shard_map/pallas_call | solution.py:456
  18.8 0.6 collective-permute-start.3
  19.5 0.3 collective-permute-start.2
  19.7 1.6 %collective-permute-start.4 = (bf16[1,4,16,1536]{3,2,1,0:T(8,128)(2,1)S(1)}, bf16[1,4,16,1536]{3,2,1,0:T(8,128)(2,1)S(1)}, u32[]{:S(2)}, u32[]{:S(2)}) collective-permute-start(bf16[1,4,16,1536]{3,2,1,0:T(8,128)(2,1)S(1)} %get-tuple-element.64), channel_id=1, source_target_pairs={{0,16},{16,32},{32,48},{48,64},{64,80},{80,96},{96,112},{112,0},{1... | collective-permute-start | bytes 589832 | tf_op jit(solution)/shard_map/ppermute | solution.py:493
  21.3 1.2 %collective-permute-start.1 = (bf16[1,3,16,1536]{3,2,1,0:T(8,128)(2,1)S(1)}, bf16[1,3,16,1536]{3,2,1,0:T(8,128)(2,1)S(1)}, u32[]{:S(2)}, u32[]{:S(2)}) collective-permute-start(bf16[1,3,16,1536]{3,2,1,0:T(8,128)(2,1)S(1)} %get-tuple-element.61), channel_id=1, source_target_pairs={{0,1},{1,2},{2,3},{3,4},{4,5},{5,6},{6,7},{7,8},{8,9},{9,10},{10,1... | collective-permute-start | bytes 442376 | tf_op jit(solution)/shard_map/ppermute | solution.py:493
  22.4 5.4 %collective-permute-done.3.last_row_target = bf16[1,3,16,1536]{3,2,1,0:T(8,128)(2,1)S(1)} collective-permute-done((bf16[1,3,16,1536]{3,2,1,0:T(8,128)(2,1)S(1)}, bf16[1,3,16,1536]{3,2,1,0:T(8,128)(2,1)S(1)}, u32[]{:S(2)}, u32[]{:S(2)}) %collective-permute-start.3) | collective-permute-done | bytes 147488 | tf_op jit(solution)/shard_map/ppermute | solution.py:493
  27.9 2.2 %collective-permute-start.5 = (bf16[1,3,16,1536]{3,2,1,0:T(8,128)(2,1)S(1)}, bf16[1,3,16,1536]{3,2,1,0:T(8,128)(2,1)S(1)}, u32[]{:S(2)}, u32[]{:S(2)}) collective-permute-start(bf16[1,3,16,1536]{3,2,1,0:T(8,128)(2,1)S(1)} %collective-permute-done.3.last_row_target), channel_id=1, source_target_pairs={{0,16},{16,32},{32,48},{48,64},{64,80},{80,96},{96,112},{112,0},{1... | collective-permute-start | bytes 442376 | tf_op jit(solution)/shard_map/ppermute | solution.py:493
  30.1 4.6 %shard_map.97 = (bf16[128,1024]{1,0:T(8,128)(2,1)S(1)}, bf16[128,3072]{1,0:T(8,128)(2,1)S(1)}, bf16[2,8,64,128]{3,2,1,0:T(8,128)(2,1)S(1)}, f32[128,128]{1,0:T(8...) custom-call(s32[8,128]{1,0:T(8,128)S(1)} %get-tuple-element.36.shift, ...), custom_call_target="tpu_custom_call" | custom-call | tf_op jit(solution)/shard_map/pallas_call | solution.py:462
  34.7 0.0 collective-permute-done.behind_ref
  34.7 0.0 copy-start
  34.7 4.3 %shard_map.98 = (bf16[128,1024]{1,0:T(8,128)(2,1)S(1)}, bf16[128,3072]{1,0:T(8,128)(2,1)S(1)}, bf16[2,8,64,128]{3,2,1,0:T(8,128)(2,1)S(1)}, f32[128,128]{1,0:T(8...) custom-call(s32[8,128]{1,0:T(8,128)S(1)} %get-tuple-element.36.shift, ...), custom_call_target="tpu_custom_call" | custom-call | tf_op jit(solution)/shard_map/pallas_call | solution.py:475
  39.1 0.0 collective-permute-done.1.first_row_target
  39.1 0.0 collective-permute-done.4.time_target
  39.1 0.0 collective-permute-done.5.corner_target
  39.1 0.0 collective-permute-done.2.row_target
  39.1 0.0 copy-done
  39.1 6.7 %shard_map.99 = (bf16[128,1024]{1,0:T(8,128)(2,1)S(1)}, bf16[32,1024]{1,0:T(8,128)(2,1)S(1)}, f32[8,128]{1,0:T(8,128)S(1)}) custom-call(s32[2,2]{1,0:T(2,128)S(1)} %copy-done, bf16[128,1024]{1,0:T(8,128)(2,1)S(1)} %get-tuple-element.47.embedded_0_ref, bf16[128,3072]{1,0:T(8,128)(2,1)S(1)} %get-tuple-element.48.qkv_0_ref, ...), custom_call_target="tpu_custom_call" | custom-call | tf_op jit(solution)/shard_map/pallas_call | solution.py:488
  45.8 0.7 %collective-permute-start.6 = (bf16[32,1024]{1,0:T(8,128)(2,1)S(1)}, bf16[32,1024]{1,0:T(8,128)(2,1)S(1)}, u32[]{:S(2)}, u32[]{:S(2)}) collective-permute-start(bf16[32,1024]{1,0:T(8,128)(2,1)S(1)} %get-tuple-element.66), channel_id=1, source_target_pairs={{0,112},{16,0},{32,16},{48,32},{64,48},{80,64},{96,80},{112,96},{1... | collective-permute-start | bytes 196616 | tf_op jit(solution)/shard_map/ppermute | solution.py:493
  46.5 0.0 collective-permute-start.7
  46.5 1.2 %collective-permute-done.7 = f32[8,128]{1,0:T(8,128)S(1)} collective-permute-done((f32[8,128]{1,0:T(8,128)S(1)}, f32[8,128]{1,0:T(8,128)S(1)}, u32[]{:S(2)}, u32[]{:S(2)}) %collective-permute-start.7) | collective-permute-done | bytes 4128 | tf_op jit(solution)/shard_map/ppermute | solution.py:493
  47.7 1.4 %collective-permute-start.8 = (f32[8,128]{1,0:T(8,128)S(1)}, f32[8,128]{1,0:T(8,128)S(1)}, u32[]{:S(2)}, u32[]{:S(2)}) collective-permute-start(f32[8,128]{1,0:T(8,128)S(1)} %add.6), channel_id=1, source_target_pairs={{0,32},{32,0},{64,96},{96,64},{1,33},{33,1},{65,97},{97,65},{2,34}... | collective-permute-start | bytes 12296 | tf_op jit(solution)/shard_map/ppermute | solution.py:533
  49.1 2.2 %collective-permute-done.8 = f32[8,128]{1,0:T(8,128)S(1)} collective-permute-done((f32[8,128]{1,0:T(8,128)S(1)}, f32[8,128]{1,0:T(8,128)S(1)}, u32[]{:S(2)}, u32[]{:S(2)}) %collective-permute-start.8) | collective-permute-done | bytes 4128 | tf_op jit(solution)/shard_map/ppermute | solution.py:533
  51.3 3.5 %collective-permute-start.9 = (f32[8,128]{1,0:T(8,128)S(1)}, f32[8,128]{1,0:T(8,128)S(1)}, u32[]{:S(2)}, u32[]{:S(2)}) collective-permute-start(f32[8,128]{1,0:T(8,128)S(1)} %add.7.total_ref), channel_id=1, source_target_pairs={{0,64},{32,96},{64,0},{96,32},{1,65},{33,97},{65,1},{97,33},{2,66}... | collective-permute-start | bytes 12296 | tf_op jit(solution)/shard_map/ppermute | solution.py:493
  54.8 1.6 %collective-permute-done.9.far_ref = f32[8,128]{1,0:T(8,128)S(1)} collective-permute-done((f32[8,128]{1,0:T(8,128)S(1)}, f32[8,128]{1,0:T(8,128)S(1)}, u32[]{:S(2)}, u32[]{:S(2)}) %collective-permute-start.9) | collective-permute-done | bytes 4128 | tf_op jit(solution)/shard_map/ppermute | solution.py:493
  56.4 0.0 collective-permute-done.6.next_ref
  56.4 0.2 shard_map.100
  56.7 11.6 %all_to_all.11.back_ref = bf16[16,8,1280]{2,1,0:T(8,128)(2,1)S(1)} all-to-all(bf16[16,8,1280]{2,1,0:T(8,128)(2,1)S(1)} %shard_map.100), channel_id=1, replica_groups=mesh['tm_0'=4,'tm_1'=2,'row_0'=4,'row_1'=4] {'row_0','row_1'}, dimensions={0} | all-to-all | bytes 655360 | tf_op jit(solution)/shard_map/all_to_all | solution.py:537
  68.3 0.8 %shard_map.101 = (bf16[16,4,1024]{2,1,0:T(4,128)(2,1)}, f32[8,128]{1,0:T(8,128)}) custom-call(bf16[16,8,1280]{2,1,0:T(8,128)(2,1)S(1)} %all_to_all.11.back_ref), custom_call_target="tpu_custom_call" | custom-call | tf_op jit(solution)/shard_map/pallas_call | solution.py:541
  (2 shorter events, 0.0 us)
Async XLA Ops:
  17.9 16.8 %collective-permute-start = (bf16[128,1152]{1,0:T(8,128)(2,1)S(1)}, bf16[128,1152]{1,0:T(8,128)(2,1)S(1)}, u32[]{:S(2)}, u32[]{:S(2)}) collective-permute-start(bf16[128,1152]{1,0:T(8,128)(2,1)S(1)} %bitcast.8), channel_id=1, source_target_pairs={{0,16},{16,32},{32,48},{48,64},{64,80},{80,96},{96,112},{112,0},{1... | collective-permute-start | bytes 884744 | tf_op jit(solution)/shard_map/ppermute | solution.py:493
  18.8 9.0 %collective-permute-start.3 = (bf16[1,3,16,1536]{3,2,1,0:T(8,128)(2,1)S(1)}, bf16[1,3,16,1536]{3,2,1,0:T(8,128)(2,1)S(1)}, u32[]{:S(2)}, u32[]{:S(2)}) collective-permute-start(bf16[1,3,16,1536]{3,2,1,0:T(8,128)(2,1)S(1)} %get-tuple-element.63), channel_id=1, source_target_pairs={{0,1},{1,2},{2,3},{3,4},{4,5},{5,6},{6,7},{7,8},{8,9},{9,10},{10,1... | collective-permute-start | bytes 442376 | tf_op jit(solution)/shard_map/ppermute | solution.py:493
  19.5 19.7 %collective-permute-start.2 = (bf16[2,3,16,1536]{3,2,1,0:T(8,128)(2,1)S(1)}, bf16[2,3,16,1536]{3,2,1,0:T(8,128)(2,1)S(1)}, u32[]{:S(2)}, u32[]{:S(2)}) collective-permute-start(bf16[2,3,16,1536]{3,2,1,0:T(8,128)(2,1)S(1)} %get-tuple-element.62), channel_id=1, source_target_pairs={{0,1},{1,2},{2,3},{3,4},{4,5},{5,6},{6,7},{7,8},{8,9},{9,10},{10,1... | collective-permute-start | bytes 884744 | tf_op jit(solution)/shard_map/ppermute | solution.py:493
  19.7 19.4 %collective-permute-start.4 = (bf16[1,4,16,1536]{3,2,1,0:T(8,128)(2,1)S(1)}, bf16[1,4,16,1536]{3,2,1,0:T(8,128)(2,1)S(1)}, u32[]{:S(2)}, u32[]{:S(2)}) collective-permute-start(bf16[1,4,16,1536]{3,2,1,0:T(8,128)(2,1)S(1)} %get-tuple-element.64), channel_id=1, source_target_pairs={{0,16},{16,32},{32,48},{48,64},{64,80},{80,96},{96,112},{112,0},{1... | collective-permute-start | bytes 589832 | tf_op jit(solution)/shard_map/ppermute | solution.py:493
  21.3 17.8 %collective-permute-start.1 = (bf16[1,3,16,1536]{3,2,1,0:T(8,128)(2,1)S(1)}, bf16[1,3,16,1536]{3,2,1,0:T(8,128)(2,1)S(1)}, u32[]{:S(2)}, u32[]{:S(2)}) collective-permute-start(bf16[1,3,16,1536]{3,2,1,0:T(8,128)(2,1)S(1)} %get-tuple-element.61), channel_id=1, source_target_pairs={{0,1},{1,2},{2,3},{3,4},{4,5},{5,6},{6,7},{7,8},{8,9},{9,10},{10,1... | collective-permute-start | bytes 442376 | tf_op jit(solution)/shard_map/ppermute | solution.py:493
  27.9 11.2 %collective-permute-start.5 = (bf16[1,3,16,1536]{3,2,1,0:T(8,128)(2,1)S(1)}, bf16[1,3,16,1536]{3,2,1,0:T(8,128)(2,1)S(1)}, u32[]{:S(2)}, u32[]{:S(2)}) collective-permute-start(bf16[1,3,16,1536]{3,2,1,0:T(8,128)(2,1)S(1)} %collective-permute-done.3.last_row_target), channel_id=1, source_target_pairs={{0,16},{16,32},{32,48},{48,64},{64,80},{80,96},{96,112},{112,0},{1... | collective-permute-start | bytes 442376 | tf_op jit(solution)/shard_map/ppermute | solution.py:493
  34.7 4.4 %copy-start = (s32[2,2]{1,0:T(2,128)S(1)}, s32[2,2]{1,0:T(2,128)}, u32[]{:S(2)}) copy-start(s32[2,2]{1,0:T(2,128)} %shift_ref.1) | copy-start | bytes 52
  45.8 10.6 %collective-permute-start.6 = (bf16[32,1024]{1,0:T(8,128)(2,1)S(1)}, bf16[32,1024]{1,0:T(8,128)(2,1)S(1)}, u32[]{:S(2)}, u32[]{:S(2)}) collective-permute-start(bf16[32,1024]{1,0:T(8,128)(2,1)S(1)} %get-tuple-element.66), channel_id=1, source_target_pairs={{0,112},{16,0},{32,16},{48,32},{64,48},{80,64},{96,80},{112,96},{1... | collective-permute-start | bytes 196616 | tf_op jit(solution)/shard_map/ppermute | solution.py:493
  46.5 1.2 %collective-permute-start.7 = (f32[8,128]{1,0:T(8,128)S(1)}, f32[8,128]{1,0:T(8,128)S(1)}, u32[]{:S(2)}, u32[]{:S(2)}) collective-permute-start(f32[8,128]{1,0:T(8,128)S(1)} %get-tuple-element.67), channel_id=1, source_target_pairs={{0,16},{16,0},{1,17},{17,1},{2,18},{18,2},{3,19},{19,3},{4,20},{20... | collective-permute-start | bytes 12296 | tf_op jit(solution)/shard_map/ppermute | solution.py:493
  47.7 3.6 %collective-permute-start.8 = (f32[8,128]{1,0:T(8,128)S(1)}, f32[8,128]{1,0:T(8,128)S(1)}, u32[]{:S(2)}, u32[]{:S(2)}) collective-permute-start(f32[8,128]{1,0:T(8,128)S(1)} %add.6), channel_id=1, source_target_pairs={{0,32},{32,0},{64,96},{96,64},{1,33},{33,1},{65,97},{97,65},{2,34}... | collective-permute-start | bytes 12296 | tf_op jit(solution)/shard_map/ppermute | solution.py:533
  51.3 5.1 %collective-permute-start.9 = (f32[8,128]{1,0:T(8,128)S(1)}, f32[8,128]{1,0:T(8,128)S(1)}, u32[]{:S(2)}, u32[]{:S(2)}) collective-permute-start(f32[8,128]{1,0:T(8,128)S(1)} %add.7.total_ref), channel_id=1, source_target_pairs={{0,64},{32,96},{64,0},{96,32},{1,65},{33,97},{65,1},{97,33},{2,66}... | collective-permute-start | bytes 12296 | tf_op jit(solution)/shard_map/ppermute | solution.py:493
